TPU v7x, 256 devices: a whole 4x4x8 slice. The times are simulated.
256 devices in a mesh: replica: 64 (over z_hi, y, x, core), mp: 4 (over z_lo).
Axes of the slice: x: 4, y: 4, z: 8 (z_hi: 2, z_lo: 4; z = z_hi * 4 + z_lo), core: 2. Of those that a mesh axis runs over, the one named last changes fastest.
Arguments:
- pseudo_grad: bfloat16 [64, 2, 3072, 2048], P('replica', None, None, 'mp'), may hold values from -16 to 16
- outer_params: float32 [2, 3072, 2048], P(None, 'replica', 'mp'), may hold values from -6 to 6
- momentum: float32 [2, 3072, 2048], P(None, 'replica', 'mp'), may hold values from -3 to 3
- acts: bfloat16 [8192, 3072], P('replica', 'mp'), may hold values from -6 to 6
- queries: bfloat16 [8192, 2048], P('replica', 'mp'), may hold values from -6 to 6
- keys: bfloat16 [8192, 2048], P('replica', 'mp'), may hold values from -6 to 6
- doc_ids: int32 [8192], P('replica'), may hold values from 0 to 255, never falling along the last dimension, each value on 1 to 64 neighbouring positions
Outputs:
- new_outer: float32 [2, 3072, 2048], P(None, 'replica', 'mp')
- new_momentum: float32 [2, 3072, 2048], P(None, 'replica', 'mp')
- new_local: bfloat16 [64, 3072, 2048], P('replica', None, 'mp')
Inputs may be any that keep to these rules, and one draw needn't show every extreme that they name: doc_ids never fall along the rows; each document covers 1 to 64 positions.
All inputs are finite; a program needn't handle non-finite values.
Results may differ from a plain program's by a relative error of at most 0.0037.
The roundings to bfloat16 on the way count: a program that leaves them out, or rounds other values in their place, can miss the bound.
Values may be sent and summed in bfloat16 or wider, within the bound.
No kernel may reach another device: no remote copies, remote signals or barrier semaphores. Data moves between devices by JAX's collectives and lax.ppermute only.
A program may use at most 64 MiB of HBM per device.

v0:
```python
import jax
import jax.numpy as jnp
from jax import lax
from jax.experimental import pallas as pl
from jax.experimental.pallas import tpu as pltpu
from jax.sharding import Mesh, PartitionSpec as P


HD = 256

norm_eps = 1e-06
outer_rate = 0.7
outer_beta = 0.9
inner_rate = 0.1


PLANE = ("y", "x", "c")
OWNERS = ("zh", "y", "x", "c")
F32 = jnp.float32
BF16 = jnp.bfloat16
NEAR = (1, 3)


def place(n, near):
    gray = n ^ (n >> 1)
    return gray if near == 3 else (3 * gray) & 3


def plane_swap(value, mask, first):
    pairs = []
    for y in range(4):
        for x in range(4):
            for c in range(2):
                along_x = (c == 0) == first
                ny, nx = (y, x ^ mask) if along_x else (y ^ mask, x)
                pairs.append(((y * 4 + x) * 2 + c, (ny * 4 + nx) * 2 + c))
    return lax.ppermute(value, PLANE, pairs)


def swap(value, axis):
    return lax.ppermute(value, axis, [(0, 1), (1, 0)])


def mp_swap(value, mask):
    return lax.ppermute(value, "mp", [(i, i ^ mask) for i in range(4)])


def local(body, ins, outs, mib, scratch=()):
    spec = pl.BlockSpec(memory_space=pltpu.VMEM)
    return pl.pallas_call(
        body,
        in_specs=[spec] * len(ins),
        out_specs=[spec] * len(outs),
        out_shape=[jax.ShapeDtypeStruct(shape, dtype) for shape, dtype in outs],
        scratch_shapes=scratch,
        compiler_params=pltpu.CompilerParams(vmem_limit_bytes=mib * 2**20),
    )(*ins)


def owner_of(core, first, second):
    return jnp.where(core == 0, second * 4 + first, first * 4 + second)


def pair_sums(grads, received, m):
    rows, cols = received.shape[1:]

    def body(grads_ref, received_ref, *outs):
        zh, y, x, c = (lax.axis_index(name) for name in OWNERS)
        first, second = jnp.where(c == 0, x, y), jnp.where(c == 0, y, x)
        for half in range(2):

            def step(n, carry, half=half):
                i, j, z = n >> 3, (n >> 1) & 3, n & 1
                chip = owner_of(c, first ^ place(2 * half + i, NEAR[m]), second ^ place(j, 3))
                chip = chip + (zh ^ z) * 16
                total = grads_ref[m, chip, c].astype(F32) + received_ref[chip].astype(F32)
                outs[half][i, j, z] = total.astype(BF16)
                return carry

            lax.fori_loop(0, 16, step, 0)

    return local(body, [grads, received], [((2, 4, 2, rows, cols), BF16)] * 2, 20)


def all_rows(parts, m, pieces):
    rows, cols = parts[0].shape[3:]
    part = 2 * rows // pieces

    def body(*refs):
        zh, y, x, c = (lax.axis_index(name) for name in OWNERS)
        for source in range(4):
            core = c if source < 2 else 1 - c
            first, second = jnp.where(core == 0, x, y), jnp.where(core == 0, y, x)

            def step(n, carry, source=source, core=core, first=first, second=second):
                i, j, z = n >> 3, (n >> 1) & 3, n & 1
                chip = owner_of(
                    core, first ^ place(2 * (source % 2) + i, NEAR[m]), second ^ place(j, 3)
                )
                value = refs[source][i, j, z]
                if m == 0:
                    refs[4][(zh ^ z) * 32 + chip * 2 + core] = value
                else:
                    for h in range(rows // part):
                        at = z * (rows // part) + h
                        refs[4][at, chip * 2 + core] = value[h * part : (h + 1) * part]
                return carry

            lax.fori_loop(0, 16, step, 0)

    shape = (64, rows, cols) if m == 0 else (pieces, 32, part, cols)
    return local(body, parts, [(shape, BF16)], 16)[0]


def dot(a, b, a_dim=1, b_dim=0):
    return lax.dot_general(a, b, (((a_dim,), (b_dim,)), ((), ())), preferred_element_type=F32)


def prepare(acts_parts, queries, keys, docs_row, docs_col):
    count, width = acts_parts[0].shape
    heads = queries.shape[1] // HD

    def body(*refs):
        query_ref, key_ref, row_ref, col_ref = refs[4:8]
        full_ref, normed_ref, turned_ref, gram_ref, probs_ref = refs[8:]
        here = lax.axis_index("mp")
        for k in range(4):
            full_ref[:, pl.ds(pl.multiple_of((here ^ k) * width, 128), width)] = refs[k][...]
        rows_f = full_ref[...].astype(F32)
        mean = jnp.mean(rows_f * rows_f, axis=-1, keepdims=True)
        normed = (rows_f * lax.rsqrt(mean + norm_eps)).astype(BF16)
        normed_ref[...] = normed
        turned_ref[...] = jnp.transpose(normed.astype(F32)).astype(BF16)
        gram_ref[...] = dot(normed, normed, 1, 1)
        row_pos = lax.broadcasted_iota(jnp.int32, (count, count), 0)
        col_pos = lax.broadcasted_iota(jnp.int32, (count, count), 1)
        allowed = (row_pos >= col_pos) & (row_ref[...] == col_ref[...])
        for h in range(heads):
            span = slice(h * HD, (h + 1) * HD)
            scores = dot(query_ref[:, span], key_ref[:, span], 1, 1) * HD ** (-0.5)
            scores = jnp.where(allowed, scores, -1e30)
            raised = jnp.exp(scores - jnp.max(scores, axis=-1, keepdims=True))
            probs_ref[h] = (raised / jnp.sum(raised, axis=-1, keepdims=True)).astype(BF16)

    outs = [
        ((count, 4 * width), BF16),
        ((count, 4 * width), BF16),
        ((4 * width, count), BF16),
        ((count, count), F32),
        ((heads, count, count), BF16),
    ]
    return local(body, [*acts_parts, queries, keys, docs_row, docs_col], outs, 16)


def attend(normed, value_proj, probs):
    count, width = normed.shape
    cols = value_proj.shape[1]

    def body(normed_ref, proj_ref, probs_ref, ctx_ref):
        values = (dot(normed_ref[...], proj_ref[...]) * width ** (-0.5)).astype(BF16)
        for h in range(cols // HD):
            span = slice(h * HD, (h + 1) * HD)
            ctx_ref[:, span] = dot(probs_ref[h], values[:, span]).astype(BF16)

    return local(body, [normed, value_proj, probs], [((count, cols), BF16)], 16)[0]


def first_branch(parts, out_proj):
    shape = (parts[0].shape[0], out_proj.shape[1])

    def body(*refs):
        total = dot(refs[0][...], refs[-2][0], 1, 1)
        for k in range(1, len(parts)):
            total = total + dot(refs[k][...], refs[-2][k], 1, 1)
        refs[-1][...] = total

    return local(body, [*parts, out_proj], [(shape, F32)], 16)[0]


def output_grad(branch, last, out_proj, moved):
    count, cols = last.shape
    scale = (4 * cols) ** (-0.5)

    def body(branch_ref, last_ref, proj_ref, moved_ref, *outs):
        total = (branch_ref[...] + dot(last_ref[...], proj_ref[3], 1, 1)) * scale
        dout = (moved_ref[...] + total).astype(BF16)
        for k in range(4):
            outs[k][...] = (dot(dout, proj_ref[k]) * scale).astype(outs[k].dtype)

    return local(
        body,
        [branch, last, out_proj, moved],
        [((count, cols), F32 if k == 0 else BF16) for k in range(4)],
        16,
    )


def values_grad(parts, probs, gram, width):
    count, cols = parts[0].shape

    def body(*refs):
        probs_ref, gram_ref, pulled_ref, squares_ref = refs[4:]
        total = refs[0][...]
        for k in range(1, 4):
            total = total + refs[k][...].astype(F32)
        dctx = total.astype(BF16)
        pulled = jnp.concatenate(
            [
                dot(probs_ref[h], dctx[:, h * HD : (h + 1) * HD], 0, 0).astype(BF16)
                for h in range(cols // HD)
            ],
            axis=1,
        )
        pulled_ref[...] = pulled
        product = gram_ref[...] * dot(pulled, pulled, 1, 1)
        total = jnp.sum(jnp.sum(product, axis=1, keepdims=True), axis=0, keepdims=True)
        squares_ref[...] = jnp.broadcast_to(total / width, (8, 128))

    return local(
        body, [*parts, probs, gram], [((count, cols), BF16), ((8, 128), F32)], 8
    )


def weight_grad(turned, pulled):
    def body(turned_ref, pulled_ref, out_ref):
        out_ref[...] = dot(turned_ref[...], pulled_ref[...])

    return local(body, [turned, pulled], [((turned.shape[0], pulled.shape[1]), F32)], 16)[0]


def inner_update(grad, value_proj, squares, entries):
    width, cols = value_proj.shape
    block = 512

    def body(grad_ref, proj_ref, squares_ref, out_ref):
        rms = jnp.sqrt(squares_ref[0:1, 0:1] / entries + norm_eps)
        scale = inner_rate * width ** (-0.5) / rms
        out_ref[...] = (proj_ref[...].astype(F32) - grad_ref[...] * scale).astype(BF16)

    return pl.pallas_call(
        body,
        grid=(width // block,),
        in_specs=[
            pl.BlockSpec((block, cols), lambda i: (i, 0)),
            pl.BlockSpec((block, cols), lambda i: (i, 0)),
            pl.BlockSpec((8, 128), lambda i: (0, 0)),
        ],
        out_specs=pl.BlockSpec((block, cols), lambda i: (i, 0)),
        out_shape=jax.ShapeDtypeStruct((width, cols), BF16),
        compiler_params=pltpu.CompilerParams(vmem_limit_bytes=12 * 2**20),
    )(grad, value_proj, squares)


def shards(pseudo_grad, outer_params, momentum, acts, queries, keys, doc_ids):
    workers = lax.axis_size(OWNERS)
    groups = lax.axis_size("mp")
    here = lax.axis_index("mp")
    zh, c = lax.axis_index("zh"), lax.axis_index("c")
    matrices, rows, cols = outer_params.shape
    grads = pseudo_grad.reshape(matrices, 32, 2, rows, cols)

    received = [
        swap(
            lax.dynamic_slice(grads, (m, 0, 1 - c, 0, 0), (1, 32, 1, rows, cols)).reshape(
                32, rows, cols
            ),
            "c",
        )
        for m in range(matrices)
    ]
    state = jnp.stack([outer_params, momentum])
    kept = []
    for m in range(matrices):
        keep, send = pair_sums(grads, received[m], m)
        if m == 1:
            acts, state, send = lax.optimization_barrier((acts, state, send))
        got = plane_swap(send, NEAR[m], True)
        total = keep.astype(F32) + got.astype(F32)
        kept.append(total[0] + plane_swap(total[1].astype(BF16), NEAR[m] ^ 2, True).astype(F32))
    acts_parts = [acts] + [mp_swap(acts, k) for k in (1, 2, 3)]
    far_state = swap(state, "zh")
    ready = prepare(acts_parts, queries, keys, doc_ids.reshape(1, -1), doc_ids.reshape(-1, 1))

    send = jnp.stack([value[2:] for value in kept]).astype(BF16)
    got = plane_swap(send, 3, False)
    total = jnp.stack([value[:2] for value in kept]) + got.astype(F32)
    total, ready, far_state = lax.optimization_barrier((total, ready, far_state))
    full_x, normed, turned, gram, probs = ready
    width = 64 * rows
    count = full_x.shape[0]
    half = lax.dynamic_slice(full_x, (0, (zh ^ (here >> 1)) * (width // 2)), (count, width // 2))
    part = 2 * rows // groups
    row_at = lax.broadcasted_iota(jnp.int32, (width // 2, width // groups), 0)
    col_at = lax.broadcasted_iota(jnp.int32, (width // 2, width // groups), 1)
    pick = row_at == (col_at // part) * rows + (here & 1) * part + col_at % part
    acts_here = dot(half, pick.astype(BF16))
    moved = acts_here - jnp.roll(acts_here, -1, axis=0)

    total = total[:, 0] + plane_swap(total[:, 1].astype(BF16), 1, False).astype(F32)
    total = total + swap(total.astype(BF16), "zh").astype(F32)[:, ::-1]
    total, moved = lax.optimization_barrier((total, moved))

    def outer_update(summed, params, moment):
        delta = summed / workers
        moment_next = outer_beta * moment + delta
        return params - outer_rate * (delta + outer_beta * moment_next), moment_next

    new_outer, new_momentum = outer_update(total[:, 0], outer_params, momentum)
    other_outer, _ = outer_update(total[:, 1], far_state[0], far_state[1])
    weights = [
        jnp.stack([new_outer[m].astype(BF16), other_outer[m].astype(BF16)]) for m in range(matrices)
    ]
    gathered = []
    for m in range(matrices):
        both = weights[m]
        if m == 1:
            quarters = both.reshape(groups, 2 * rows // groups, cols)
            taken = [
                lax.dynamic_index_in_dim(quarters, here ^ k, 0, keepdims=False)
                for k in range(groups)
            ]
            taken = [taken[0]] + [mp_swap(taken[k], k) for k in range(1, groups)]
            both = jnp.stack(taken).reshape(both.shape)
        two = jnp.stack([both, plane_swap(both, 1, False)])
        line = jnp.concatenate([two, plane_swap(two, 3, False)])
        two = jnp.stack([line, plane_swap(line, NEAR[m] ^ 2, True)])
        others = plane_swap(two, NEAR[m], True)
        parts = [two, others, swap(two, "c"), swap(others, "c")]
        gathered.append(all_rows(parts, m, groups))
    value_proj = gathered[0].reshape(width, cols)
    out_proj = gathered[1].reshape(groups, width // groups, cols)

    ctx = attend(normed, value_proj, probs)
    ctx_parts = [mp_swap(ctx, k) for k in (3, 2, 1)][::-1]
    branch = first_branch([ctx, *ctx_parts[:2]], out_proj)
    mine, *sends = output_grad(branch, ctx_parts[2], out_proj, moved)
    dctx_parts = [mine] + [mp_swap(sends[k - 1], k) for k in (3, 2, 1)]
    pulled, squares = values_grad(dctx_parts, probs, gram, width)
    grad = weight_grad(turned, pulled)
    squares = squares + mp_swap(squares, 2)
    squares = squares + mp_swap(squares, 1)
    new_local = inner_update(grad, value_proj, squares, width * cols * groups)
    return (new_outer, new_momentum, new_local[None])


def solution(mesh):
    fine = Mesh(mesh.devices.reshape(2, 4, 4, 2, 4), (*OWNERS, "mp"))
    placed = (
        P(OWNERS, None, None, "mp"),
        P(None, OWNERS, "mp"),
        P(None, OWNERS, "mp"),
        P(OWNERS, "mp"),
        P(OWNERS, "mp"),
        P(OWNERS, "mp"),
        P(OWNERS),
    )

    return jax.shard_map(
        shards,
        mesh=fine,
        in_specs=placed,
        out_specs=(P(None, OWNERS, "mp"), P(None, OWNERS, "mp"), P(OWNERS, None, "mp")),
        check_vma=False,
    )
```

profile of v0, /device:TPU:2, one launch (start us, length us, event | category | flops | bytes accessed | tf_op | source)
XLA Modules:
  0.0 175.2 jit_solution(3354288428367700427)
XLA Ops:
  3.5 2.9 %collective-permute-done.received_ref = bf16[32,48,512]{2,1,0:T(8,128)(2,1)S(1)} collective-permute-done((bf16[32,48,512]{2,1,0:T(8,128)(2,1)S(1)}, bf16[32,48,512]{2,1,0:T(8,128)(2,1)S(1)}, u32[]{:S(2)}, u32[]{:S(2)}) %collective-permute-start) | collective-permute-done | bytes 1572896 | tf_op jit(solution)/shard_map/ppermute | solution.py:41
  12.5 4.7 %collective-permute-start.9 = (bf16[128,768]{1,0:T(8,128)(2,1)S(1)}, bf16[128,768]{1,0:T(8,128)(2,1)S(1)}, u32[]{:S(2)}, u32[]{:S(2)}) collective-permute-start(bf16[128,768]{1,0:T(8,128)(2,1)S(1)} %copy-done.1), channel_id=1, source_target_pairs={{0,3},{1,2},{2,1},{3,0},{4,7},{5,6},{6,5},{7,4},{8,11},{9,10},{10,... | collective-permute-start | bytes 589832 | tf_op jit(solution)/shard_map/ppermute | solution.py:45
  17.9 5.2 %collective-permute-done.9.refs_3_ = bf16[128,768]{1,0:T(8,128)(2,1)S(1)} collective-permute-done((bf16[128,768]{1,0:T(8,128)(2,1)S(1)}, bf16[128,768]{1,0:T(8,128)(2,1)S(1)}, u32[]{:S(2)}, u32[]{:S(2)}) %collective-permute-start.9) | collective-permute-done | bytes 196640 | tf_op jit(solution)/shard_map/ppermute | solution.py:45
  23.1 6.4 %collective-permute-start.10 = (f32[2,2,48,512]{3,2,1,0:T(8,128)}, f32[2,2,48,512]{3,2,1,0:T(8,128)S(1)}, u32[]{:S(2)}, u32[]{:S(2)}) collective-permute-start(f32[2,2,48,512]{3,2,1,0:T(8,128)} %pad_maximum_fusion.3), channel_id=1, source_target_pairs={{0,128},{128,0},{1,129},{129,1},{2,130},{130,2},{3,131},{131,3},{4... | collective-permute-start | bytes 1179656 | tf_op jit(solution)/shard_map/ppermute | solution.py:41
  29.5 13.4 %collective-permute-done.8.refs_2_ = bf16[128,768]{1,0:T(8,128)(2,1)S(1)} collective-permute-done((bf16[128,768]{1,0:T(8,128)(2,1)S(1)}, bf16[128,768]{1,0:T(8,128)(2,1)S(1)}, u32[]{:S(2)}, u32[]{:S(2)}) %collective-permute-start.8) | collective-permute-done | bytes 196640 | tf_op jit(solution)/shard_map/ppermute | solution.py:45
  48.8 4.4 %collective-permute-done.2 = bf16[4,2,48,512]{3,2,1,0:T(8,128)(2,1)S(1)} collective-permute-done((bf16[4,2,48,512]{3,2,1,0:T(8,128)(2,1)S(1)}, bf16[4,2,48,512]{3,2,1,0:T(8,128)(2,1)S(1)}, u32[]{:S(2)}, u32[]{:S(2)}) %collective-permute-start.2) | collective-permute-done | bytes 393248 | tf_op jit(solution)/shard_map/ppermute | solution.py:37
  54.9 3.6 %collective-permute-start.6 = (bf16[2,2,2,48,512]{4,3,0,2,1:T(8,128)(2,1)S(1)}, bf16[2,2,2,48,512]{4,3,0,2,1:T(8,128)(2,1)S(1)}, u32[]{:S(2)}, u32[]{:S(2)}) collective-permute-start(bf16[2,2,2,48,512]{4,3,0,2,1:T(8,128)(2,1)S(1)} %pad_maximum_fusion.4), channel_id=1, source_target_pairs={{0,96},{4,28},{8,104},{12,20},{16,112},{20,12},{24,120},{28,4},{32... | collective-permute-start | bytes 1179656 | tf_op jit(solution)/shard_map/ppermute | solution.py:37
  58.5 5.7 %collective-permute-done.6 = bf16[2,2,2,48,512]{4,3,0,2,1:T(8,128)(2,1)S(1)} collective-permute-done((bf16[2,2,2,48,512]{4,3,0,2,1:T(8,128)(2,1)S(1)}, bf16[2,2,2,48,512]{4,3,0,2,1:T(8,128)(2,1)S(1)}, u32[]{:S(2)}, u32[]{:S(2)}) %collective-permute-start.6) | collective-permute-done | bytes 393248 | tf_op jit(solution)/shard_map/ppermute | solution.py:37
  65.9 4.2 %collective-permute-done.11 = bf16[2,2,48,512]{3,2,0,1:T(8,128)(2,1)S(1)} collective-permute-done((bf16[2,2,48,512]{3,2,0,1:T(8,128)(2,1)S(1)}, bf16[2,2,48,512]{3,2,0,1:T(8,128)(2,1)S(1)}, u32[]{:S(2)}, u32[]{:S(2)}) %collective-permute-start.11) | collective-permute-done | bytes 196640 | tf_op jit(solution)/shard_map/ppermute | solution.py:37
  70.2 14.5 %collective-permute-start.12 = (bf16[2,2,48,512]{3,2,0,1:T(8,128)(2,1)S(1)}, bf16[2,2,48,512]{3,2,0,1:T(8,128)(2,1)S(1)}, u32[]{:S(2)}, u32[]{:S(2)}) collective-permute-start(bf16[2,2,48,512]{3,2,0,1:T(8,128)(2,1)S(1)} %fusion.14), channel_id=1, source_target_pairs={{0,128},{128,0},{1,129},{129,1},{2,130},{130,2},{3,131},{131,3},{4... | collective-permute-start | bytes 589832 | tf_op jit(solution)/shard_map/ppermute | solution.py:41
  84.7 3.6 %collective-permute-done.12 = bf16[2,2,48,512]{3,2,0,1:T(8,128)(2,1)S(1)} collective-permute-done((bf16[2,2,48,512]{3,2,0,1:T(8,128)(2,1)S(1)}, bf16[2,2,48,512]{3,2,0,1:T(8,128)(2,1)S(1)}, u32[]{:S(2)}, u32[]{:S(2)}) %collective-permute-start.12) | collective-permute-done | bytes 196640 | tf_op jit(solution)/shard_map/ppermute | solution.py:41
  89.9 4.0 %collective-permute-start.21 = (bf16[24,512]{1,0:T(8,128)(2,1)S(1)}, bf16[24,512]{1,0:T(8,128)(2,1)S(1)}, u32[]{:S(2)}, u32[]{:S(2)}) collective-permute-start(bf16[24,512]{1,0:T(8,128)(2,1)S(1)} %get-tuple-element.70), channel_id=1, source_target_pairs={{0,1},{1,0},{2,3},{3,2},{4,5},{5,4},{6,7},{7,6},{8,9},{9,8},{10,11... | collective-permute-start | bytes 73736 | tf_op jit(solution)/shard_map/ppermute | solution.py:45
  96.2 2.4 %collective-permute-done.13 = bf16[2,48,512]{2,1,0:T(8,128)(2,1)S(1)} collective-permute-done((bf16[2,48,512]{2,1,0:T(8,128)(2,1)S(1)}, bf16[2,48,512]{2,1,0:T(8,128)(2,1)S(1)}, u32[]{:S(2)}, u32[]{:S(2)}) %collective-permute-start.13) | collective-permute-done | bytes 98336 | tf_op jit(solution)/shard_map/ppermute | solution.py:37
  102.7 5.0 %collective-permute-done.14 = bf16[2,2,48,512]{3,2,1,0:T(8,128)(2,1)S(1)} collective-permute-done((bf16[2,2,48,512]{3,2,1,0:T(8,128)(2,1)S(1)}, bf16[2,2,48,512]{3,2,1,0:T(8,128)(2,1)S(1)}, u32[]{:S(2)}, u32[]{:S(2)}) %collective-permute-start.14) | collective-permute-done | bytes 196640 | tf_op jit(solution)/shard_map/ppermute | solution.py:37
  115.7 4.9 %collective-permute-start.16 = (bf16[2,4,2,48,512]{4,3,2,1,0:T(8,128)(2,1)S(1)}, bf16[2,4,2,48,512]{4,3,2,1,0:T(8,128)(2,1)S(1)}, u32[]{:S(2)}, u32[]{:S(2)}) collective-permute-start(bf16[2,4,2,48,512]{4,3,2,1,0:T(8,128)(2,1)S(1)} %pad_maximum_fusion.1.refs_0_), channel_id=1, source_target_pairs={{0,8},{4,36},{8,0},{12,44},{16,24},{20,52},{24,16},{28,60},{32,40}... | collective-permute-start | bytes 2359304 | tf_op jit(solution)/shard_map/ppermute | solution.py:37
  120.9 9.7 %collective-permute-done.16.refs_1_ = bf16[2,4,2,48,512]{4,3,2,1,0:T(8,128)(2,1)S(1)} collective-permute-done((bf16[2,4,2,48,512]{4,3,2,1,0:T(8,128)(2,1)S(1)}, bf16[2,4,2,48,512]{4,3,2,1,0:T(8,128)(2,1)S(1)}, u32[]{:S(2)}, u32[]{:S(2)}) %collective-permute-start.16) | collective-permute-done | bytes 786464 | tf_op jit(solution)/shard_map/ppermute | solution.py:37
  136.4 2.6 %collective-permute-start.30 = (bf16[128,512]{1,0:T(8,128)(2,1)S(1)}, bf16[128,512]{1,0:T(8,128)(2,1)S(1)}, u32[]{:S(2)}, u32[]{:S(2)}) collective-permute-start(bf16[128,512]{1,0:T(8,128)(2,1)S(1)} %shard_map.98.refs_0_), channel_id=1, source_target_pairs={{0,3},{1,2},{2,1},{3,0},{4,7},{5,6},{6,5},{7,4},{8,11},{9,10},{10,... | collective-permute-start | bytes 393224 | tf_op jit(solution)/shard_map/ppermute | solution.py:45
  139.9 4.6 %collective-permute-done.20.refs_2_ = bf16[128,512]{1,0:T(8,128)(2,1)S(1)} collective-permute-done((bf16[128,512]{1,0:T(8,128)(2,1)S(1)}, bf16[128,512]{1,0:T(8,128)(2,1)S(1)}, u32[]{:S(2)}, u32[]{:S(2)}) %collective-permute-start.20) | collective-permute-done | bytes 131104 | tf_op jit(solution)/shard_map/ppermute | solution.py:45
  150.1 2.6 %collective-permute-start.32 = (bf16[128,512]{1,0:T(8,128)(2,1)S(1)}, bf16[128,512]{1,0:T(8,128)(2,1)S(1)}, u32[]{:S(2)}, u32[]{:S(2)}) collective-permute-start(bf16[128,512]{1,0:T(8,128)(2,1)S(1)} %get-tuple-element.52), channel_id=1, source_target_pairs={{0,2},{1,3},{2,0},{3,1},{4,6},{5,7},{6,4},{7,5},{8,10},{9,11},{10,... | collective-permute-start | bytes 393224 | tf_op jit(solution)/shard_map/ppermute | solution.py:45
  152.6 2.6 %collective-permute-done.31.refs_1_ = bf16[128,512]{1,0:T(8,128)(2,1)S(1)} collective-permute-done((bf16[128,512]{1,0:T(8,128)(2,1)S(1)}, bf16[128,512]{1,0:T(8,128)(2,1)S(1)}, u32[]{:S(2)}, u32[]{:S(2)}) %collective-permute-start.31) | collective-permute-done | bytes 131104 | tf_op jit(solution)/shard_map/ppermute | solution.py:45
  155.2 7.9 %collective-permute-done.32.refs_2_ = bf16[128,512]{1,0:T(8,128)(2,1)S(1)} collective-permute-done((bf16[128,512]{1,0:T(8,128)(2,1)S(1)}, bf16[128,512]{1,0:T(8,128)(2,1)S(1)}, u32[]{:S(2)}, u32[]{:S(2)}) %collective-permute-start.32) | collective-permute-done | bytes 131104 | tf_op jit(solution)/shard_map/ppermute | solution.py:45
  163.7 4.5 %collective-permute-done.34 = f32[8,128]{1,0:T(8,128)S(1)} collective-permute-done((f32[8,128]{1,0:T(8,128)S(1)}, f32[8,128]{1,0:T(8,128)S(1)}, u32[]{:S(2)}, u32[]{:S(2)}) %collective-permute-start.34) | collective-permute-done | bytes 4128 | tf_op jit(solution)/shard_map/ppermute | solution.py:45
  169.1 2.6 %collective-permute-done.35 = f32[8,128]{1,0:T(8,128)S(1)} collective-permute-done((f32[8,128]{1,0:T(8,128)S(1)}, f32[8,128]{1,0:T(8,128)S(1)}, u32[]{:S(2)}, u32[]{:S(2)}) %collective-permute-start.35) | collective-permute-done | bytes 4128 | tf_op jit(solution)/shard_map/ppermute | solution.py:45
  171.8 3.4 %shard_map.104 = bf16[3072,512]{1,0:T(8,128)(2,1)} custom-call(f32[3072,512]{1,0:T(8,128)S(1)} %shard_map.103.grad_ref, bf16[3072,512]{1,0:T(8,128)(2,1)S(1)} %bitcast.93, f32[8,128]{1,0:T(8,128)S(1)} %add.100.squares_ref), custom_call_target="tpu_custom_call" | custom-call | tf_op jit(solution)/shard_map/pallas_call | solution.py:240
  (114 shorter events, 48.9 us)
Async XLA Ops:
  7.1 36.7 %collective-permute-start.1 = (bf16[2,4,2,48,512]{4,3,2,1,0:T(8,128)(2,1)S(1)}, bf16[2,4,2,48,512]{4,3,2,1,0:T(8,128)(2,1)}, u32[]{:S(2)}, u32[]{:S(2)}) collective-permute-start(bf16[2,4,2,48,512]{4,3,2,1,0:T(8,128)(2,1)S(1)} %get-tuple-element.31), channel_id=1, source_target_pairs={{0,8},{4,36},{8,0},{12,44},{16,24},{20,52},{24,16},{28,60},{32,40}... | collective-permute-start | bytes 2359304 | tf_op jit(solution)/shard_map/ppermute | solution.py:37
  11.9 33.5 %collective-permute-start.4 = (bf16[2,4,2,48,512]{4,3,2,1,0:T(8,128)(2,1)}, bf16[2,4,2,48,512]{4,3,2,1,0:T(8,128)(2,1)}, u32[]{:S(2)}, u32[]{:S(2)}) collective-permute-start(bf16[2,4,2,48,512]{4,3,2,1,0:T(8,128)(2,1)} %get-tuple-element.34), channel_id=1, source_target_pairs={{0,24},{4,100},{8,16},{12,108},{16,8},{20,116},{24,0},{28,124},{32... | collective-permute-start | bytes 2359304 | tf_op jit(solution)/shard_map/ppermute | solution.py:37
  12.5 10.6 %collective-permute-start.9 = (bf16[128,768]{1,0:T(8,128)(2,1)S(1)}, bf16[128,768]{1,0:T(8,128)(2,1)S(1)}, u32[]{:S(2)}, u32[]{:S(2)}) collective-permute-start(bf16[128,768]{1,0:T(8,128)(2,1)S(1)} %copy-done.1), channel_id=1, source_target_pairs={{0,3},{1,2},{2,1},{3,0},{4,7},{5,6},{6,5},{7,4},{8,11},{9,10},{10,... | collective-permute-start | bytes 589832 | tf_op jit(solution)/shard_map/ppermute | solution.py:45
  17.2 25.7 %collective-permute-start.8 = (bf16[128,768]{1,0:T(8,128)(2,1)S(1)}, bf16[128,768]{1,0:T(8,128)(2,1)S(1)}, u32[]{:S(2)}, u32[]{:S(2)}) collective-permute-start(bf16[128,768]{1,0:T(8,128)(2,1)S(1)} %copy-done.1), channel_id=1, source_target_pairs={{0,2},{1,3},{2,0},{3,1},{4,6},{5,7},{6,4},{7,5},{8,10},{9,11},{10,... | collective-permute-start | bytes 589832 | tf_op jit(solution)/shard_map/ppermute | solution.py:45
  17.2 25.7 %collective-permute-start.7 = (bf16[128,768]{1,0:T(8,128)(2,1)S(1)}, bf16[128,768]{1,0:T(8,128)(2,1)S(1)}, u32[]{:S(2)}, u32[]{:S(2)}) collective-permute-start(bf16[128,768]{1,0:T(8,128)(2,1)S(1)} %copy-done.1), channel_id=1, source_target_pairs={{0,1},{1,0},{2,3},{3,2},{4,5},{5,4},{6,7},{7,6},{8,9},{9,8},{10,11... | collective-permute-start | bytes 589832 | tf_op jit(solution)/shard_map/ppermute | solution.py:45
  23.1 41.3 %collective-permute-start.10 = (f32[2,2,48,512]{3,2,1,0:T(8,128)}, f32[2,2,48,512]{3,2,1,0:T(8,128)S(1)}, u32[]{:S(2)}, u32[]{:S(2)}) collective-permute-start(f32[2,2,48,512]{3,2,1,0:T(8,128)} %pad_maximum_fusion.3), channel_id=1, source_target_pairs={{0,128},{128,0},{1,129},{129,1},{2,130},{130,2},{3,131},{131,3},{4... | collective-permute-start | bytes 1179656 | tf_op jit(solution)/shard_map/ppermute | solution.py:41
  45.3 7.9 %collective-permute-start.2 = (bf16[4,2,48,512]{3,2,1,0:T(8,128)(2,1)S(1)}, bf16[4,2,48,512]{3,2,1,0:T(8,128)(2,1)S(1)}, u32[]{:S(2)}, u32[]{:S(2)}) collective-permute-start(bf16[4,2,48,512]{3,2,1,0:T(8,128)(2,1)S(1)} %fusion.11), channel_id=1, source_target_pairs={{0,24},{4,100},{8,16},{12,108},{16,8},{20,116},{24,0},{28,124},{32... | collective-permute-start | bytes 1179656 | tf_op jit(solution)/shard_map/ppermute | solution.py:37
  46.8 7.9 %collective-permute-start.5 = (bf16[4,2,48,512]{3,2,1,0:T(8,128)(2,1)S(1)}, bf16[4,2,48,512]{3,2,1,0:T(8,128)(2,1)S(1)}, u32[]{:S(2)}, u32[]{:S(2)}) collective-permute-start(bf16[4,2,48,512]{3,2,1,0:T(8,128)(2,1)S(1)} %fusion.12), channel_id=1, source_target_pairs={{0,8},{4,36},{8,0},{12,44},{16,24},{20,52},{24,16},{28,60},{32,40}... | collective-permute-start | bytes 1179656 | tf_op jit(solution)/shard_map/ppermute | solution.py:37
  54.9 9.4 %collective-permute-start.6 = (bf16[2,2,2,48,512]{4,3,0,2,1:T(8,128)(2,1)S(1)}, bf16[2,2,2,48,512]{4,3,0,2,1:T(8,128)(2,1)S(1)}, u32[]{:S(2)}, u32[]{:S(2)}) collective-permute-start(bf16[2,2,2,48,512]{4,3,0,2,1:T(8,128)(2,1)S(1)} %pad_maximum_fusion.4), channel_id=1, source_target_pairs={{0,96},{4,28},{8,104},{12,20},{16,112},{20,12},{24,120},{28,4},{32... | collective-permute-start | bytes 1179656 | tf_op jit(solution)/shard_map/ppermute | solution.py:37
  70.2 18.1 %collective-permute-start.12 = (bf16[2,2,48,512]{3,2,0,1:T(8,128)(2,1)S(1)}, bf16[2,2,48,512]{3,2,0,1:T(8,128)(2,1)S(1)}, u32[]{:S(2)}, u32[]{:S(2)}) collective-permute-start(bf16[2,2,48,512]{3,2,0,1:T(8,128)(2,1)S(1)} %fusion.14), channel_id=1, source_target_pairs={{0,128},{128,0},{1,129},{129,1},{2,130},{130,2},{3,131},{131,3},{4... | collective-permute-start | bytes 589832 | tf_op jit(solution)/shard_map/ppermute | solution.py:41
  98.6 9.1 %collective-permute-start.14 = (bf16[2,2,48,512]{3,2,1,0:T(8,128)(2,1)S(1)}, bf16[2,2,48,512]{3,2,1,0:T(8,128)(2,1)S(1)}, u32[]{:S(2)}, u32[]{:S(2)}) collective-permute-start(bf16[2,2,48,512]{3,2,1,0:T(8,128)(2,1)S(1)} %pad_maximum_fusion.7), channel_id=1, source_target_pairs={{0,96},{4,28},{8,104},{12,20},{16,112},{20,12},{24,120},{28,4},{32... | collective-permute-start | bytes 589832 | tf_op jit(solution)/shard_map/ppermute | solution.py:37
  100.9 10.2 %collective-permute-start.25 = (bf16[2,2,48,512]{3,2,1,0:T(8,128)(2,1)S(1)}, bf16[2,2,48,512]{3,2,1,0:T(8,128)(2,1)S(1)}, u32[]{:S(2)}, u32[]{:S(2)}) collective-permute-start(bf16[2,2,48,512]{3,2,1,0:T(8,128)(2,1)S(1)} %pad_maximum_fusion.8), channel_id=1, source_target_pairs={{0,96},{4,28},{8,104},{12,20},{16,112},{20,12},{24,120},{28,4},{32... | collective-permute-start | bytes 589832 | tf_op jit(solution)/shard_map/ppermute | solution.py:37
  107.8 7.9 %collective-permute-start.15 = (bf16[4,2,48,512]{3,2,1,0:T(8,128)(2,1)S(1)}, bf16[4,2,48,512]{3,2,1,0:T(8,128)(2,1)S(1)}, u32[]{:S(2)}, u32[]{:S(2)}) collective-permute-start(bf16[4,2,48,512]{3,2,1,0:T(8,128)(2,1)S(1)} %get-tuple-element.65), channel_id=1, source_target_pairs={{0,24},{4,100},{8,16},{12,108},{16,8},{20,116},{24,0},{28,124},{32... | collective-permute-start | bytes 1179656 | tf_op jit(solution)/shard_map/ppermute | solution.py:37
  111.2 9.5 %collective-permute-start.26 = (bf16[4,2,48,512]{3,2,1,0:T(8,128)(2,1)S(1)}, bf16[4,2,48,512]{3,2,1,0:T(8,128)(2,1)S(1)}, u32[]{:S(2)}, u32[]{:S(2)}) collective-permute-start(bf16[4,2,48,512]{3,2,1,0:T(8,128)(2,1)S(1)} %get-tuple-element.63), channel_id=1, source_target_pairs={{0,8},{4,36},{8,0},{12,44},{16,24},{20,52},{24,16},{28,60},{32,40}... | collective-permute-start | bytes 1179656 | tf_op jit(solution)/shard_map/ppermute | solution.py:37
  115.7 14.9 %collective-permute-start.16 = (bf16[2,4,2,48,512]{4,3,2,1,0:T(8,128)(2,1)S(1)}, bf16[2,4,2,48,512]{4,3,2,1,0:T(8,128)(2,1)S(1)}, u32[]{:S(2)}, u32[]{:S(2)}) collective-permute-start(bf16[2,4,2,48,512]{4,3,2,1,0:T(8,128)(2,1)S(1)} %pad_maximum_fusion.1.refs_0_), channel_id=1, source_target_pairs={{0,8},{4,36},{8,0},{12,44},{16,24},{20,52},{24,16},{28,60},{32,40}... | collective-permute-start | bytes 2359304 | tf_op jit(solution)/shard_map/ppermute | solution.py:37
  120.7 12.1 %collective-permute-start.27 = (bf16[2,4,2,48,512]{4,3,2,1,0:T(8,128)(2,1)S(1)}, bf16[2,4,2,48,512]{4,3,2,1,0:T(8,128)(2,1)S(1)}, u32[]{:S(2)}, u32[]{:S(2)}) collective-permute-start(bf16[2,4,2,48,512]{4,3,2,1,0:T(8,128)(2,1)S(1)} %pad_maximum_fusion.2.refs_0_), channel_id=1, source_target_pairs={{0,24},{4,100},{8,16},{12,108},{16,8},{20,116},{24,0},{28,124},{32... | collective-permute-start | bytes 2359304 | tf_op jit(solution)/shard_map/ppermute | solution.py:37
  120.8 12.0 %collective-permute-start.17 = (bf16[2,4,2,48,512]{4,3,2,1,0:T(8,128)(2,1)S(1)}, bf16[2,4,2,48,512]{4,3,2,1,0:T(8,128)(2,1)S(1)}, u32[]{:S(2)}, u32[]{:S(2)}) collective-permute-start(bf16[2,4,2,48,512]{4,3,2,1,0:T(8,128)(2,1)S(1)} %pad_maximum_fusion.1.refs_0_), channel_id=1, source_target_pairs={{0,4},{4,0},{1,5},{5,1},{2,6},{6,2},{3,7},{7,3},{8,12},{12,8},{9,1... | collective-permute-start | bytes 2359304 | tf_op jit(solution)/shard_map/ppermute | solution.py:41
  130.6 8.4 %collective-permute-start.28 = (bf16[2,4,2,48,512]{4,3,2,1,0:T(8,128)(2,1)S(1)}, bf16[2,4,2,48,512]{4,3,2,1,0:T(8,128)(2,1)S(1)}, u32[]{:S(2)}, u32[]{:S(2)}) collective-permute-start(bf16[2,4,2,48,512]{4,3,2,1,0:T(8,128)(2,1)S(1)} %pad_maximum_fusion.2.refs_0_), channel_id=1, source_target_pairs={{0,4},{4,0},{1,5},{5,1},{2,6},{6,2},{3,7},{7,3},{8,12},{12,8},{9,1... | collective-permute-start | bytes 2359304 | tf_op jit(solution)/shard_map/ppermute | solution.py:41
  134.5 9.9 %collective-permute-start.20 = (bf16[128,512]{1,0:T(8,128)(2,1)S(1)}, bf16[128,512]{1,0:T(8,128)(2,1)S(1)}, u32[]{:S(2)}, u32[]{:S(2)}) collective-permute-start(bf16[128,512]{1,0:T(8,128)(2,1)S(1)} %shard_map.98.refs_0_), channel_id=1, source_target_pairs={{0,2},{1,3},{2,0},{3,1},{4,6},{5,7},{6,4},{7,5},{8,10},{9,11},{10,... | collective-permute-start | bytes 393224 | tf_op jit(solution)/shard_map/ppermute | solution.py:45
  135.6 8.9 %collective-permute-start.19 = (bf16[128,512]{1,0:T(8,128)(2,1)S(1)}, bf16[128,512]{1,0:T(8,128)(2,1)S(1)}, u32[]{:S(2)}, u32[]{:S(2)}) collective-permute-start(bf16[128,512]{1,0:T(8,128)(2,1)S(1)} %shard_map.98.refs_0_), channel_id=1, source_target_pairs={{0,1},{1,0},{2,3},{3,2},{4,5},{5,4},{6,7},{7,6},{8,9},{9,8},{10,11... | collective-permute-start | bytes 393224 | tf_op jit(solution)/shard_map/ppermute | solution.py:45
  136.4 10.4 %collective-permute-start.30 = (bf16[128,512]{1,0:T(8,128)(2,1)S(1)}, bf16[128,512]{1,0:T(8,128)(2,1)S(1)}, u32[]{:S(2)}, u32[]{:S(2)}) collective-permute-start(bf16[128,512]{1,0:T(8,128)(2,1)S(1)} %shard_map.98.refs_0_), channel_id=1, source_target_pairs={{0,3},{1,2},{2,1},{3,0},{4,7},{5,6},{6,5},{7,4},{8,11},{9,10},{10,... | collective-permute-start | bytes 393224 | tf_op jit(solution)/shard_map/ppermute | solution.py:45
  147.8 7.4 %collective-permute-start.31 = (bf16[128,512]{1,0:T(8,128)(2,1)S(1)}, bf16[128,512]{1,0:T(8,128)(2,1)S(1)}, u32[]{:S(2)}, u32[]{:S(2)}) collective-permute-start(bf16[128,512]{1,0:T(8,128)(2,1)S(1)} %get-tuple-element.51), channel_id=1, source_target_pairs={{0,3},{1,2},{2,1},{3,0},{4,7},{5,6},{6,5},{7,4},{8,11},{9,10},{10,... | collective-permute-start | bytes 393224 | tf_op jit(solution)/shard_map/ppermute | solution.py:45
  150.1 13.0 %collective-permute-start.32 = (bf16[128,512]{1,0:T(8,128)(2,1)S(1)}, bf16[128,512]{1,0:T(8,128)(2,1)S(1)}, u32[]{:S(2)}, u32[]{:S(2)}) collective-permute-start(bf16[128,512]{1,0:T(8,128)(2,1)S(1)} %get-tuple-element.52), channel_id=1, source_target_pairs={{0,2},{1,3},{2,0},{3,1},{4,6},{5,7},{6,4},{7,5},{8,10},{9,11},{10,... | collective-permute-start | bytes 393224 | tf_op jit(solution)/shard_map/ppermute | solution.py:45
  152.6 10.5 %collective-permute-start.33 = (bf16[128,512]{1,0:T(8,128)(2,1)S(1)}, bf16[128,512]{1,0:T(8,128)(2,1)S(1)}, u32[]{:S(2)}, u32[]{:S(2)}) collective-permute-start(bf16[128,512]{1,0:T(8,128)(2,1)S(1)} %get-tuple-element.53), channel_id=1, source_target_pairs={{0,1},{1,0},{2,3},{3,2},{4,5},{5,4},{6,7},{7,6},{8,9},{9,8},{10,11... | collective-permute-start | bytes 393224 | tf_op jit(solution)/shard_map/ppermute | solution.py:45
  (19 other events, 148.1 us)
where the time goes:
time: 176 us; the launch traced here: 175 us
  waiting for transfers between devices  88.5 us (50%)
  starting transfers between devices  64 us (36%)
  Pallas kernels  12.5 us (7%)
  other arithmetic  5.38 us (3%)
  local copies, waits for them, and re-layouts  2.7 us (2%)
    ppermute x14, waiting for transfers between devices, mp_swap(): return lax.ppermute(value, 'mp', [(i, i ^ mask) for i in range(4)])  43.6 us
    ppermute x14, waiting for transfers between devices, plane_swap(): return lax.ppermute(value, PLANE, pairs)  38.3 us
    ppermute x14, starting transfers between devices, plane_swap(): return lax.ppermute(value, PLANE, pairs)  22.7 us
    ppermute x8, starting transfers between devices, swap(): return lax.ppermute(value, axis, [(0, 1), (1, 0)])  22 us
    ppermute x14, starting transfers between devices, mp_swap(): return lax.ppermute(value, 'mp', [(i, i ^ mask) for i in range(4)])  19.2 us
    pallas_call x10, Pallas kernels, local(): pl.pallas_call(body, in_specs=[spec] * len(ins), out_specs=[spec] * len(o...  9.02 us
    ppermute x8, waiting for transfers between devices, swap(): return lax.ppermute(value, axis, [(0, 1), (1, 0)])  6.6 us
  transfers between devices with their start and end apart: 36, of which 23 were waited for; matrix products, arithmetic and copies ran while one was open for 3% of the time, Pallas kernels for 4%

commit v1 on v0

--- a/solution.py
+++ b/solution.py
@@ -19,6 +19,7 @@
 F32 = jnp.float32
 BF16 = jnp.bfloat16
 NEAR = (1, 3)
+GATHER_NEAR = 1
 
 
 def place(n, near):
@@ -95,7 +96,7 @@
             def step(n, carry, source=source, core=core, first=first, second=second):
                 i, j, z = n >> 3, (n >> 1) & 3, n & 1
                 chip = owner_of(
-                    core, first ^ place(2 * (source % 2) + i, NEAR[m]), second ^ place(j, 3)
+                    core, first ^ place(2 * (source % 2) + i, GATHER_NEAR), second ^ place(j, 3)
                 )
                 value = refs[source][i, j, z]
                 if m == 0:
@@ -116,14 +117,16 @@
     return lax.dot_general(a, b, (((a_dim,), (b_dim,)), ((), ())), preferred_element_type=F32)
 
 
-def prepare(acts_parts, queries, keys, docs_row, docs_col):
+def prepare(acts_parts, queries, keys, docs_row, docs_col, rows):
     count, width = acts_parts[0].shape
     heads = queries.shape[1] // HD
+    part = rows // 2
+    group = 16 * rows
 
     def body(*refs):
         query_ref, key_ref, row_ref, col_ref = refs[4:8]
-        full_ref, normed_ref, turned_ref, gram_ref, probs_ref = refs[8:]
-        here = lax.axis_index("mp")
+        normed_ref, turned_ref, gram_ref, probs_ref, moved_ref, full_ref = refs[8:]
+        here, zh = lax.axis_index("mp"), lax.axis_index("zh")
         for k in range(4):
             full_ref[:, pl.ds(pl.multiple_of((here ^ k) * width, 128), width)] = refs[k][...]
         rows_f = full_ref[...].astype(F32)
@@ -141,15 +144,44 @@
             scores = jnp.where(allowed, scores, -1e30)
             raised = jnp.exp(scores - jnp.max(scores, axis=-1, keepdims=True))
             probs_ref[h] = (raised / jnp.sum(raised, axis=-1, keepdims=True)).astype(BF16)
+        from_row = lax.broadcasted_iota(jnp.int32, (group, group // 2), 0)
+        to_col = lax.broadcasted_iota(jnp.int32, (1, group // 2), 1)
+        run = ((to_col.astype(F32) + 0.5) * (1.0 / part)).astype(jnp.int32)
+        pick = (from_row == to_col + (run + (here & 1)) * part).astype(F32).astype(BF16)
+        for g in range(2):
+            start = (zh ^ (here >> 1)) * (2 * width) + g * group
+            taken = dot(full_ref[:, pl.ds(pl.multiple_of(start, 128), group)], pick)
+            moved = taken - pltpu.roll(taken, count - 1, 0)
+            moved_ref[:, g * (group // 2) : (g + 1) * (group // 2)] = moved
 
     outs = [
-        ((count, 4 * width), BF16),
         ((count, 4 * width), BF16),
         ((4 * width, count), BF16),
         ((count, count), F32),
         ((heads, count, count), BF16),
+        ((count, width), F32),
     ]
-    return local(body, [*acts_parts, queries, keys, docs_row, docs_col], outs, 16)
+    return local(
+        body,
+        [*acts_parts, queries, keys, docs_row, docs_col],
+        outs,
+        16,
+        [pltpu.VMEM((count, 4 * width), BF16)],
+    )
+
+
+def quarters_of(both):
+    rows, cols = both.shape[1:]
+    part = rows // 2
+
+    def body(both_ref, *outs):
+        here = lax.axis_index("mp")
+        for k in range(4):
+            value = both_ref[(here ^ k) >> 1]
+            odd = ((here ^ k) & 1) == 1
+            outs[k][...] = jnp.where(odd, value[part:], value[:part])
+
+    return local(body, [both], [((part, cols), BF16)] * 4, 4)
 
 
 def attend(normed, value_proj, probs):
@@ -230,32 +262,36 @@
 
 def inner_update(grad, value_proj, squares, entries):
     width, cols = value_proj.shape
-    block = 512
-
-    def body(grad_ref, proj_ref, squares_ref, out_ref):
+    steps = 12
+    block = width // steps
+
+    def body(grad_ref, proj_ref, squares_ref, out_ref, held, sems):
         rms = jnp.sqrt(squares_ref[0:1, 0:1] / entries + norm_eps)
         scale = inner_rate * width ** (-0.5) / rms
-        out_ref[...] = (proj_ref[...].astype(F32) - grad_ref[...] * scale).astype(BF16)
-
+        copies = []
+        for i in range(steps):
+            span = pl.ds(i * block, block)
+            held[span, :] = (proj_ref[span, :].astype(F32) - grad_ref[span, :] * scale).astype(BF16)
+            copies.append(pltpu.make_async_copy(held.at[span, :], out_ref.at[span, :], sems.at[i]))
+            copies[-1].start()
+        for copy in copies:
+            copy.wait()
+
+    vmem = pl.BlockSpec(memory_space=pltpu.VMEM)
     return pl.pallas_call(
         body,
-        grid=(width // block,),
-        in_specs=[
-            pl.BlockSpec((block, cols), lambda i: (i, 0)),
-            pl.BlockSpec((block, cols), lambda i: (i, 0)),
-            pl.BlockSpec((8, 128), lambda i: (0, 0)),
-        ],
-        out_specs=pl.BlockSpec((block, cols), lambda i: (i, 0)),
+        in_specs=[vmem] * 3,
+        out_specs=pl.BlockSpec(memory_space=pl.ANY),
         out_shape=jax.ShapeDtypeStruct((width, cols), BF16),
-        compiler_params=pltpu.CompilerParams(vmem_limit_bytes=12 * 2**20),
+        scratch_shapes=[pltpu.VMEM((width, cols), BF16), pltpu.SemaphoreType.DMA((steps,))],
+        compiler_params=pltpu.CompilerParams(vmem_limit_bytes=20 * 2**20),
     )(grad, value_proj, squares)
 
 
 def shards(pseudo_grad, outer_params, momentum, acts, queries, keys, doc_ids):
     workers = lax.axis_size(OWNERS)
     groups = lax.axis_size("mp")
-    here = lax.axis_index("mp")
-    zh, c = lax.axis_index("zh"), lax.axis_index("c")
+    c = lax.axis_index("c")
     matrices, rows, cols = outer_params.shape
     grads = pseudo_grad.reshape(matrices, 32, 2, rows, cols)
 
@@ -268,37 +304,28 @@
         )
         for m in range(matrices)
     ]
-    state = jnp.stack([outer_params, momentum])
     kept = []
     for m in range(matrices):
         keep, send = pair_sums(grads, received[m], m)
         if m == 1:
-            acts, state, send = lax.optimization_barrier((acts, state, send))
+            acts, old_outer, old_momentum, send = lax.optimization_barrier(
+                (acts, outer_params, momentum, send)
+            )
         got = plane_swap(send, NEAR[m], True)
         total = keep.astype(F32) + got.astype(F32)
-        kept.append(total[0] + plane_swap(total[1].astype(BF16), NEAR[m] ^ 2, True).astype(F32))
+        got = plane_swap(total[1].astype(BF16), NEAR[m] ^ 2, True)
+        kept.append(total[0] + got.astype(F32))
     acts_parts = [acts] + [mp_swap(acts, k) for k in (1, 2, 3)]
-    far_state = swap(state, "zh")
-    ready = prepare(acts_parts, queries, keys, doc_ids.reshape(1, -1), doc_ids.reshape(-1, 1))
+    far_state = swap(jnp.stack([old_outer, old_momentum]), "zh")
+    normed, turned, gram, probs, moved = prepare(
+        acts_parts, queries, keys, doc_ids.reshape(1, -1), doc_ids.reshape(-1, 1), rows
+    )
 
     send = jnp.stack([value[2:] for value in kept]).astype(BF16)
-    got = plane_swap(send, 3, False)
-    total = jnp.stack([value[:2] for value in kept]) + got.astype(F32)
-    total, ready, far_state = lax.optimization_barrier((total, ready, far_state))
-    full_x, normed, turned, gram, probs = ready
-    width = 64 * rows
-    count = full_x.shape[0]
-    half = lax.dynamic_slice(full_x, (0, (zh ^ (here >> 1)) * (width // 2)), (count, width // 2))
-    part = 2 * rows // groups
-    row_at = lax.broadcasted_iota(jnp.int32, (width // 2, width // groups), 0)
-    col_at = lax.broadcasted_iota(jnp.int32, (width // 2, width // groups), 1)
-    pick = row_at == (col_at // part) * rows + (here & 1) * part + col_at % part
-    acts_here = dot(half, pick.astype(BF16))
-    moved = acts_here - jnp.roll(acts_here, -1, axis=0)
-
+    total = jnp.stack([value[:2] for value in kept]) + plane_swap(send, 3, False).astype(F32)
     total = total[:, 0] + plane_swap(total[:, 1].astype(BF16), 1, False).astype(F32)
-    total = total + swap(total.astype(BF16), "zh").astype(F32)[:, ::-1]
-    total, moved = lax.optimization_barrier((total, moved))
+    got = swap(total.astype(BF16), "zh")
+    total = total + got.astype(F32)[:, ::-1]
 
     def outer_update(summed, params, moment):
         delta = summed / workers
@@ -314,24 +341,24 @@
     for m in range(matrices):
         both = weights[m]
         if m == 1:
-            quarters = both.reshape(groups, 2 * rows // groups, cols)
-            taken = [
-                lax.dynamic_index_in_dim(quarters, here ^ k, 0, keepdims=False)
-                for k in range(groups)
-            ]
+            taken = quarters_of(both)
             taken = [taken[0]] + [mp_swap(taken[k], k) for k in range(1, groups)]
             both = jnp.stack(taken).reshape(both.shape)
         two = jnp.stack([both, plane_swap(both, 1, False)])
         line = jnp.concatenate([two, plane_swap(two, 3, False)])
-        two = jnp.stack([line, plane_swap(line, NEAR[m] ^ 2, True)])
-        others = plane_swap(two, NEAR[m], True)
-        parts = [two, others, swap(two, "c"), swap(others, "c")]
+        two = jnp.stack([line, plane_swap(line, GATHER_NEAR ^ 2, True)])
+        others = plane_swap(two, GATHER_NEAR, True)
+        near_parts = swap(two, "c")
+        parts = [two, others, near_parts, swap(others, "c")]
         gathered.append(all_rows(parts, m, groups))
+    width = 64 * rows
     value_proj = gathered[0].reshape(width, cols)
     out_proj = gathered[1].reshape(groups, width // groups, cols)
 
     ctx = attend(normed, value_proj, probs)
-    ctx_parts = [mp_swap(ctx, k) for k in (3, 2, 1)][::-1]
+    ctx_parts = []
+    for k in (1, 2, 3):
+        ctx_parts.append(mp_swap(ctx, k))
     branch = first_branch([ctx, *ctx_parts[:2]], out_proj)
     mine, *sends = output_grad(branch, ctx_parts[2], out_proj, moved)
     dctx_parts = [mine] + [mp_swap(sends[k - 1], k) for k in (3, 2, 1)]

time: 176 us -> 200 us (1.14)
  waiting for transfers between devices: 88.5 us -> 121 us
  starting transfers between devices: 64 us -> 52.3 us
  local copies, waits for them, and re-layouts: 2.7 us -> 6.75 us
  other arithmetic: 5.38 us -> 2.33 us
    ppermute x8, waiting for transfers between devices: 6.6 us -> 26.1 us  [swap(): return lax.ppermute(value, axis, [(0, 1), (1, 0)])]
    ppermute x8, starting transfers between devices: 22 us -> 7.21 us  [swap(): return lax.ppermute(value, axis, [(0, 1), (1, 0)])]
    ppermute x14, waiting for transfers between devices: 38.3 us -> 49.8 us  [plane_swap(): return lax.ppermute(value, PLANE, pairs)]
    unnamed x14 -> x22, local copies, waits for them, and re-layouts: 0.03 us -> 4.13 us
    ppermute x14, starting transfers between devices: 22.7 us -> 25.6 us  [plane_swap(): return lax.ppermute(value, PLANE, pairs)]
    pallas_call x10 -> x11, Pallas kernels: 9.02 us -> 11.9 us  [local(): pl.pallas_call(body, in_specs=[spec] * len(ins), out_specs=[spec] * len(o...]
    add x2, other arithmetic: 2.73 us -> 0.48 us  [shards(): total = keep.astype(F32) + got.astype(F32)]
  transfers between devices with their start and end apart: 36 -> 36, of which waited for: 23 -> 26; matrix products, arithmetic and copies ran while one was open for 3% -> 1% of each run, Pallas kernels for 4% -> 5%
where the time goes in v1:
time: 200 us; the launch traced here: 197 us
  waiting for transfers between devices  121 us (60%)
  starting transfers between devices  52.3 us (26%)
  Pallas kernels  14.1 us (7%)
  local copies, waits for them, and re-layouts  6.75 us (3%)
  other arithmetic  2.33 us (1%)
    ppermute x14, waiting for transfers between devices, plane_swap(): return lax.ppermute(value, PLANE, pairs)  49.8 us
    ppermute x14, waiting for transfers between devices, mp_swap(): return lax.ppermute(value, 'mp', [(i, i ^ mask) for i in range(4)])  44.9 us
    ppermute x8, waiting for transfers between devices, swap(): return lax.ppermute(value, axis, [(0, 1), (1, 0)])  26.1 us
    ppermute x14, starting transfers between devices, plane_swap(): return lax.ppermute(value, PLANE, pairs)  25.6 us
    ppermute x14, starting transfers between devices, mp_swap(): return lax.ppermute(value, 'mp', [(i, i ^ mask) for i in range(4)])  19.4 us
    pallas_call x11, Pallas kernels, local(): pl.pallas_call(body, in_specs=[spec] * len(ins), out_specs=[spec] * len(o...  11.9 us
    ppermute x8, starting transfers between devices, swap(): return lax.ppermute(value, axis, [(0, 1), (1, 0)])  7.21 us
    unnamed x22, local copies, waits for them, and re-layouts  4.13 us
  transfers between devices with their start and end apart: 36, of which 26 were waited for; matrix products, arithmetic and copies ran while one was open for 1% of the time, Pallas kernels for 5%

profile of v1, /device:TPU:2, one launch (start us, length us, event | category | flops | bytes accessed | tf_op | source)
XLA Modules:
  0.0 197.4 jit_solution(13862806856565625242)
XLA Ops:
  3.5 2.9 %collective-permute-done.received_ref = bf16[32,48,512]{2,1,0:T(8,128)(2,1)S(1)} collective-permute-done((bf16[32,48,512]{2,1,0:T(8,128)(2,1)S(1)}, bf16[32,48,512]{2,1,0:T(8,128)(2,1)S(1)}, u32[]{:S(2)}, u32[]{:S(2)}) %collective-permute-start) | collective-permute-done | bytes 1572896 | tf_op jit(solution)/shard_map/ppermute | solution.py:42
  10.9 8.5 %collective-permute-done.1 = bf16[2,4,2,48,512]{4,3,2,1,0:T(8,128)(2,1)S(1)} collective-permute-done((bf16[2,4,2,48,512]{4,3,2,1,0:T(8,128)(2,1)S(1)}, bf16[2,4,2,48,512]{4,3,2,1,0:T(8,128)(2,1)S(1)}, u32[]{:S(2)}, u32[]{:S(2)}) %collective-permute-start.1) | collective-permute-done | bytes 786464 | tf_op jit(solution)/shard_map/ppermute | solution.py:38
  27.8 3.2 %collective-permute-done.5 = bf16[4,2,48,512]{3,2,1,0:T(8,128)(2,1)S(1)} collective-permute-done((bf16[4,2,48,512]{3,2,1,0:T(8,128)(2,1)S(1)}, bf16[4,2,48,512]{3,2,1,0:T(8,128)(2,1)S(1)}, u32[]{:S(2)}, u32[]{:S(2)}) %collective-permute-start.5) | collective-permute-done | bytes 393248 | tf_op jit(solution)/shard_map/ppermute | solution.py:38
  33.0 7.3 %collective-permute-done.6 = bf16[2,2,2,48,512]{4,3,0,2,1:T(8,128)(2,1)S(1)} collective-permute-done((bf16[2,2,2,48,512]{4,3,0,2,1:T(8,128)(2,1)S(1)}, bf16[2,2,2,48,512]{4,3,0,2,1:T(8,128)(2,1)S(1)}, u32[]{:S(2)}, u32[]{:S(2)}) %collective-permute-start.6) | collective-permute-done | bytes 393248 | tf_op jit(solution)/shard_map/ppermute | solution.py:38
  40.6 5.7 %collective-permute-done.7 = bf16[2,2,48,512]{3,2,0,1:T(8,128)(2,1)S(1)} collective-permute-done((bf16[2,2,48,512]{3,2,0,1:T(8,128)(2,1)S(1)}, bf16[2,2,48,512]{3,2,0,1:T(8,128)(2,1)S(1)}, u32[]{:S(2)}, u32[]{:S(2)}) %collective-permute-start.7) | collective-permute-done | bytes 196640 | tf_op jit(solution)/shard_map/ppermute | solution.py:38
  46.3 5.8 %collective-permute-start.8 = (bf16[2,2,48,512]{3,2,0,1:T(8,128)(2,1)S(1)}, bf16[2,2,48,512]{3,2,0,1:T(8,128)(2,1)S(1)}, u32[]{:S(2)}, u32[]{:S(2)}) collective-permute-start(bf16[2,2,48,512]{3,2,0,1:T(8,128)(2,1)S(1)} %fusion.5), channel_id=1, source_target_pairs={{0,128},{128,0},{1,129},{129,1},{2,130},{130,2},{3,131},{131,3},{4... | collective-permute-start | bytes 589832 | tf_op jit(solution)/shard_map/ppermute | solution.py:42
  52.5 8.8 %collective-permute-done.8 = bf16[2,2,48,512]{3,2,0,1:T(8,128)(2,1)S(1)} collective-permute-done((bf16[2,2,48,512]{3,2,0,1:T(8,128)(2,1)S(1)}, bf16[2,2,48,512]{3,2,0,1:T(8,128)(2,1)S(1)}, u32[]{:S(2)}, u32[]{:S(2)}) %collective-permute-start.8) | collective-permute-done | bytes 196640 | tf_op jit(solution)/shard_map/ppermute | solution.py:42
  61.4 14.3 %collective-permute-done.12 = f32[2,2,48,512]{3,2,1,0:T(8,128)S(1)} collective-permute-done((f32[2,2,48,512]{3,2,1,0:T(8,128)S(1)}, f32[2,2,48,512]{3,2,1,0:T(8,128)S(1)}, u32[]{:S(2)}, u32[]{:S(2)}) %collective-permute-start.12) | collective-permute-done | bytes 393248 | tf_op jit(solution)/shard_map/ppermute | solution.py:42
  76.8 3.7 %collective-permute-start.22 = (bf16[24,512]{1,0:T(8,128)(2,1)S(1)}, bf16[24,512]{1,0:T(8,128)(2,1)S(1)}, u32[]{:S(2)}, u32[]{:S(2)}) collective-permute-start(bf16[24,512]{1,0:T(8,128)(2,1)S(1)} %get-tuple-element.39), channel_id=1, source_target_pairs={{0,2},{1,3},{2,0},{3,1},{4,6},{5,7},{6,4},{7,5},{8,10},{9,11},{10,... | collective-permute-start | bytes 73736 | tf_op jit(solution)/shard_map/ppermute | solution.py:46
  82.3 3.8 %collective-permute-done.23 = bf16[24,512]{1,0:T(8,128)(2,1)S(1)} collective-permute-done((bf16[24,512]{1,0:T(8,128)(2,1)S(1)}, bf16[24,512]{1,0:T(8,128)(2,1)S(1)}, u32[]{:S(2)}, u32[]{:S(2)}) %collective-permute-start.23) | collective-permute-done | bytes 24608 | tf_op jit(solution)/shard_map/ppermute | solution.py:46
  90.9 3.0 %collective-permute-start.25 = (bf16[2,2,48,512]{3,2,1,0:T(8,128)(2,1)S(1)}, bf16[2,2,48,512]{3,2,1,0:T(8,128)(2,1)S(1)}, u32[]{:S(2)}, u32[]{:S(2)}) collective-permute-start(bf16[2,2,48,512]{3,2,1,0:T(8,128)(2,1)S(1)} %pad_maximum_fusion.8), channel_id=1, source_target_pairs={{0,96},{4,28},{8,104},{12,20},{16,112},{20,12},{24,120},{28,4},{32... | collective-permute-start | bytes 589832 | tf_op jit(solution)/shard_map/ppermute | solution.py:38
  103.6 2.8 %collective-permute-start.16 = (bf16[2,4,2,48,512]{4,3,2,1,0:T(8,128)(2,1)S(1)}, bf16[2,4,2,48,512]{4,3,2,1,0:T(8,128)(2,1)S(1)}, u32[]{:S(2)}, u32[]{:S(2)}) collective-permute-start(bf16[2,4,2,48,512]{4,3,2,1,0:T(8,128)(2,1)S(1)} %pad_maximum_fusion.1.refs_0_), channel_id=1, source_target_pairs={{0,8},{4,36},{8,0},{12,44},{16,24},{20,52},{24,16},{28,60},{32,40}... | collective-permute-start | bytes 2359304 | tf_op jit(solution)/shard_map/ppermute | solution.py:38
  108.2 3.0 %collective-permute-start.27 = (bf16[2,4,2,48,512]{4,3,2,1,0:T(8,128)(2,1)S(1)}, bf16[2,4,2,48,512]{4,3,2,1,0:T(8,128)(2,1)S(1)}, u32[]{:S(2)}, u32[]{:S(2)}) collective-permute-start(bf16[2,4,2,48,512]{4,3,2,1,0:T(8,128)(2,1)S(1)} %pad_maximum_fusion.2.refs_0_), channel_id=1, source_target_pairs={{0,8},{4,36},{8,0},{12,44},{16,24},{20,52},{24,16},{28,60},{32,40}... | collective-permute-start | bytes 2359304 | tf_op jit(solution)/shard_map/ppermute | solution.py:38
  111.1 5.2 %collective-permute-done.16.refs_1_ = bf16[2,4,2,48,512]{4,3,2,1,0:T(8,128)(2,1)S(1)} collective-permute-done((bf16[2,4,2,48,512]{4,3,2,1,0:T(8,128)(2,1)S(1)}, bf16[2,4,2,48,512]{4,3,2,1,0:T(8,128)(2,1)S(1)}, u32[]{:S(2)}, u32[]{:S(2)}) %collective-permute-start.16) | collective-permute-done | bytes 786464 | tf_op jit(solution)/shard_map/ppermute | solution.py:38
  116.9 7.9 %collective-permute-done.27.refs_1_ = bf16[2,4,2,48,512]{4,3,2,1,0:T(8,128)(2,1)S(1)} collective-permute-done((bf16[2,4,2,48,512]{4,3,2,1,0:T(8,128)(2,1)S(1)}, bf16[2,4,2,48,512]{4,3,2,1,0:T(8,128)(2,1)S(1)}, u32[]{:S(2)}, u32[]{:S(2)}) %collective-permute-start.27) | collective-permute-done | bytes 786464 | tf_op jit(solution)/shard_map/ppermute | solution.py:38
  124.8 2.8 %collective-permute-start.11 = (bf16[128,768]{1,0:T(8,128)(2,1)S(1)}, bf16[128,768]{1,0:T(8,128)(2,1)S(1)}, u32[]{:S(2)}, u32[]{:S(2)}) collective-permute-start(bf16[128,768]{1,0:T(8,128)(2,1)S(1)} %copy-done.1), channel_id=1, source_target_pairs={{0,3},{1,2},{2,1},{3,0},{4,7},{5,6},{6,5},{7,4},{8,11},{9,10},{10,... | collective-permute-start | bytes 589832 | tf_op jit(solution)/shard_map/ppermute | solution.py:46
  127.6 6.4 %collective-permute-done.11.refs_3_ = bf16[128,768]{1,0:T(8,128)(2,1)S(1)} collective-permute-done((bf16[128,768]{1,0:T(8,128)(2,1)S(1)}, bf16[128,768]{1,0:T(8,128)(2,1)S(1)}, u32[]{:S(2)}, u32[]{:S(2)}) %collective-permute-start.11) | collective-permute-done | bytes 196640 | tf_op jit(solution)/shard_map/ppermute | solution.py:46
  134.7 2.8 %collective-permute-start.10 = (bf16[128,768]{1,0:T(8,128)(2,1)S(1)}, bf16[128,768]{1,0:T(8,128)(2,1)S(1)}, u32[]{:S(2)}, u32[]{:S(2)}) collective-permute-start(bf16[128,768]{1,0:T(8,128)(2,1)S(1)} %copy-done.1), channel_id=1, source_target_pairs={{0,2},{1,3},{2,0},{3,1},{4,6},{5,7},{6,4},{7,5},{8,10},{9,11},{10,... | collective-permute-start | bytes 589832 | tf_op jit(solution)/shard_map/ppermute | solution.py:46
  137.5 8.9 %collective-permute-done.10.refs_2_ = bf16[128,768]{1,0:T(8,128)(2,1)S(1)} collective-permute-done((bf16[128,768]{1,0:T(8,128)(2,1)S(1)}, bf16[128,768]{1,0:T(8,128)(2,1)S(1)}, u32[]{:S(2)}, u32[]{:S(2)}) %collective-permute-start.10) | collective-permute-done | bytes 196640 | tf_op jit(solution)/shard_map/ppermute | solution.py:46
  147.2 5.8 %collective-permute-done.9.refs_1_ = bf16[128,768]{1,0:T(8,128)(2,1)} collective-permute-done((bf16[128,768]{1,0:T(8,128)(2,1)S(1)}, bf16[128,768]{1,0:T(8,128)(2,1)}, u32[]{:S(2)}, u32[]{:S(2)}) %collective-permute-start.9) | collective-permute-done | bytes 196640 | tf_op jit(solution)/shard_map/ppermute | solution.py:46
  167.5 4.7 %collective-permute-done.20.refs_2_ = bf16[128,512]{1,0:T(8,128)(2,1)S(1)} collective-permute-done((bf16[128,512]{1,0:T(8,128)(2,1)S(1)}, bf16[128,512]{1,0:T(8,128)(2,1)S(1)}, u32[]{:S(2)}, u32[]{:S(2)}) %collective-permute-start.20) | collective-permute-done | bytes 131104 | tf_op jit(solution)/shard_map/ppermute | solution.py:46
  178.6 3.8 %collective-permute-done.31.refs_1_ = bf16[128,512]{1,0:T(8,128)(2,1)S(1)} collective-permute-done((bf16[128,512]{1,0:T(8,128)(2,1)S(1)}, bf16[128,512]{1,0:T(8,128)(2,1)S(1)}, u32[]{:S(2)}, u32[]{:S(2)}) %collective-permute-start.31) | collective-permute-done | bytes 131104 | tf_op jit(solution)/shard_map/ppermute | solution.py:46
  182.3 3.8 %collective-permute-done.32.refs_2_ = bf16[128,512]{1,0:T(8,128)(2,1)S(1)} collective-permute-done((bf16[128,512]{1,0:T(8,128)(2,1)S(1)}, bf16[128,512]{1,0:T(8,128)(2,1)S(1)}, u32[]{:S(2)}, u32[]{:S(2)}) %collective-permute-start.32) | collective-permute-done | bytes 131104 | tf_op jit(solution)/shard_map/ppermute | solution.py:46
  186.9 4.5 %collective-permute-done.34 = f32[8,128]{1,0:T(8,128)S(1)} collective-permute-done((f32[8,128]{1,0:T(8,128)S(1)}, f32[8,128]{1,0:T(8,128)S(1)}, u32[]{:S(2)}, u32[]{:S(2)}) %collective-permute-start.34) | collective-permute-done | bytes 4128 | tf_op jit(solution)/shard_map/ppermute | solution.py:46
  (114 shorter events, 66.7 us)
Async XLA Ops:
  7.1 12.3 %collective-permute-start.1 = (bf16[2,4,2,48,512]{4,3,2,1,0:T(8,128)(2,1)S(1)}, bf16[2,4,2,48,512]{4,3,2,1,0:T(8,128)(2,1)S(1)}, u32[]{:S(2)}, u32[]{:S(2)}) collective-permute-start(bf16[2,4,2,48,512]{4,3,2,1,0:T(8,128)(2,1)S(1)} %get-tuple-element.27), channel_id=1, source_target_pairs={{0,8},{4,36},{8,0},{12,44},{16,24},{20,52},{24,16},{28,60},{32,40}... | collective-permute-start | bytes 2359304 | tf_op jit(solution)/shard_map/ppermute | solution.py:38
  10.2 12.1 %collective-permute-start.4 = (bf16[2,4,2,48,512]{4,3,2,1,0:T(8,128)(2,1)S(1)}, bf16[2,4,2,48,512]{4,3,2,1,0:T(8,128)(2,1)S(1)}, u32[]{:S(2)}, u32[]{:S(2)}) collective-permute-start(bf16[2,4,2,48,512]{4,3,2,1,0:T(8,128)(2,1)S(1)} %get-tuple-element.30), channel_id=1, source_target_pairs={{0,24},{4,100},{8,16},{12,108},{16,8},{20,116},{24,0},{28,124},{32... | collective-permute-start | bytes 2359304 | tf_op jit(solution)/shard_map/ppermute | solution.py:38
  19.8 7.9 %collective-permute-start.2 = (bf16[4,2,48,512]{3,2,1,0:T(8,128)(2,1)S(1)}, bf16[4,2,48,512]{3,2,1,0:T(8,128)(2,1)S(1)}, u32[]{:S(2)}, u32[]{:S(2)}) collective-permute-start(bf16[4,2,48,512]{3,2,1,0:T(8,128)(2,1)S(1)} %fusion.2), channel_id=1, source_target_pairs={{0,24},{4,100},{8,16},{12,108},{16,8},{20,116},{24,0},{28,124},{32... | collective-permute-start | bytes 1179656 | tf_op jit(solution)/shard_map/ppermute | solution.py:38
  22.6 8.5 %collective-permute-start.5 = (bf16[4,2,48,512]{3,2,1,0:T(8,128)(2,1)S(1)}, bf16[4,2,48,512]{3,2,1,0:T(8,128)(2,1)S(1)}, u32[]{:S(2)}, u32[]{:S(2)}) collective-permute-start(bf16[4,2,48,512]{3,2,1,0:T(8,128)(2,1)S(1)} %fusion.3), channel_id=1, source_target_pairs={{0,8},{4,36},{8,0},{12,44},{16,24},{20,52},{24,16},{28,60},{32,40}... | collective-permute-start | bytes 1179656 | tf_op jit(solution)/shard_map/ppermute | solution.py:38
  31.3 9.1 %collective-permute-start.6 = (bf16[2,2,2,48,512]{4,3,0,2,1:T(8,128)(2,1)S(1)}, bf16[2,2,2,48,512]{4,3,0,2,1:T(8,128)(2,1)S(1)}, u32[]{:S(2)}, u32[]{:S(2)}) collective-permute-start(bf16[2,2,2,48,512]{4,3,0,2,1:T(8,128)(2,1)S(1)} %pad_maximum_fusion.3), channel_id=1, source_target_pairs={{0,96},{4,28},{8,104},{12,20},{16,112},{20,12},{24,120},{28,4},{32... | collective-permute-start | bytes 1179656 | tf_op jit(solution)/shard_map/ppermute | solution.py:38
  46.3 15.0 %collective-permute-start.8 = (bf16[2,2,48,512]{3,2,0,1:T(8,128)(2,1)S(1)}, bf16[2,2,48,512]{3,2,0,1:T(8,128)(2,1)S(1)}, u32[]{:S(2)}, u32[]{:S(2)}) collective-permute-start(bf16[2,2,48,512]{3,2,0,1:T(8,128)(2,1)S(1)} %fusion.5), channel_id=1, source_target_pairs={{0,128},{128,0},{1,129},{129,1},{2,130},{130,2},{3,131},{131,3},{4... | collective-permute-start | bytes 589832 | tf_op jit(solution)/shard_map/ppermute | solution.py:42
  52.2 23.6 %collective-permute-start.12 = (f32[2,2,48,512]{3,2,1,0:T(8,128)S(1)}, f32[2,2,48,512]{3,2,1,0:T(8,128)S(1)}, u32[]{:S(2)}, u32[]{:S(2)}) collective-permute-start(f32[2,2,48,512]{3,2,1,0:T(8,128)S(1)} %pad_maximum_fusion.4), channel_id=1, source_target_pairs={{0,128},{128,0},{1,129},{129,1},{2,130},{130,2},{3,131},{131,3},{4... | collective-permute-start | bytes 1179656 | tf_op jit(solution)/shard_map/ppermute | solution.py:42
  86.5 9.1 %collective-permute-start.14 = (bf16[2,2,48,512]{3,2,1,0:T(8,128)(2,1)S(1)}, bf16[2,2,48,512]{3,2,1,0:T(8,128)(2,1)S(1)}, u32[]{:S(2)}, u32[]{:S(2)}) collective-permute-start(bf16[2,2,48,512]{3,2,1,0:T(8,128)(2,1)S(1)} %pad_maximum_fusion.7), channel_id=1, source_target_pairs={{0,96},{4,28},{8,104},{12,20},{16,112},{20,12},{24,120},{28,4},{32... | collective-permute-start | bytes 589832 | tf_op jit(solution)/shard_map/ppermute | solution.py:38
  90.9 9.1 %collective-permute-start.25 = (bf16[2,2,48,512]{3,2,1,0:T(8,128)(2,1)S(1)}, bf16[2,2,48,512]{3,2,1,0:T(8,128)(2,1)S(1)}, u32[]{:S(2)}, u32[]{:S(2)}) collective-permute-start(bf16[2,2,48,512]{3,2,1,0:T(8,128)(2,1)S(1)} %pad_maximum_fusion.8), channel_id=1, source_target_pairs={{0,96},{4,28},{8,104},{12,20},{16,112},{20,12},{24,120},{28,4},{32... | collective-permute-start | bytes 589832 | tf_op jit(solution)/shard_map/ppermute | solution.py:38
  100.0 8.1 %collective-permute-start.26 = (bf16[4,2,48,512]{3,2,1,0:T(8,128)(2,1)S(1)}, bf16[4,2,48,512]{3,2,1,0:T(8,128)(2,1)S(1)}, u32[]{:S(2)}, u32[]{:S(2)}) collective-permute-start(bf16[4,2,48,512]{3,2,1,0:T(8,128)(2,1)S(1)} %get-tuple-element.55), channel_id=1, source_target_pairs={{0,24},{4,100},{8,16},{12,108},{16,8},{20,116},{24,0},{28,124},{32... | collective-permute-start | bytes 1179656 | tf_op jit(solution)/shard_map/ppermute | solution.py:38
  103.6 12.7 %collective-permute-start.16 = (bf16[2,4,2,48,512]{4,3,2,1,0:T(8,128)(2,1)S(1)}, bf16[2,4,2,48,512]{4,3,2,1,0:T(8,128)(2,1)S(1)}, u32[]{:S(2)}, u32[]{:S(2)}) collective-permute-start(bf16[2,4,2,48,512]{4,3,2,1,0:T(8,128)(2,1)S(1)} %pad_maximum_fusion.1.refs_0_), channel_id=1, source_target_pairs={{0,8},{4,36},{8,0},{12,44},{16,24},{20,52},{24,16},{28,60},{32,40}... | collective-permute-start | bytes 2359304 | tf_op jit(solution)/shard_map/ppermute | solution.py:38
  108.2 16.6 %collective-permute-start.27 = (bf16[2,4,2,48,512]{4,3,2,1,0:T(8,128)(2,1)S(1)}, bf16[2,4,2,48,512]{4,3,2,1,0:T(8,128)(2,1)S(1)}, u32[]{:S(2)}, u32[]{:S(2)}) collective-permute-start(bf16[2,4,2,48,512]{4,3,2,1,0:T(8,128)(2,1)S(1)} %pad_maximum_fusion.2.refs_0_), channel_id=1, source_target_pairs={{0,8},{4,36},{8,0},{12,44},{16,24},{20,52},{24,16},{28,60},{32,40}... | collective-permute-start | bytes 2359304 | tf_op jit(solution)/shard_map/ppermute | solution.py:38
  111.1 46.6 %collective-permute-start.17 = (bf16[2,4,2,48,512]{4,3,2,1,0:T(8,128)(2,1)S(1)}, bf16[2,4,2,48,512]{4,3,2,1,0:T(8,128)(2,1)}, u32[]{:S(2)}, u32[]{:S(2)}) collective-permute-start(bf16[2,4,2,48,512]{4,3,2,1,0:T(8,128)(2,1)S(1)} %pad_maximum_fusion.1.refs_0_), channel_id=1, source_target_pairs={{0,4},{4,0},{1,5},{5,1},{2,6},{6,2},{3,7},{7,3},{8,12},{12,8},{9,1... | collective-permute-start | bytes 2359304 | tf_op jit(solution)/shard_map/ppermute | solution.py:42
  116.3 41.4 %collective-permute-start.18 = (bf16[2,4,2,48,512]{4,3,2,1,0:T(8,128)(2,1)S(1)}, bf16[2,4,2,48,512]{4,3,2,1,0:T(8,128)(2,1)}, u32[]{:S(2)}, u32[]{:S(2)}) collective-permute-start(bf16[2,4,2,48,512]{4,3,2,1,0:T(8,128)(2,1)S(1)} %collective-permute-done.16.refs_1_), channel_id=1, source_target_pairs={{0,4},{4,0},{1,5},{5,1},{2,6},{6,2},{3,7},{7,3},{8,12},{12,8},{9,1... | collective-permute-start | bytes 2359304 | tf_op jit(solution)/shard_map/ppermute | solution.py:42
  116.4 48.9 %collective-permute-start.28 = (bf16[2,4,2,48,512]{4,3,2,1,0:T(8,128)(2,1)S(1)}, bf16[2,4,2,48,512]{4,3,2,1,0:T(8,128)(2,1)}, u32[]{:S(2)}, u32[]{:S(2)}) collective-permute-start(bf16[2,4,2,48,512]{4,3,2,1,0:T(8,128)(2,1)S(1)} %pad_maximum_fusion.2.refs_0_), channel_id=1, source_target_pairs={{0,4},{4,0},{1,5},{5,1},{2,6},{6,2},{3,7},{7,3},{8,12},{12,8},{9,1... | collective-permute-start | bytes 2359304 | tf_op jit(solution)/shard_map/ppermute | solution.py:42
  124.8 40.5 %collective-permute-start.29 = (bf16[2,4,2,48,512]{4,3,2,1,0:T(8,128)(2,1)S(1)}, bf16[2,4,2,48,512]{4,3,2,1,0:T(8,128)(2,1)}, u32[]{:S(2)}, u32[]{:S(2)}) collective-permute-start(bf16[2,4,2,48,512]{4,3,2,1,0:T(8,128)(2,1)S(1)} %collective-permute-done.27.refs_1_), channel_id=1, source_target_pairs={{0,4},{4,0},{1,5},{5,1},{2,6},{6,2},{3,7},{7,3},{8,12},{12,8},{9,1... | collective-permute-start | bytes 2359304 | tf_op jit(solution)/shard_map/ppermute | solution.py:42
  124.8 9.2 %collective-permute-start.11 = (bf16[128,768]{1,0:T(8,128)(2,1)S(1)}, bf16[128,768]{1,0:T(8,128)(2,1)S(1)}, u32[]{:S(2)}, u32[]{:S(2)}) collective-permute-start(bf16[128,768]{1,0:T(8,128)(2,1)S(1)} %copy-done.1), channel_id=1, source_target_pairs={{0,3},{1,2},{2,1},{3,0},{4,7},{5,6},{6,5},{7,4},{8,11},{9,10},{10,... | collective-permute-start | bytes 589832 | tf_op jit(solution)/shard_map/ppermute | solution.py:46
  134.7 11.8 %collective-permute-start.10 = (bf16[128,768]{1,0:T(8,128)(2,1)S(1)}, bf16[128,768]{1,0:T(8,128)(2,1)S(1)}, u32[]{:S(2)}, u32[]{:S(2)}) collective-permute-start(bf16[128,768]{1,0:T(8,128)(2,1)S(1)} %copy-done.1), channel_id=1, source_target_pairs={{0,2},{1,3},{2,0},{3,1},{4,6},{5,7},{6,4},{7,5},{8,10},{9,11},{10,... | collective-permute-start | bytes 589832 | tf_op jit(solution)/shard_map/ppermute | solution.py:46
  160.8 11.4 %collective-permute-start.20 = (bf16[128,512]{1,0:T(8,128)(2,1)S(1)}, bf16[128,512]{1,0:T(8,128)(2,1)S(1)}, u32[]{:S(2)}, u32[]{:S(2)}) collective-permute-start(bf16[128,512]{1,0:T(8,128)(2,1)S(1)} %shard_map.98.refs_0_), channel_id=1, source_target_pairs={{0,2},{1,3},{2,0},{3,1},{4,6},{5,7},{6,4},{7,5},{8,10},{9,11},{10,... | collective-permute-start | bytes 393224 | tf_op jit(solution)/shard_map/ppermute | solution.py:46
  162.2 10.0 %collective-permute-start.19 = (bf16[128,512]{1,0:T(8,128)(2,1)S(1)}, bf16[128,512]{1,0:T(8,128)(2,1)S(1)}, u32[]{:S(2)}, u32[]{:S(2)}) collective-permute-start(bf16[128,512]{1,0:T(8,128)(2,1)S(1)} %shard_map.98.refs_0_), channel_id=1, source_target_pairs={{0,1},{1,0},{2,3},{3,2},{4,5},{5,4},{6,7},{7,6},{8,9},{9,8},{10,11... | collective-permute-start | bytes 393224 | tf_op jit(solution)/shard_map/ppermute | solution.py:46
  163.9 9.1 %collective-permute-start.30 = (bf16[128,512]{1,0:T(8,128)(2,1)S(1)}, bf16[128,512]{1,0:T(8,128)(2,1)S(1)}, u32[]{:S(2)}, u32[]{:S(2)}) collective-permute-start(bf16[128,512]{1,0:T(8,128)(2,1)S(1)} %shard_map.98.refs_0_), channel_id=1, source_target_pairs={{0,3},{1,2},{2,1},{3,0},{4,7},{5,6},{6,5},{7,4},{8,11},{9,10},{10,... | collective-permute-start | bytes 393224 | tf_op jit(solution)/shard_map/ppermute | solution.py:46
  174.1 8.3 %collective-permute-start.31 = (bf16[128,512]{1,0:T(8,128)(2,1)S(1)}, bf16[128,512]{1,0:T(8,128)(2,1)S(1)}, u32[]{:S(2)}, u32[]{:S(2)}) collective-permute-start(bf16[128,512]{1,0:T(8,128)(2,1)S(1)} %get-tuple-element.43), channel_id=1, source_target_pairs={{0,3},{1,2},{2,1},{3,0},{4,7},{5,6},{6,5},{7,4},{8,11},{9,10},{10,... | collective-permute-start | bytes 393224 | tf_op jit(solution)/shard_map/ppermute | solution.py:46
  176.7 9.4 %collective-permute-start.32 = (bf16[128,512]{1,0:T(8,128)(2,1)S(1)}, bf16[128,512]{1,0:T(8,128)(2,1)S(1)}, u32[]{:S(2)}, u32[]{:S(2)}) collective-permute-start(bf16[128,512]{1,0:T(8,128)(2,1)S(1)} %get-tuple-element.44), channel_id=1, source_target_pairs={{0,2},{1,3},{2,0},{3,1},{4,6},{5,7},{6,4},{7,5},{8,10},{9,11},{10,... | collective-permute-start | bytes 393224 | tf_op jit(solution)/shard_map/ppermute | solution.py:46
  176.9 9.3 %collective-permute-start.33 = (bf16[128,512]{1,0:T(8,128)(2,1)S(1)}, bf16[128,512]{1,0:T(8,128)(2,1)S(1)}, u32[]{:S(2)}, u32[]{:S(2)}) collective-permute-start(bf16[128,512]{1,0:T(8,128)(2,1)S(1)} %get-tuple-element.45), channel_id=1, source_target_pairs={{0,1},{1,0},{2,3},{3,2},{4,5},{5,4},{6,7},{7,6},{8,9},{9,8},{10,11... | collective-permute-start | bytes 393224 | tf_op jit(solution)/shard_map/ppermute | solution.py:46
  (23 other events, 226.7 us)

commit v2 on v1

--- a/solution.py
+++ b/solution.py
@@ -19,7 +19,7 @@
 F32 = jnp.float32
 BF16 = jnp.bfloat16
 NEAR = (1, 3)
-GATHER_NEAR = 1
+SECOND_NEAR = (3, 1)
 
 
 def place(n, near):
@@ -72,7 +72,9 @@
 
             def step(n, carry, half=half):
                 i, j, z = n >> 3, (n >> 1) & 3, n & 1
-                chip = owner_of(c, first ^ place(2 * half + i, NEAR[m]), second ^ place(j, 3))
+                chip = owner_of(
+                    c, first ^ place(2 * half + i, NEAR[m]), second ^ place(j, SECOND_NEAR[m])
+                )
                 chip = chip + (zh ^ z) * 16
                 total = grads_ref[m, chip, c].astype(F32) + received_ref[chip].astype(F32)
                 outs[half][i, j, z] = total.astype(BF16)
@@ -83,34 +85,46 @@
     return local(body, [grads, received], [((2, 4, 2, rows, cols), BF16)] * 2, 20)
 
 
-def all_rows(parts, m, pieces):
-    rows, cols = parts[0].shape[3:]
+def all_rows(own, other, m, pieces):
+    rows, cols = own[0][0].shape[3:]
     part = 2 * rows // pieces
 
     def body(*refs):
         zh, y, x, c = (lax.axis_index(name) for name in OWNERS)
-        for source in range(4):
-            core = c if source < 2 else 1 - c
+        out_ref = refs[7]
+        for source in range(2):
+            core = c if source == 0 else 1 - c
             first, second = jnp.where(core == 0, x, y), jnp.where(core == 0, y, x)
-
-            def step(n, carry, source=source, core=core, first=first, second=second):
-                i, j, z = n >> 3, (n >> 1) & 3, n & 1
-                chip = owner_of(
-                    core, first ^ place(2 * (source % 2) + i, GATHER_NEAR), second ^ place(j, 3)
-                )
-                value = refs[source][i, j, z]
-                if m == 0:
-                    refs[4][(zh ^ z) * 32 + chip * 2 + core] = value
-                else:
-                    for h in range(rows // part):
-                        at = z * (rows // part) + h
-                        refs[4][at, chip * 2 + core] = value[h * part : (h + 1) * part]
-                return carry
-
-            lax.fori_loop(0, 16, step, 0)
+            for h in range(2):
+                for p in range(2):
+
+                    def step(n, carry, source=source, h=h, p=p, core=core, first=first, second=second):
+                        i, j, z = n >> 2, (n >> 1) & 1, n & 1
+                        if h == 0:
+                            mask_a = 3 * i if p == 0 else 1 + i
+                            mask_b = j
+                        else:
+                            mask_a = i if p == 0 else 3 - i
+                            mask_b = 3 - j
+                        chip = owner_of(core, first ^ mask_a, second ^ mask_b)
+                        if source == 0:
+                            value = refs[2 * h + p][i, j, z]
+                        elif p == 0:
+                            value = refs[4][h, i, j, z]
+                        else:
+                            value = refs[5 + h][i, j, z]
+                        if m == 0:
+                            out_ref[(zh ^ z) * 32 + chip * 2 + core] = value
+                        else:
+                            for q in range(rows // part):
+                                at = z * (rows // part) + q
+                                out_ref[at, chip * 2 + core] = value[q * part : (q + 1) * part]
+                        return carry
+
+                    lax.fori_loop(0, 8, step, 0)
 
     shape = (64, rows, cols) if m == 0 else (pieces, 32, part, cols)
-    return local(body, parts, [(shape, BF16)], 16)[0]
+    return local(body, [*own[0], *own[1], *other], [(shape, BF16)], 16)[0]
 
 
 def dot(a, b, a_dim=1, b_dim=0):
@@ -295,15 +309,10 @@
     matrices, rows, cols = outer_params.shape
     grads = pseudo_grad.reshape(matrices, 32, 2, rows, cols)
 
-    received = [
-        swap(
-            lax.dynamic_slice(grads, (m, 0, 1 - c, 0, 0), (1, 32, 1, rows, cols)).reshape(
-                32, rows, cols
-            ),
-            "c",
-        )
-        for m in range(matrices)
-    ]
+    received = []
+    for m in range(matrices):
+        send = lax.dynamic_slice(grads, (m, 0, 1 - c, 0, 0), (1, 32, 1, rows, cols))
+        received.append(swap(send.reshape(32, rows, cols), "c"))
     kept = []
     for m in range(matrices):
         keep, send = pair_sums(grads, received[m], m)
@@ -316,24 +325,24 @@
         got = plane_swap(total[1].astype(BF16), NEAR[m] ^ 2, True)
         kept.append(total[0] + got.astype(F32))
     acts_parts = [acts] + [mp_swap(acts, k) for k in (1, 2, 3)]
-    far_state = swap(jnp.stack([old_outer, old_momentum]), "zh")
+    far_state = swap(old_outer - outer_rate * outer_beta**2 * old_momentum, "zh")
     normed, turned, gram, probs, moved = prepare(
         acts_parts, queries, keys, doc_ids.reshape(1, -1), doc_ids.reshape(-1, 1), rows
     )
 
-    send = jnp.stack([value[2:] for value in kept]).astype(BF16)
-    total = jnp.stack([value[:2] for value in kept]) + plane_swap(send, 3, False).astype(F32)
-    total = total[:, 0] + plane_swap(total[:, 1].astype(BF16), 1, False).astype(F32)
+    totals = []
+    for m in range(matrices):
+        near = SECOND_NEAR[m]
+        got = plane_swap(kept[m][2:].astype(BF16), near, False)
+        total = kept[m][:2] + got.astype(F32)
+        got = plane_swap(total[1].astype(BF16), near ^ 2, False)
+        totals.append(total[0] + got.astype(F32))
+    total = jnp.stack(totals)
     got = swap(total.astype(BF16), "zh")
-    total = total + got.astype(F32)[:, ::-1]
-
-    def outer_update(summed, params, moment):
-        delta = summed / workers
-        moment_next = outer_beta * moment + delta
-        return params - outer_rate * (delta + outer_beta * moment_next), moment_next
-
-    new_outer, new_momentum = outer_update(total[:, 0], outer_params, momentum)
-    other_outer, _ = outer_update(total[:, 1], far_state[0], far_state[1])
+    delta = (total + got.astype(F32)[:, ::-1]) / workers
+    new_momentum = outer_beta * momentum + delta[:, 0]
+    new_outer = outer_params - outer_rate * (delta[:, 0] + outer_beta * new_momentum)
+    other_outer = far_state - outer_rate * (1 + outer_beta) * delta[:, 1]
     weights = [
         jnp.stack([new_outer[m].astype(BF16), other_outer[m].astype(BF16)]) for m in range(matrices)
     ]
@@ -345,12 +354,16 @@
             taken = [taken[0]] + [mp_swap(taken[k], k) for k in range(1, groups)]
             both = jnp.stack(taken).reshape(both.shape)
         two = jnp.stack([both, plane_swap(both, 1, False)])
-        line = jnp.concatenate([two, plane_swap(two, 3, False)])
-        two = jnp.stack([line, plane_swap(line, GATHER_NEAR ^ 2, True)])
-        others = plane_swap(two, GATHER_NEAR, True)
-        near_parts = swap(two, "c")
-        parts = [two, others, near_parts, swap(others, "c")]
-        gathered.append(all_rows(parts, m, groups))
+        rest = plane_swap(two, 3, False)
+        fore = jnp.stack([two, plane_swap(two, 3, True)])
+        hind = jnp.stack([rest, plane_swap(rest, 1, True)])
+        fore_rest = plane_swap(fore, 1, True)
+        hind_rest = plane_swap(hind, 3, True)
+        other = [swap(jnp.stack([fore, hind]), "c")]
+        other.append(swap(fore_rest, "c"))
+        other.append(swap(hind_rest, "c"))
+        own = [[fore, fore_rest], [hind, hind_rest]]
+        gathered.append(all_rows(own, other, m, groups))
     width = 64 * rows
     value_proj = gathered[0].reshape(width, cols)
     out_proj = gathered[1].reshape(groups, width // groups, cols)

time: 200 us -> 169 us (0.84)
  waiting for transfers between devices: 121 us -> 76.9 us
  starting transfers between devices: 52.3 us -> 59 us
  local copies, waits for them, and re-layouts: 6.75 us -> 13.1 us
    ppermute x14, waiting for transfers between devices: 44.9 us -> 27.6 us  [mp_swap(): return lax.ppermute(value, 'mp', [(i, i ^ mask) for i in range(4)])]
    ppermute x14 -> x20, waiting for transfers between devices: 49.8 us -> 33.6 us  [plane_swap(): return lax.ppermute(value, PLANE, pairs)]
    ppermute x8 -> x10, waiting for transfers between devices: 26.1 us -> 15.7 us  [swap(): return lax.ppermute(value, axis, [(0, 1), (1, 0)])]
    unnamed x22 -> x38, local copies, waits for them, and re-layouts: 4.13 us -> 9.88 us
    ppermute x14 -> x20, starting transfers between devices: 25.6 us -> 30.9 us  [plane_swap(): return lax.ppermute(value, PLANE, pairs)]
    ppermute x8 -> x10, starting transfers between devices: 7.21 us -> 8.7 us  [swap(): return lax.ppermute(value, axis, [(0, 1), (1, 0)])]
  transfers between devices with their start and end apart: 36 -> 44, of which waited for: 26 -> 24; matrix products, arithmetic and copies ran while one was open for 1% -> 2% of each run, Pallas kernels for 5% -> 5%
where the time goes in v2:
time: 169 us; the launch traced here: 167 us
  waiting for transfers between devices  76.9 us (46%)
  starting transfers between devices  59 us (35%)
  local copies, waits for them, and re-layouts  13.1 us (8%)
  Pallas kernels  12.7 us (8%)
  other arithmetic  4.14 us (2%)
    ppermute x20, waiting for transfers between devices, plane_swap(): return lax.ppermute(value, PLANE, pairs)  33.6 us
    ppermute x20, starting transfers between devices, plane_swap(): return lax.ppermute(value, PLANE, pairs)  30.9 us
    ppermute x14, waiting for transfers between devices, mp_swap(): return lax.ppermute(value, 'mp', [(i, i ^ mask) for i in range(4)])  27.6 us
    ppermute x14, starting transfers between devices, mp_swap(): return lax.ppermute(value, 'mp', [(i, i ^ mask) for i in range(4)])  19.3 us
    ppermute x10, waiting for transfers between devices, swap(): return lax.ppermute(value, axis, [(0, 1), (1, 0)])  15.7 us
    pallas_call x11, Pallas kernels, local(): pl.pallas_call(body, in_specs=[spec] * len(ins), out_specs=[spec] * len(o...  10.5 us
    unnamed x38, local copies, waits for them, and re-layouts  9.88 us
    ppermute x10, starting transfers between devices, swap(): return lax.ppermute(value, axis, [(0, 1), (1, 0)])  8.7 us
  transfers between devices with their start and end apart: 44, of which 24 were waited for; matrix products, arithmetic and copies ran while one was open for 2% of the time, Pallas kernels for 5%

profile of v2, /device:TPU:2, one launch (start us, length us, event | category | flops | bytes accessed | tf_op | source)
XLA Modules:
  0.0 166.9 jit_solution(4300798422160672196)
XLA Ops:
  3.5 2.9 %collective-permute-done.received_ref = bf16[32,48,512]{2,1,0:T(8,128)(2,1)S(1)} collective-permute-done((bf16[32,48,512]{2,1,0:T(8,128)(2,1)S(1)}, bf16[32,48,512]{2,1,0:T(8,128)(2,1)S(1)}, u32[]{:S(2)}, u32[]{:S(2)}) %collective-permute-start) | collective-permute-done | bytes 1572896 | tf_op jit(solution)/shard_map/ppermute | solution.py:42
  7.1 2.3 %collective-permute-start.1 = (bf16[2,4,2,48,512]{4,3,2,1,0:T(8,128)(2,1)S(1)}, bf16[2,4,2,48,512]{4,3,2,1,0:T(8,128)(2,1)S(1)}, u32[]{:S(2)}, u32[]{:S(2)}) collective-permute-start(bf16[2,4,2,48,512]{4,3,2,1,0:T(8,128)(2,1)S(1)} %get-tuple-element.27), channel_id=1, source_target_pairs={{0,8},{4,36},{8,0},{12,44},{16,24},{20,52},{24,16},{28,60},{32,40}... | collective-permute-start | bytes 2359304 | tf_op jit(solution)/shard_map/ppermute | solution.py:38
  11.0 8.5 %collective-permute-done.1 = bf16[2,4,2,48,512]{4,3,2,1,0:T(8,128)(2,1)S(1)} collective-permute-done((bf16[2,4,2,48,512]{4,3,2,1,0:T(8,128)(2,1)S(1)}, bf16[2,4,2,48,512]{4,3,2,1,0:T(8,128)(2,1)S(1)}, u32[]{:S(2)}, u32[]{:S(2)}) %collective-permute-start.1) | collective-permute-done | bytes 786464 | tf_op jit(solution)/shard_map/ppermute | solution.py:38
  22.6 2.7 %collective-permute-start.7 = (bf16[4,2,48,512]{3,2,1,0:T(8,128)(2,1)S(1)}, bf16[4,2,48,512]{3,2,1,0:T(8,128)(2,1)S(1)}, u32[]{:S(2)}, u32[]{:S(2)}) collective-permute-start(bf16[4,2,48,512]{3,2,1,0:T(8,128)(2,1)S(1)} %fusion.3), channel_id=1, source_target_pairs={{0,8},{4,36},{8,0},{12,44},{16,24},{20,52},{24,16},{28,60},{32,40}... | collective-permute-start | bytes 1179656 | tf_op jit(solution)/shard_map/ppermute | solution.py:38
  27.8 2.9 %collective-permute-start.3 = (bf16[2,2,48,512]{3,2,1,0:T(8,128)(2,1)S(1)}, bf16[2,2,48,512]{3,2,1,0:T(8,128)(2,1)S(1)}, u32[]{:S(2)}, u32[]{:S(2)}) collective-permute-start(bf16[2,2,48,512]{3,2,1,0:T(8,128)(2,1)S(1)} %slice.146), channel_id=1, source_target_pairs={{0,96},{4,28},{8,104},{12,20},{16,112},{20,12},{24,120},{28,4},{32... | collective-permute-start | bytes 589832 | tf_op jit(solution)/shard_map/ppermute | solution.py:38
  31.5 3.3 %collective-permute-done.3 = bf16[2,2,48,512]{3,2,1,0:T(8,128)(2,1)S(1)} collective-permute-done((bf16[2,2,48,512]{3,2,1,0:T(8,128)(2,1)S(1)}, bf16[2,2,48,512]{3,2,1,0:T(8,128)(2,1)S(1)}, u32[]{:S(2)}, u32[]{:S(2)}) %collective-permute-start.3) | collective-permute-done | bytes 196640 | tf_op jit(solution)/shard_map/ppermute | solution.py:38
  39.6 3.4 %collective-permute-done.9 = bf16[2,48,512]{2,1,0:T(8,128)(2,1)S(1)} collective-permute-done((bf16[2,48,512]{2,1,0:T(8,128)(2,1)S(1)}, bf16[2,48,512]{2,1,0:T(8,128)(2,1)S(1)}, u32[]{:S(2)}, u32[]{:S(2)}) %collective-permute-start.9) | collective-permute-done | bytes 98336 | tf_op jit(solution)/shard_map/ppermute | solution.py:38
  43.0 6.9 %collective-permute-start.10 = (bf16[2,2,48,512]{3,2,0,1:T(8,128)(2,1)S(1)}, bf16[2,2,48,512]{3,2,0,1:T(8,128)(2,1)S(1)}, u32[]{:S(2)}, u32[]{:S(2)}) collective-permute-start(bf16[2,2,48,512]{3,2,0,1:T(8,128)(2,1)S(1)} %fusion.4), channel_id=1, source_target_pairs={{0,128},{128,0},{1,129},{129,1},{2,130},{130,2},{3,131},{131,3},{4... | collective-permute-start | bytes 589832 | tf_op jit(solution)/shard_map/ppermute | solution.py:42
  50.1 8.1 %collective-permute-done.10 = bf16[2,2,48,512]{3,2,0,1:T(8,128)(2,1)S(1)} collective-permute-done((bf16[2,2,48,512]{3,2,0,1:T(8,128)(2,1)S(1)}, bf16[2,2,48,512]{3,2,0,1:T(8,128)(2,1)S(1)}, u32[]{:S(2)}, u32[]{:S(2)}) %collective-permute-start.10) | collective-permute-done | bytes 196640 | tf_op jit(solution)/shard_map/ppermute | solution.py:42
  58.4 4.6 %collective-permute-done.14 = f32[2,48,512]{2,1,0:T(8,128)S(1)} collective-permute-done((f32[2,48,512]{2,1,0:T(8,128)S(1)}, f32[2,48,512]{2,1,0:T(8,128)S(1)}, u32[]{:S(2)}, u32[]{:S(2)}) %collective-permute-start.14) | collective-permute-done | bytes 196640 | tf_op jit(solution)/shard_map/ppermute | solution.py:42
  74.9 3.0 %collective-permute-start.18 = (bf16[2,2,48,512]{3,2,1,0:T(8,128)(2,1)S(1)}, bf16[2,2,48,512]{3,2,1,0:T(8,128)(2,1)S(1)}, u32[]{:S(2)}, u32[]{:S(2)}) collective-permute-start(bf16[2,2,48,512]{3,2,1,0:T(8,128)(2,1)S(1)} %get-tuple-element.66), channel_id=1, source_target_pairs={{0,96},{4,28},{8,104},{12,20},{16,112},{20,12},{24,120},{28,4},{32... | collective-permute-start | bytes 589832 | tf_op jit(solution)/shard_map/ppermute | solution.py:38
  78.9 2.6 %collective-permute-start.32 = (bf16[2,2,48,512]{3,2,1,0:T(8,128)(2,1)S(1)}, bf16[2,2,48,512]{3,2,1,0:T(8,128)(2,1)S(1)}, u32[]{:S(2)}, u32[]{:S(2)}) collective-permute-start(bf16[2,2,48,512]{3,2,1,0:T(8,128)(2,1)S(1)} %get-tuple-element.64), channel_id=1, source_target_pairs={{0,96},{4,28},{8,104},{12,20},{16,112},{20,12},{24,120},{28,4},{32... | collective-permute-start | bytes 589832 | tf_op jit(solution)/shard_map/ppermute | solution.py:38
  83.1 3.4 %collective-permute-start.19 = (bf16[2,2,48,512]{3,2,1,0:T(8,128)(2,1)S(1)}, bf16[2,2,48,512]{3,2,1,0:T(8,128)(2,1)S(1)}, u32[]{:S(2)}, u32[]{:S(2)}) collective-permute-start(bf16[2,2,48,512]{3,2,1,0:T(8,128)(2,1)S(1)} %collective-permute-done.18), channel_id=1, source_target_pairs={{0,8},{4,36},{8,0},{12,44},{16,24},{20,52},{24,16},{28,60},{32,40}... | collective-permute-start | bytes 589832 | tf_op jit(solution)/shard_map/ppermute | solution.py:38
  92.3 4.5 %collective-permute-done.33 = bf16[2,2,48,512]{3,2,1,0:T(8,128)(2,1)S(1)} collective-permute-done((bf16[2,2,48,512]{3,2,1,0:T(8,128)(2,1)S(1)}, bf16[2,2,48,512]{3,2,1,0:T(8,128)(2,1)S(1)}, u32[]{:S(2)}, u32[]{:S(2)}) %collective-permute-start.33) | collective-permute-done | bytes 196640 | tf_op jit(solution)/shard_map/ppermute | solution.py:38
  96.7 3.7 %collective-permute-start.11 = (bf16[128,768]{1,0:T(8,128)(2,1)S(1)}, bf16[128,768]{1,0:T(8,128)(2,1)S(1)}, u32[]{:S(2)}, u32[]{:S(2)}) collective-permute-start(bf16[128,768]{1,0:T(8,128)(2,1)S(1)} %copy-done.6), channel_id=1, source_target_pairs={{0,1},{1,0},{2,3},{3,2},{4,5},{5,4},{6,7},{7,6},{8,9},{9,8},{10,11... | collective-permute-start | bytes 589832 | tf_op jit(solution)/shard_map/ppermute | solution.py:46
  106.8 2.6 %collective-permute-done.20.refs_3_ = bf16[2,2,2,48,512]{4,3,2,1,0:T(8,128)(2,1)} collective-permute-done((bf16[2,2,2,48,512]{4,3,2,1,0:T(8,128)(2,1)S(1)}, bf16[2,2,2,48,512]{4,3,2,1,0:T(8,128)(2,1)}, u32[]{:S(2)}, u32[]{:S(2)}) %collective-permute-start.20) | collective-permute-done | bytes 393248 | tf_op jit(solution)/shard_map/ppermute | solution.py:38
  109.4 4.2 %collective-permute-done.34.refs_3_ = bf16[2,2,2,48,512]{4,3,2,1,0:T(8,128)(2,1)} collective-permute-done((bf16[2,2,2,48,512]{4,3,2,1,0:T(8,128)(2,1)S(1)}, bf16[2,2,2,48,512]{4,3,2,1,0:T(8,128)(2,1)}, u32[]{:S(2)}, u32[]{:S(2)}) %collective-permute-start.34) | collective-permute-done | bytes 393248 | tf_op jit(solution)/shard_map/ppermute | solution.py:38
  128.9 3.4 %collective-permute-start.38 = (bf16[128,512]{1,0:T(8,128)(2,1)S(1)}, bf16[128,512]{1,0:T(8,128)(2,1)S(1)}, u32[]{:S(2)}, u32[]{:S(2)}) collective-permute-start(bf16[128,512]{1,0:T(8,128)(2,1)S(1)} %shard_map.98.refs_0_), channel_id=1, source_target_pairs={{0,3},{1,2},{2,1},{3,0},{4,7},{5,6},{6,5},{7,4},{8,11},{9,10},{10,... | collective-permute-start | bytes 393224 | tf_op jit(solution)/shard_map/ppermute | solution.py:46
  134.3 3.6 %collective-permute-done.25.refs_2_ = bf16[128,512]{1,0:T(8,128)(2,1)S(1)} collective-permute-done((bf16[128,512]{1,0:T(8,128)(2,1)S(1)}, bf16[128,512]{1,0:T(8,128)(2,1)S(1)}, u32[]{:S(2)}, u32[]{:S(2)}) %collective-permute-start.25) | collective-permute-done | bytes 131104 | tf_op jit(solution)/shard_map/ppermute | solution.py:46
  142.2 3.3 %collective-permute-start.40 = (bf16[128,512]{1,0:T(8,128)(2,1)S(1)}, bf16[128,512]{1,0:T(8,128)(2,1)S(1)}, u32[]{:S(2)}, u32[]{:S(2)}) collective-permute-start(bf16[128,512]{1,0:T(8,128)(2,1)S(1)} %get-tuple-element.44), channel_id=1, source_target_pairs={{0,2},{1,3},{2,0},{3,1},{4,6},{5,7},{6,4},{7,5},{8,10},{9,11},{10,... | collective-permute-start | bytes 393224 | tf_op jit(solution)/shard_map/ppermute | solution.py:46
  145.5 2.6 %collective-permute-done.39.refs_1_ = bf16[128,512]{1,0:T(8,128)(2,1)S(1)} collective-permute-done((bf16[128,512]{1,0:T(8,128)(2,1)S(1)}, bf16[128,512]{1,0:T(8,128)(2,1)S(1)}, u32[]{:S(2)}, u32[]{:S(2)}) %collective-permute-start.39) | collective-permute-done | bytes 131104 | tf_op jit(solution)/shard_map/ppermute | solution.py:46
  148.1 7.8 %collective-permute-done.40.refs_2_ = bf16[128,512]{1,0:T(8,128)(2,1)S(1)} collective-permute-done((bf16[128,512]{1,0:T(8,128)(2,1)S(1)}, bf16[128,512]{1,0:T(8,128)(2,1)S(1)}, u32[]{:S(2)}, u32[]{:S(2)}) %collective-permute-start.40) | collective-permute-done | bytes 131104 | tf_op jit(solution)/shard_map/ppermute | solution.py:46
  156.4 4.5 %collective-permute-done.42 = f32[8,128]{1,0:T(8,128)S(1)} collective-permute-done((f32[8,128]{1,0:T(8,128)S(1)}, f32[8,128]{1,0:T(8,128)S(1)}, u32[]{:S(2)}, u32[]{:S(2)}) %collective-permute-start.42) | collective-permute-done | bytes 4128 | tf_op jit(solution)/shard_map/ppermute | solution.py:46
  161.9 2.6 %collective-permute-done.43 = f32[8,128]{1,0:T(8,128)S(1)} collective-permute-done((f32[8,128]{1,0:T(8,128)S(1)}, f32[8,128]{1,0:T(8,128)S(1)}, u32[]{:S(2)}, u32[]{:S(2)}) %collective-permute-start.43) | collective-permute-done | bytes 4128 | tf_op jit(solution)/shard_map/ppermute | solution.py:46
  (149 shorter events, 68.4 us)
Async XLA Ops:
  7.1 12.3 %collective-permute-start.1 = (bf16[2,4,2,48,512]{4,3,2,1,0:T(8,128)(2,1)S(1)}, bf16[2,4,2,48,512]{4,3,2,1,0:T(8,128)(2,1)S(1)}, u32[]{:S(2)}, u32[]{:S(2)}) collective-permute-start(bf16[2,4,2,48,512]{4,3,2,1,0:T(8,128)(2,1)S(1)} %get-tuple-element.27), channel_id=1, source_target_pairs={{0,8},{4,36},{8,0},{12,44},{16,24},{20,52},{24,16},{28,60},{32,40}... | collective-permute-start | bytes 2359304 | tf_op jit(solution)/shard_map/ppermute | solution.py:38
  10.2 12.1 %collective-permute-start.6 = (bf16[2,4,2,48,512]{4,3,2,1,0:T(8,128)(2,1)S(1)}, bf16[2,4,2,48,512]{4,3,2,1,0:T(8,128)(2,1)S(1)}, u32[]{:S(2)}, u32[]{:S(2)}) collective-permute-start(bf16[2,4,2,48,512]{4,3,2,1,0:T(8,128)(2,1)S(1)} %get-tuple-element.30), channel_id=1, source_target_pairs={{0,24},{4,100},{8,16},{12,108},{16,8},{20,116},{24,0},{28,124},{32... | collective-permute-start | bytes 2359304 | tf_op jit(solution)/shard_map/ppermute | solution.py:38
  22.6 8.5 %collective-permute-start.7 = (bf16[4,2,48,512]{3,2,1,0:T(8,128)(2,1)S(1)}, bf16[4,2,48,512]{3,2,1,0:T(8,128)(2,1)S(1)}, u32[]{:S(2)}, u32[]{:S(2)}) collective-permute-start(bf16[4,2,48,512]{3,2,1,0:T(8,128)(2,1)S(1)} %fusion.3), channel_id=1, source_target_pairs={{0,8},{4,36},{8,0},{12,44},{16,24},{20,52},{24,16},{28,60},{32,40}... | collective-permute-start | bytes 1179656 | tf_op jit(solution)/shard_map/ppermute | solution.py:38
  43.0 15.2 %collective-permute-start.10 = (bf16[2,2,48,512]{3,2,0,1:T(8,128)(2,1)S(1)}, bf16[2,2,48,512]{3,2,0,1:T(8,128)(2,1)S(1)}, u32[]{:S(2)}, u32[]{:S(2)}) collective-permute-start(bf16[2,2,48,512]{3,2,0,1:T(8,128)(2,1)S(1)} %fusion.4), channel_id=1, source_target_pairs={{0,128},{128,0},{1,129},{129,1},{2,130},{130,2},{3,131},{131,3},{4... | collective-permute-start | bytes 589832 | tf_op jit(solution)/shard_map/ppermute | solution.py:42
  50.0 13.0 %collective-permute-start.14 = (f32[2,48,512]{2,1,0:T(8,128)S(1)}, f32[2,48,512]{2,1,0:T(8,128)S(1)}, u32[]{:S(2)}, u32[]{:S(2)}) collective-permute-start(f32[2,48,512]{2,1,0:T(8,128)S(1)} %multiply_subtract_fusion), channel_id=1, source_target_pairs={{0,128},{128,0},{1,129},{129,1},{2,130},{130,2},{3,131},{131,3},{4... | collective-permute-start | bytes 589832 | tf_op jit(solution)/shard_map/ppermute | solution.py:42
  74.0 8.9 %collective-permute-start.16 = (bf16[2,2,48,512]{3,2,1,0:T(8,128)(2,1)S(1)}, bf16[2,2,48,512]{3,2,1,0:T(8,128)(2,1)S(1)}, u32[]{:S(2)}, u32[]{:S(2)}) collective-permute-start(bf16[2,2,48,512]{3,2,1,0:T(8,128)(2,1)S(1)} %get-tuple-element.66), channel_id=1, source_target_pairs={{0,24},{4,100},{8,16},{12,108},{16,8},{20,116},{24,0},{28,124},{32... | collective-permute-start | bytes 589832 | tf_op jit(solution)/shard_map/ppermute | solution.py:38
  74.9 8.2 %collective-permute-start.18 = (bf16[2,2,48,512]{3,2,1,0:T(8,128)(2,1)S(1)}, bf16[2,2,48,512]{3,2,1,0:T(8,128)(2,1)S(1)}, u32[]{:S(2)}, u32[]{:S(2)}) collective-permute-start(bf16[2,2,48,512]{3,2,1,0:T(8,128)(2,1)S(1)} %get-tuple-element.66), channel_id=1, source_target_pairs={{0,96},{4,28},{8,104},{12,20},{16,112},{20,12},{24,120},{28,4},{32... | collective-permute-start | bytes 589832 | tf_op jit(solution)/shard_map/ppermute | solution.py:38
  77.9 8.7 %collective-permute-start.30 = (bf16[2,2,48,512]{3,2,1,0:T(8,128)(2,1)S(1)}, bf16[2,2,48,512]{3,2,1,0:T(8,128)(2,1)S(1)}, u32[]{:S(2)}, u32[]{:S(2)}) collective-permute-start(bf16[2,2,48,512]{3,2,1,0:T(8,128)(2,1)S(1)} %get-tuple-element.64), channel_id=1, source_target_pairs={{0,24},{4,100},{8,16},{12,108},{16,8},{20,116},{24,0},{28,124},{32... | collective-permute-start | bytes 589832 | tf_op jit(solution)/shard_map/ppermute | solution.py:38
  78.9 9.9 %collective-permute-start.32 = (bf16[2,2,48,512]{3,2,1,0:T(8,128)(2,1)S(1)}, bf16[2,2,48,512]{3,2,1,0:T(8,128)(2,1)S(1)}, u32[]{:S(2)}, u32[]{:S(2)}) collective-permute-start(bf16[2,2,48,512]{3,2,1,0:T(8,128)(2,1)S(1)} %get-tuple-element.64), channel_id=1, source_target_pairs={{0,96},{4,28},{8,104},{12,20},{16,112},{20,12},{24,120},{28,4},{32... | collective-permute-start | bytes 589832 | tf_op jit(solution)/shard_map/ppermute | solution.py:38
  81.5 19.9 %collective-permute-start.13 = (bf16[128,768]{1,0:T(8,128)(2,1)S(1)}, bf16[128,768]{1,0:T(8,128)(2,1)S(1)}, u32[]{:S(2)}, u32[]{:S(2)}) collective-permute-start(bf16[128,768]{1,0:T(8,128)(2,1)S(1)} %copy-done.6), channel_id=1, source_target_pairs={{0,3},{1,2},{2,1},{3,0},{4,7},{5,6},{6,5},{7,4},{8,11},{9,10},{10,... | collective-permute-start | bytes 589832 | tf_op jit(solution)/shard_map/ppermute | solution.py:46
  82.9 19.0 %collective-permute-start.12 = (bf16[128,768]{1,0:T(8,128)(2,1)S(1)}, bf16[128,768]{1,0:T(8,128)(2,1)S(1)}, u32[]{:S(2)}, u32[]{:S(2)}) collective-permute-start(bf16[128,768]{1,0:T(8,128)(2,1)S(1)} %copy-done.6), channel_id=1, source_target_pairs={{0,2},{1,3},{2,0},{3,1},{4,6},{5,7},{6,4},{7,5},{8,10},{9,11},{10,... | collective-permute-start | bytes 589832 | tf_op jit(solution)/shard_map/ppermute | solution.py:46
  86.6 18.9 %collective-permute-start.17 = (bf16[2,2,2,48,512]{4,3,2,1,0:T(8,128)(2,1)S(1)}, bf16[2,2,2,48,512]{4,3,2,1,0:T(8,128)(2,1)S(1)}, u32[]{:S(2)}, u32[]{:S(2)}) collective-permute-start(bf16[2,2,2,48,512]{4,3,2,1,0:T(8,128)(2,1)S(1)} %get-tuple-element.59.refs_0_), channel_id=1, source_target_pairs={{0,8},{4,36},{8,0},{12,44},{16,24},{20,52},{24,16},{28,60},{32,40}... | collective-permute-start | bytes 1179656 | tf_op jit(solution)/shard_map/ppermute | solution.py:38
  90.2 15.4 %collective-permute-start.31 = (bf16[2,2,2,48,512]{4,3,2,1,0:T(8,128)(2,1)S(1)}, bf16[2,2,2,48,512]{4,3,2,1,0:T(8,128)(2,1)S(1)}, u32[]{:S(2)}, u32[]{:S(2)}) collective-permute-start(bf16[2,2,2,48,512]{4,3,2,1,0:T(8,128)(2,1)S(1)} %get-tuple-element.55.refs_0_), channel_id=1, source_target_pairs={{0,8},{4,36},{8,0},{12,44},{16,24},{20,52},{24,16},{28,60},{32,40}... | collective-permute-start | bytes 1179656 | tf_op jit(solution)/shard_map/ppermute | solution.py:38
  101.9 21.1 %collective-permute-start.21 = (bf16[2,2,2,2,48,512]{5,4,3,2,1,0:T(8,128)(2,1)}, bf16[2,2,2,2,48,512]{5,4,3,2,1,0:T(8,128)(2,1)S(1)}, u32[]{:S(2)}, u32[]{:S(2)}) collective-permute-start(bf16[2,2,2,2,48,512]{5,4,3,2,1,0:T(8,128)(2,1)} %pad_maximum_fusion), channel_id=1, source_target_pairs={{0,4},{4,0},{1,5},{5,1},{2,6},{6,2},{3,7},{7,3},{8,12},{12,8},{9,1... | collective-permute-start | bytes 2359304 | tf_op jit(solution)/shard_map/ppermute | solution.py:42
  104.1 9.6 %collective-permute-start.34 = (bf16[2,2,2,48,512]{4,3,2,1,0:T(8,128)(2,1)S(1)}, bf16[2,2,2,48,512]{4,3,2,1,0:T(8,128)(2,1)}, u32[]{:S(2)}, u32[]{:S(2)}) collective-permute-start(bf16[2,2,2,48,512]{4,3,2,1,0:T(8,128)(2,1)S(1)} %get-tuple-element.57.refs_2_), channel_id=1, source_target_pairs={{0,24},{4,100},{8,16},{12,108},{16,8},{20,116},{24,0},{28,124},{32... | collective-permute-start | bytes 1179656 | tf_op jit(solution)/shard_map/ppermute | solution.py:38
  105.5 26.8 %collective-permute-start.35 = (bf16[2,2,2,2,48,512]{5,4,3,2,1,0:T(8,128)(2,1)}, bf16[2,2,2,2,48,512]{5,4,3,2,1,0:T(8,128)(2,1)S(1)}, u32[]{:S(2)}, u32[]{:S(2)}) collective-permute-start(bf16[2,2,2,2,48,512]{5,4,3,2,1,0:T(8,128)(2,1)} %pad_maximum_fusion.1), channel_id=1, source_target_pairs={{0,4},{4,0},{1,5},{5,1},{2,6},{6,2},{3,7},{7,3},{8,12},{12,8},{9,1... | collective-permute-start | bytes 2359304 | tf_op jit(solution)/shard_map/ppermute | solution.py:42
  109.4 13.6 %collective-permute-start.23 = (bf16[2,2,2,48,512]{4,3,2,1,0:T(8,128)(2,1)}, bf16[2,2,2,48,512]{4,3,2,1,0:T(8,128)(2,1)}, u32[]{:S(2)}, u32[]{:S(2)}) collective-permute-start(bf16[2,2,2,48,512]{4,3,2,1,0:T(8,128)(2,1)} %collective-permute-done.20.refs_3_), channel_id=1, source_target_pairs={{0,4},{4,0},{1,5},{5,1},{2,6},{6,2},{3,7},{7,3},{8,12},{12,8},{9,1... | collective-permute-start | bytes 1179656 | tf_op jit(solution)/shard_map/ppermute | solution.py:42
  113.6 15.2 %collective-permute-start.36 = (bf16[2,2,2,48,512]{4,3,2,1,0:T(8,128)(2,1)S(1)}, bf16[2,2,2,48,512]{4,3,2,1,0:T(8,128)(2,1)}, u32[]{:S(2)}, u32[]{:S(2)}) collective-permute-start(bf16[2,2,2,48,512]{4,3,2,1,0:T(8,128)(2,1)S(1)} %collective-permute-done.31.refs_1_), channel_id=1, source_target_pairs={{0,4},{4,0},{1,5},{5,1},{2,6},{6,2},{3,7},{7,3},{8,12},{12,8},{9,1... | collective-permute-start | bytes 1179656 | tf_op jit(solution)/shard_map/ppermute | solution.py:42
  114.4 17.9 %collective-permute-start.37 = (bf16[2,2,2,48,512]{4,3,2,1,0:T(8,128)(2,1)}, bf16[2,2,2,48,512]{4,3,2,1,0:T(8,128)(2,1)}, u32[]{:S(2)}, u32[]{:S(2)}) collective-permute-start(bf16[2,2,2,48,512]{4,3,2,1,0:T(8,128)(2,1)} %collective-permute-done.34.refs_3_), channel_id=1, source_target_pairs={{0,4},{4,0},{1,5},{5,1},{2,6},{6,2},{3,7},{7,3},{8,12},{12,8},{9,1... | collective-permute-start | bytes 1179656 | tf_op jit(solution)/shard_map/ppermute | solution.py:42
  127.8 10.0 %collective-permute-start.25 = (bf16[128,512]{1,0:T(8,128)(2,1)S(1)}, bf16[128,512]{1,0:T(8,128)(2,1)S(1)}, u32[]{:S(2)}, u32[]{:S(2)}) collective-permute-start(bf16[128,512]{1,0:T(8,128)(2,1)S(1)} %shard_map.98.refs_0_), channel_id=1, source_target_pairs={{0,2},{1,3},{2,0},{3,1},{4,6},{5,7},{6,4},{7,5},{8,10},{9,11},{10,... | collective-permute-start | bytes 393224 | tf_op jit(solution)/shard_map/ppermute | solution.py:46
  127.9 9.9 %collective-permute-start.24 = (bf16[128,512]{1,0:T(8,128)(2,1)S(1)}, bf16[128,512]{1,0:T(8,128)(2,1)S(1)}, u32[]{:S(2)}, u32[]{:S(2)}) collective-permute-start(bf16[128,512]{1,0:T(8,128)(2,1)S(1)} %shard_map.98.refs_0_), channel_id=1, source_target_pairs={{0,1},{1,0},{2,3},{3,2},{4,5},{5,4},{6,7},{7,6},{8,9},{9,8},{10,11... | collective-permute-start | bytes 393224 | tf_op jit(solution)/shard_map/ppermute | solution.py:46
  128.9 10.8 %collective-permute-start.38 = (bf16[128,512]{1,0:T(8,128)(2,1)S(1)}, bf16[128,512]{1,0:T(8,128)(2,1)S(1)}, u32[]{:S(2)}, u32[]{:S(2)}) collective-permute-start(bf16[128,512]{1,0:T(8,128)(2,1)S(1)} %shard_map.98.refs_0_), channel_id=1, source_target_pairs={{0,3},{1,2},{2,1},{3,0},{4,7},{5,6},{6,5},{7,4},{8,11},{9,10},{10,... | collective-permute-start | bytes 393224 | tf_op jit(solution)/shard_map/ppermute | solution.py:46
  142.2 13.7 %collective-permute-start.40 = (bf16[128,512]{1,0:T(8,128)(2,1)S(1)}, bf16[128,512]{1,0:T(8,128)(2,1)S(1)}, u32[]{:S(2)}, u32[]{:S(2)}) collective-permute-start(bf16[128,512]{1,0:T(8,128)(2,1)S(1)} %get-tuple-element.44), channel_id=1, source_target_pairs={{0,2},{1,3},{2,0},{3,1},{4,6},{5,7},{6,4},{7,5},{8,10},{9,11},{10,... | collective-permute-start | bytes 393224 | tf_op jit(solution)/shard_map/ppermute | solution.py:46
  145.5 10.4 %collective-permute-start.41 = (bf16[128,512]{1,0:T(8,128)(2,1)S(1)}, bf16[128,512]{1,0:T(8,128)(2,1)S(1)}, u32[]{:S(2)}, u32[]{:S(2)}) collective-permute-start(bf16[128,512]{1,0:T(8,128)(2,1)S(1)} %get-tuple-element.45), channel_id=1, source_target_pairs={{0,1},{1,0},{2,3},{3,2},{4,5},{5,4},{6,7},{7,6},{8,9},{9,8},{10,11... | collective-permute-start | bytes 393224 | tf_op jit(solution)/shard_map/ppermute | solution.py:46
  (39 other events, 207.5 us)

commit v3 on v2

--- a/solution.py
+++ b/solution.py
@@ -68,21 +68,21 @@
     def body(grads_ref, received_ref, *outs):
         zh, y, x, c = (lax.axis_index(name) for name in OWNERS)
         first, second = jnp.where(c == 0, x, y), jnp.where(c == 0, y, x)
-        for half in range(2):
-
-            def step(n, carry, half=half):
-                i, j, z = n >> 3, (n >> 1) & 3, n & 1
+        for n0 in range(4):
+
+            def step(n, carry, n0=n0):
+                j, z = n >> 1, n & 1
                 chip = owner_of(
-                    c, first ^ place(2 * half + i, NEAR[m]), second ^ place(j, SECOND_NEAR[m])
+                    c, first ^ place(n0, NEAR[m]), second ^ place(j, SECOND_NEAR[m])
                 )
                 chip = chip + (zh ^ z) * 16
                 total = grads_ref[m, chip, c].astype(F32) + received_ref[chip].astype(F32)
-                outs[half][i, j, z] = total.astype(BF16)
+                outs[n0][j, z] = total.astype(BF16)
                 return carry
 
-            lax.fori_loop(0, 16, step, 0)
-
-    return local(body, [grads, received], [((2, 4, 2, rows, cols), BF16)] * 2, 20)
+            lax.fori_loop(0, 8, step, 0)
+
+    return local(body, [grads, received], [((4, 2, rows, cols), BF16)] * 4, 20)
 
 
 def all_rows(own, other, m, pieces):
@@ -309,21 +309,28 @@
     matrices, rows, cols = outer_params.shape
     grads = pseudo_grad.reshape(matrices, 32, 2, rows, cols)
 
-    received = []
+    received, source = [], grads
     for m in range(matrices):
-        send = lax.dynamic_slice(grads, (m, 0, 1 - c, 0, 0), (1, 32, 1, rows, cols))
-        received.append(swap(send.reshape(32, rows, cols), "c"))
+        send = lax.dynamic_slice(source, (m, 0, 1 - c, 0, 0), (1, 32, 1, rows, cols)).reshape(
+            32, rows, cols
+        )
+        if m == 0:
+            source, send = lax.optimization_barrier((source, send))
+        received.append(swap(send, "c"))
     kept = []
     for m in range(matrices):
-        keep, send = pair_sums(grads, received[m], m)
+        near = NEAR[m]
+        sums = pair_sums(grads, received[m], m)
         if m == 1:
-            acts, old_outer, old_momentum, send = lax.optimization_barrier(
-                (acts, outer_params, momentum, send)
+            acts, old_outer, old_momentum, sums = lax.optimization_barrier(
+                (acts, outer_params, momentum, sums)
             )
-        got = plane_swap(send, NEAR[m], True)
-        total = keep.astype(F32) + got.astype(F32)
-        got = plane_swap(total[1].astype(BF16), NEAR[m] ^ 2, True)
-        kept.append(total[0] + got.astype(F32))
+        got = plane_swap(sums[3], near, True)
+        far = sums[1].astype(F32) + got.astype(F32)
+        got = plane_swap(sums[2], near, True)
+        total = sums[0].astype(F32) + got.astype(F32)
+        got = plane_swap(far.astype(BF16), near ^ 2, True)
+        kept.append(total + got.astype(F32))
     acts_parts = [acts] + [mp_swap(acts, k) for k in (1, 2, 3)]
     far_state = swap(old_outer - outer_rate * outer_beta**2 * old_momentum, "zh")
     normed, turned, gram, probs, moved = prepare(

time: 169 us -> 166 us (0.982)
  starting transfers between devices: 59 us -> 55.3 us
    ppermute x20 -> x22, starting transfers between devices: 30.9 us -> 29.7 us  [plane_swap(): return lax.ppermute(value, PLANE, pairs)]
    reshape x1 -> x2, local copies, waits for them, and re-layouts: 2.26 us -> 3.51 us  [shards(): lax.dynamic_slice(source, (m, 0, 1 - c, 0, 0), (1, 32, 1, rows, cols))]
    ppermute x20 -> x22, waiting for transfers between devices: 33.6 us -> 34.4 us  [plane_swap(): return lax.ppermute(value, PLANE, pairs)]
  transfers between devices with their start and end apart: 44 -> 46, of which waited for: 24 -> 24; matrix products, arithmetic and copies ran while one was open for 2% -> 2% of each run, Pallas kernels for 5% -> 5%
where the time goes in v3:
time: 166 us; the launch traced here: 164 us
  waiting for transfers between devices  77.2 us (47%)
  starting transfers between devices  55.3 us (33%)
  local copies, waits for them, and re-layouts  14.2 us (9%)
  Pallas kernels  12.6 us (8%)
  other arithmetic  3.91 us (2%)
    ppermute x22, waiting for transfers between devices, plane_swap(): return lax.ppermute(value, PLANE, pairs)  34.4 us
    ppermute x22, starting transfers between devices, plane_swap(): return lax.ppermute(value, PLANE, pairs)  29.7 us
    ppermute x14, waiting for transfers between devices, mp_swap(): return lax.ppermute(value, 'mp', [(i, i ^ mask) for i in range(4)])  28.2 us
    ppermute x14, starting transfers between devices, mp_swap(): return lax.ppermute(value, 'mp', [(i, i ^ mask) for i in range(4)])  17.8 us
    ppermute x10, waiting for transfers between devices, swap(): return lax.ppermute(value, axis, [(0, 1), (1, 0)])  14.6 us
    pallas_call x11, Pallas kernels, local(): pl.pallas_call(body, in_specs=[spec] * len(ins), out_specs=[spec] * len(o...  10.4 us
    unnamed x38, local copies, waits for them, and re-layouts  9.86 us
    ppermute x10, starting transfers between devices, swap(): return lax.ppermute(value, axis, [(0, 1), (1, 0)])  7.83 us
  transfers between devices with their start and end apart: 46, of which 24 were waited for; matrix products, arithmetic and copies ran while one was open for 2% of the time, Pallas kernels for 5%

profile of v3, /device:TPU:2, one launch (start us, length us, event | category | flops | bytes accessed | tf_op | source)
XLA Modules:
  0.0 164.5 jit_solution(7020922976601722892)
XLA Ops:
  4.8 2.9 %collective-permute-done.6.received_ref = bf16[32,48,512]{2,1,0:T(8,128)(2,1)S(1)} collective-permute-done((bf16[32,48,512]{2,1,0:T(8,128)(2,1)S(1)}, bf16[32,48,512]{2,1,0:T(8,128)(2,1)S(1)}, u32[]{:S(2)}, u32[]{:S(2)}) %collective-permute-start.6) | collective-permute-done | bytes 1572896 | tf_op jit(solution)/shard_map/ppermute | solution.py:42
  10.6 2.3 %collective-permute-start.2 = (bf16[4,2,48,512]{3,2,1,0:T(8,128)(2,1)S(1)}, bf16[4,2,48,512]{3,2,1,0:T(8,128)(2,1)S(1)}, u32[]{:S(2)}, u32[]{:S(2)}) collective-permute-start(bf16[4,2,48,512]{3,2,1,0:T(8,128)(2,1)S(1)} %get-tuple-element.39), channel_id=1, source_target_pairs={{0,8},{4,36},{8,0},{12,44},{16,24},{20,52},{24,16},{28,60},{32,40}... | collective-permute-start | bytes 1179656 | tf_op jit(solution)/shard_map/ppermute | solution.py:38
  16.4 3.5 %collective-permute-start.9 = (bf16[4,2,48,512]{3,2,1,0:T(8,128)(2,1)S(1)}, bf16[4,2,48,512]{3,2,1,0:T(8,128)(2,1)S(1)}, u32[]{:S(2)}, u32[]{:S(2)}) collective-permute-start(bf16[4,2,48,512]{3,2,1,0:T(8,128)(2,1)S(1)} %add_convert_fusion), channel_id=1, source_target_pairs={{0,8},{4,36},{8,0},{12,44},{16,24},{20,52},{24,16},{28,60},{32,40}... | collective-permute-start | bytes 1179656 | tf_op jit(solution)/shard_map/ppermute | solution.py:38
  20.7 5.0 %collective-permute-done.9 = bf16[4,2,48,512]{3,2,1,0:T(8,128)(2,1)S(1)} collective-permute-done((bf16[4,2,48,512]{3,2,1,0:T(8,128)(2,1)S(1)}, bf16[4,2,48,512]{3,2,1,0:T(8,128)(2,1)S(1)}, u32[]{:S(2)}, u32[]{:S(2)}) %collective-permute-start.9) | collective-permute-done | bytes 393248 | tf_op jit(solution)/shard_map/ppermute | solution.py:38
  26.1 5.9 %collective-permute-done.1 = bf16[4,2,48,512]{3,2,1,0:T(8,128)(2,1)S(1)} collective-permute-done((bf16[4,2,48,512]{3,2,1,0:T(8,128)(2,1)S(1)}, bf16[4,2,48,512]{3,2,1,0:T(8,128)(2,1)S(1)}, u32[]{:S(2)}, u32[]{:S(2)}) %collective-permute-start.1) | collective-permute-done | bytes 393248 | tf_op jit(solution)/shard_map/ppermute | solution.py:38
  35.7 3.5 %collective-permute-done.4 = bf16[2,2,48,512]{3,2,1,0:T(8,128)(2,1)S(1)} collective-permute-done((bf16[2,2,48,512]{3,2,1,0:T(8,128)(2,1)S(1)}, bf16[2,2,48,512]{3,2,1,0:T(8,128)(2,1)S(1)}, u32[]{:S(2)}, u32[]{:S(2)}) %collective-permute-start.4) | collective-permute-done | bytes 196640 | tf_op jit(solution)/shard_map/ppermute | solution.py:38
  40.2 3.7 %collective-permute-done.5 = bf16[2,48,512]{2,1,0:T(8,128)(2,1)S(1)} collective-permute-done((bf16[2,48,512]{2,1,0:T(8,128)(2,1)S(1)}, bf16[2,48,512]{2,1,0:T(8,128)(2,1)S(1)}, u32[]{:S(2)}, u32[]{:S(2)}) %collective-permute-start.5) | collective-permute-done | bytes 98336 | tf_op jit(solution)/shard_map/ppermute | solution.py:38
  44.0 5.7 %collective-permute-start.12 = (bf16[2,2,48,512]{3,2,0,1:T(8,128)(2,1)S(1)}, bf16[2,2,48,512]{3,2,0,1:T(8,128)(2,1)S(1)}, u32[]{:S(2)}, u32[]{:S(2)}) collective-permute-start(bf16[2,2,48,512]{3,2,0,1:T(8,128)(2,1)S(1)} %fusion), channel_id=1, source_target_pairs={{0,128},{128,0},{1,129},{129,1},{2,130},{130,2},{3,131},{131,3},{4... | collective-permute-start | bytes 589832 | tf_op jit(solution)/shard_map/ppermute | solution.py:42
  50.1 7.1 %collective-permute-done.12 = bf16[2,2,48,512]{3,2,0,1:T(8,128)(2,1)S(1)} collective-permute-done((bf16[2,2,48,512]{3,2,0,1:T(8,128)(2,1)S(1)}, bf16[2,2,48,512]{3,2,0,1:T(8,128)(2,1)S(1)}, u32[]{:S(2)}, u32[]{:S(2)}) %collective-permute-start.12) | collective-permute-done | bytes 196640 | tf_op jit(solution)/shard_map/ppermute | solution.py:42
  57.4 4.6 %collective-permute-done.16 = f32[2,48,512]{2,1,0:T(8,128)S(1)} collective-permute-done((f32[2,48,512]{2,1,0:T(8,128)S(1)}, f32[2,48,512]{2,1,0:T(8,128)S(1)}, u32[]{:S(2)}, u32[]{:S(2)}) %collective-permute-start.16) | collective-permute-done | bytes 196640 | tf_op jit(solution)/shard_map/ppermute | solution.py:42
  62.9 2.4 %collective-permute-start.28 = (bf16[24,512]{1,0:T(8,128)(2,1)S(1)}, bf16[24,512]{1,0:T(8,128)(2,1)S(1)}, u32[]{:S(2)}, u32[]{:S(2)}) collective-permute-start(bf16[24,512]{1,0:T(8,128)(2,1)S(1)} %get-tuple-element.56), channel_id=1, source_target_pairs={{0,1},{1,0},{2,3},{3,2},{4,5},{5,4},{6,7},{7,6},{8,9},{9,8},{10,11... | collective-permute-start | bytes 73736 | tf_op jit(solution)/shard_map/ppermute | solution.py:46
  74.8 3.0 %collective-permute-start.20 = (bf16[2,2,48,512]{3,2,1,0:T(8,128)(2,1)S(1)}, bf16[2,2,48,512]{3,2,1,0:T(8,128)(2,1)S(1)}, u32[]{:S(2)}, u32[]{:S(2)}) collective-permute-start(bf16[2,2,48,512]{3,2,1,0:T(8,128)(2,1)S(1)} %get-tuple-element.82), channel_id=1, source_target_pairs={{0,96},{4,28},{8,104},{12,20},{16,112},{20,12},{24,120},{28,4},{32... | collective-permute-start | bytes 589832 | tf_op jit(solution)/shard_map/ppermute | solution.py:38
  78.6 3.0 %collective-permute-start.34 = (bf16[2,2,48,512]{3,2,1,0:T(8,128)(2,1)S(1)}, bf16[2,2,48,512]{3,2,1,0:T(8,128)(2,1)S(1)}, u32[]{:S(2)}, u32[]{:S(2)}) collective-permute-start(bf16[2,2,48,512]{3,2,1,0:T(8,128)(2,1)S(1)} %get-tuple-element.80), channel_id=1, source_target_pairs={{0,96},{4,28},{8,104},{12,20},{16,112},{20,12},{24,120},{28,4},{32... | collective-permute-start | bytes 589832 | tf_op jit(solution)/shard_map/ppermute | solution.py:38
  83.6 2.5 %collective-permute-start.21 = (bf16[2,2,48,512]{3,2,1,0:T(8,128)(2,1)S(1)}, bf16[2,2,48,512]{3,2,1,0:T(8,128)(2,1)S(1)}, u32[]{:S(2)}, u32[]{:S(2)}) collective-permute-start(bf16[2,2,48,512]{3,2,1,0:T(8,128)(2,1)S(1)} %collective-permute-done.20), channel_id=1, source_target_pairs={{0,8},{4,36},{8,0},{12,44},{16,24},{20,52},{24,16},{28,60},{32,40}... | collective-permute-start | bytes 589832 | tf_op jit(solution)/shard_map/ppermute | solution.py:38
  91.7 4.3 %collective-permute-done.35 = bf16[2,2,48,512]{3,2,1,0:T(8,128)(2,1)S(1)} collective-permute-done((bf16[2,2,48,512]{3,2,1,0:T(8,128)(2,1)S(1)}, bf16[2,2,48,512]{3,2,1,0:T(8,128)(2,1)S(1)}, u32[]{:S(2)}, u32[]{:S(2)}) %collective-permute-start.35) | collective-permute-done | bytes 196640 | tf_op jit(solution)/shard_map/ppermute | solution.py:38
  99.2 2.5 %collective-permute-done.13.refs_1_ = bf16[128,768]{1,0:T(8,128)(2,1)S(1)} collective-permute-done((bf16[128,768]{1,0:T(8,128)(2,1)S(1)}, bf16[128,768]{1,0:T(8,128)(2,1)S(1)}, u32[]{:S(2)}, u32[]{:S(2)}) %collective-permute-start.13) | collective-permute-done | bytes 196640 | tf_op jit(solution)/shard_map/ppermute | solution.py:46
  104.1 2.8 %collective-permute-done.22.refs_3_ = bf16[2,2,2,48,512]{4,3,2,1,0:T(8,128)(2,1)} collective-permute-done((bf16[2,2,2,48,512]{4,3,2,1,0:T(8,128)(2,1)S(1)}, bf16[2,2,2,48,512]{4,3,2,1,0:T(8,128)(2,1)}, u32[]{:S(2)}, u32[]{:S(2)}) %collective-permute-start.22) | collective-permute-done | bytes 393248 | tf_op jit(solution)/shard_map/ppermute | solution.py:38
  106.9 4.2 %collective-permute-done.36.refs_3_ = bf16[2,2,2,48,512]{4,3,2,1,0:T(8,128)(2,1)} collective-permute-done((bf16[2,2,2,48,512]{4,3,2,1,0:T(8,128)(2,1)S(1)}, bf16[2,2,2,48,512]{4,3,2,1,0:T(8,128)(2,1)}, u32[]{:S(2)}, u32[]{:S(2)}) %collective-permute-start.36) | collective-permute-done | bytes 393248 | tf_op jit(solution)/shard_map/ppermute | solution.py:38
  131.7 5.4 %collective-permute-done.27.refs_2_ = bf16[128,512]{1,0:T(8,128)(2,1)S(1)} collective-permute-done((bf16[128,512]{1,0:T(8,128)(2,1)S(1)}, bf16[128,512]{1,0:T(8,128)(2,1)S(1)}, u32[]{:S(2)}, u32[]{:S(2)}) %collective-permute-start.27) | collective-permute-done | bytes 131104 | tf_op jit(solution)/shard_map/ppermute | solution.py:46
  140.7 2.4 %collective-permute-start.42 = (bf16[128,512]{1,0:T(8,128)(2,1)S(1)}, bf16[128,512]{1,0:T(8,128)(2,1)S(1)}, u32[]{:S(2)}, u32[]{:S(2)}) collective-permute-start(bf16[128,512]{1,0:T(8,128)(2,1)S(1)} %get-tuple-element.62), channel_id=1, source_target_pairs={{0,2},{1,3},{2,0},{3,1},{4,6},{5,7},{6,4},{7,5},{8,10},{9,11},{10,... | collective-permute-start | bytes 393224 | tf_op jit(solution)/shard_map/ppermute | solution.py:46
  143.8 2.9 %collective-permute-done.41.refs_1_ = bf16[128,512]{1,0:T(8,128)(2,1)S(1)} collective-permute-done((bf16[128,512]{1,0:T(8,128)(2,1)S(1)}, bf16[128,512]{1,0:T(8,128)(2,1)S(1)}, u32[]{:S(2)}, u32[]{:S(2)}) %collective-permute-start.41) | collective-permute-done | bytes 131104 | tf_op jit(solution)/shard_map/ppermute | solution.py:46
  146.7 6.8 %collective-permute-done.42.refs_2_ = bf16[128,512]{1,0:T(8,128)(2,1)S(1)} collective-permute-done((bf16[128,512]{1,0:T(8,128)(2,1)S(1)}, bf16[128,512]{1,0:T(8,128)(2,1)S(1)}, u32[]{:S(2)}, u32[]{:S(2)}) %collective-permute-start.42) | collective-permute-done | bytes 131104 | tf_op jit(solution)/shard_map/ppermute | solution.py:46
  154.0 4.5 %collective-permute-done.44 = f32[8,128]{1,0:T(8,128)S(1)} collective-permute-done((f32[8,128]{1,0:T(8,128)S(1)}, f32[8,128]{1,0:T(8,128)S(1)}, u32[]{:S(2)}, u32[]{:S(2)}) %collective-permute-start.44) | collective-permute-done | bytes 4128 | tf_op jit(solution)/shard_map/ppermute | solution.py:46
  159.5 2.6 %collective-permute-done.45 = f32[8,128]{1,0:T(8,128)S(1)} collective-permute-done((f32[8,128]{1,0:T(8,128)S(1)}, f32[8,128]{1,0:T(8,128)S(1)}, u32[]{:S(2)}, u32[]{:S(2)}) %collective-permute-start.45) | collective-permute-done | bytes 4128 | tf_op jit(solution)/shard_map/ppermute | solution.py:46
  (152 shorter events, 69.8 us)
Async XLA Ops:
  10.6 9.4 %collective-permute-start.2 = (bf16[4,2,48,512]{3,2,1,0:T(8,128)(2,1)S(1)}, bf16[4,2,48,512]{3,2,1,0:T(8,128)(2,1)S(1)}, u32[]{:S(2)}, u32[]{:S(2)}) collective-permute-start(bf16[4,2,48,512]{3,2,1,0:T(8,128)(2,1)S(1)} %get-tuple-element.39), channel_id=1, source_target_pairs={{0,8},{4,36},{8,0},{12,44},{16,24},{20,52},{24,16},{28,60},{32,40}... | collective-permute-start | bytes 1179656 | tf_op jit(solution)/shard_map/ppermute | solution.py:38
  16.4 9.3 %collective-permute-start.9 = (bf16[4,2,48,512]{3,2,1,0:T(8,128)(2,1)S(1)}, bf16[4,2,48,512]{3,2,1,0:T(8,128)(2,1)S(1)}, u32[]{:S(2)}, u32[]{:S(2)}) collective-permute-start(bf16[4,2,48,512]{3,2,1,0:T(8,128)(2,1)S(1)} %add_convert_fusion), channel_id=1, source_target_pairs={{0,8},{4,36},{8,0},{12,44},{16,24},{20,52},{24,16},{28,60},{32,40}... | collective-permute-start | bytes 1179656 | tf_op jit(solution)/shard_map/ppermute | solution.py:38
  19.9 12.1 %collective-permute-start.1 = (bf16[4,2,48,512]{3,2,1,0:T(8,128)(2,1)S(1)}, bf16[4,2,48,512]{3,2,1,0:T(8,128)(2,1)S(1)}, u32[]{:S(2)}, u32[]{:S(2)}) collective-permute-start(bf16[4,2,48,512]{3,2,1,0:T(8,128)(2,1)S(1)} %get-tuple-element.37), channel_id=1, source_target_pairs={{0,8},{4,36},{8,0},{12,44},{16,24},{20,52},{24,16},{28,60},{32,40}... | collective-permute-start | bytes 1179656 | tf_op jit(solution)/shard_map/ppermute | solution.py:38
  20.1 11.9 %collective-permute-start.3 = (bf16[4,2,48,512]{3,2,1,0:T(8,128)(2,1)S(1)}, bf16[4,2,48,512]{3,2,1,0:T(8,128)(2,1)S(1)}, u32[]{:S(2)}, u32[]{:S(2)}) collective-permute-start(bf16[4,2,48,512]{3,2,1,0:T(8,128)(2,1)S(1)} %add_convert_fusion.1), channel_id=1, source_target_pairs={{0,24},{4,100},{8,16},{12,108},{16,8},{20,116},{24,0},{28,124},{32... | collective-permute-start | bytes 1179656 | tf_op jit(solution)/shard_map/ppermute | solution.py:38
  44.0 13.3 %collective-permute-start.12 = (bf16[2,2,48,512]{3,2,0,1:T(8,128)(2,1)S(1)}, bf16[2,2,48,512]{3,2,0,1:T(8,128)(2,1)S(1)}, u32[]{:S(2)}, u32[]{:S(2)}) collective-permute-start(bf16[2,2,48,512]{3,2,0,1:T(8,128)(2,1)S(1)} %fusion), channel_id=1, source_target_pairs={{0,128},{128,0},{1,129},{129,1},{2,130},{130,2},{3,131},{131,3},{4... | collective-permute-start | bytes 589832 | tf_op jit(solution)/shard_map/ppermute | solution.py:42
  49.7 12.3 %collective-permute-start.16 = (f32[2,48,512]{2,1,0:T(8,128)S(1)}, f32[2,48,512]{2,1,0:T(8,128)S(1)}, u32[]{:S(2)}, u32[]{:S(2)}) collective-permute-start(f32[2,48,512]{2,1,0:T(8,128)S(1)} %multiply_subtract_fusion), channel_id=1, source_target_pairs={{0,128},{128,0},{1,129},{129,1},{2,130},{130,2},{3,131},{131,3},{4... | collective-permute-start | bytes 589832 | tf_op jit(solution)/shard_map/ppermute | solution.py:42
  72.5 11.0 %collective-permute-start.18 = (bf16[2,2,48,512]{3,2,1,0:T(8,128)(2,1)S(1)}, bf16[2,2,48,512]{3,2,1,0:T(8,128)(2,1)S(1)}, u32[]{:S(2)}, u32[]{:S(2)}) collective-permute-start(bf16[2,2,48,512]{3,2,1,0:T(8,128)(2,1)S(1)} %get-tuple-element.82), channel_id=1, source_target_pairs={{0,24},{4,100},{8,16},{12,108},{16,8},{20,116},{24,0},{28,124},{32... | collective-permute-start | bytes 589832 | tf_op jit(solution)/shard_map/ppermute | solution.py:38
  74.8 8.8 %collective-permute-start.20 = (bf16[2,2,48,512]{3,2,1,0:T(8,128)(2,1)S(1)}, bf16[2,2,48,512]{3,2,1,0:T(8,128)(2,1)S(1)}, u32[]{:S(2)}, u32[]{:S(2)}) collective-permute-start(bf16[2,2,48,512]{3,2,1,0:T(8,128)(2,1)S(1)} %get-tuple-element.82), channel_id=1, source_target_pairs={{0,96},{4,28},{8,104},{12,20},{16,112},{20,12},{24,120},{28,4},{32... | collective-permute-start | bytes 589832 | tf_op jit(solution)/shard_map/ppermute | solution.py:38
  81.5 17.4 %collective-permute-start.15 = (bf16[128,768]{1,0:T(8,128)(2,1)S(1)}, bf16[128,768]{1,0:T(8,128)(2,1)S(1)}, u32[]{:S(2)}, u32[]{:S(2)}) collective-permute-start(bf16[128,768]{1,0:T(8,128)(2,1)S(1)} %copy-done.6), channel_id=1, source_target_pairs={{0,3},{1,2},{2,1},{3,0},{4,7},{5,6},{6,5},{7,4},{8,11},{9,10},{10,... | collective-permute-start | bytes 589832 | tf_op jit(solution)/shard_map/ppermute | solution.py:46
  83.5 15.6 %collective-permute-start.14 = (bf16[128,768]{1,0:T(8,128)(2,1)S(1)}, bf16[128,768]{1,0:T(8,128)(2,1)S(1)}, u32[]{:S(2)}, u32[]{:S(2)}) collective-permute-start(bf16[128,768]{1,0:T(8,128)(2,1)S(1)} %copy-done.6), channel_id=1, source_target_pairs={{0,2},{1,3},{2,0},{3,1},{4,6},{5,7},{6,4},{7,5},{8,10},{9,11},{10,... | collective-permute-start | bytes 589832 | tf_op jit(solution)/shard_map/ppermute | solution.py:46
  86.1 16.7 %collective-permute-start.19 = (bf16[2,2,2,48,512]{4,3,2,1,0:T(8,128)(2,1)S(1)}, bf16[2,2,2,48,512]{4,3,2,1,0:T(8,128)(2,1)S(1)}, u32[]{:S(2)}, u32[]{:S(2)}) collective-permute-start(bf16[2,2,2,48,512]{4,3,2,1,0:T(8,128)(2,1)S(1)} %get-tuple-element.75.refs_0_), channel_id=1, source_target_pairs={{0,8},{4,36},{8,0},{12,44},{16,24},{20,52},{24,16},{28,60},{32,40}... | collective-permute-start | bytes 1179656 | tf_op jit(solution)/shard_map/ppermute | solution.py:38
  87.1 8.9 %collective-permute-start.35 = (bf16[2,2,48,512]{3,2,1,0:T(8,128)(2,1)S(1)}, bf16[2,2,48,512]{3,2,1,0:T(8,128)(2,1)S(1)}, u32[]{:S(2)}, u32[]{:S(2)}) collective-permute-start(bf16[2,2,48,512]{3,2,1,0:T(8,128)(2,1)S(1)} %collective-permute-done.34), channel_id=1, source_target_pairs={{0,8},{4,36},{8,0},{12,44},{16,24},{20,52},{24,16},{28,60},{32,40}... | collective-permute-start | bytes 589832 | tf_op jit(solution)/shard_map/ppermute | solution.py:38
  89.7 13.3 %collective-permute-start.33 = (bf16[2,2,2,48,512]{4,3,2,1,0:T(8,128)(2,1)S(1)}, bf16[2,2,2,48,512]{4,3,2,1,0:T(8,128)(2,1)S(1)}, u32[]{:S(2)}, u32[]{:S(2)}) collective-permute-start(bf16[2,2,2,48,512]{4,3,2,1,0:T(8,128)(2,1)S(1)} %get-tuple-element.71.refs_0_), channel_id=1, source_target_pairs={{0,8},{4,36},{8,0},{12,44},{16,24},{20,52},{24,16},{28,60},{32,40}... | collective-permute-start | bytes 1179656 | tf_op jit(solution)/shard_map/ppermute | solution.py:38
  99.1 21.4 %collective-permute-start.23 = (bf16[2,2,2,2,48,512]{5,4,3,2,1,0:T(8,128)(2,1)}, bf16[2,2,2,2,48,512]{5,4,3,2,1,0:T(8,128)(2,1)S(1)}, u32[]{:S(2)}, u32[]{:S(2)}) collective-permute-start(bf16[2,2,2,2,48,512]{5,4,3,2,1,0:T(8,128)(2,1)} %pad_maximum_fusion), channel_id=1, source_target_pairs={{0,4},{4,0},{1,5},{5,1},{2,6},{6,2},{3,7},{7,3},{8,12},{12,8},{9,1... | collective-permute-start | bytes 2359304 | tf_op jit(solution)/shard_map/ppermute | solution.py:42
  101.7 9.4 %collective-permute-start.36 = (bf16[2,2,2,48,512]{4,3,2,1,0:T(8,128)(2,1)S(1)}, bf16[2,2,2,48,512]{4,3,2,1,0:T(8,128)(2,1)}, u32[]{:S(2)}, u32[]{:S(2)}) collective-permute-start(bf16[2,2,2,48,512]{4,3,2,1,0:T(8,128)(2,1)S(1)} %get-tuple-element.73.refs_2_), channel_id=1, source_target_pairs={{0,24},{4,100},{8,16},{12,108},{16,8},{20,116},{24,0},{28,124},{32... | collective-permute-start | bytes 1179656 | tf_op jit(solution)/shard_map/ppermute | solution.py:38
  102.7 27.0 %collective-permute-start.37 = (bf16[2,2,2,2,48,512]{5,4,3,2,1,0:T(8,128)(2,1)}, bf16[2,2,2,2,48,512]{5,4,3,2,1,0:T(8,128)(2,1)S(1)}, u32[]{:S(2)}, u32[]{:S(2)}) collective-permute-start(bf16[2,2,2,2,48,512]{5,4,3,2,1,0:T(8,128)(2,1)} %pad_maximum_fusion.1), channel_id=1, source_target_pairs={{0,4},{4,0},{1,5},{5,1},{2,6},{6,2},{3,7},{7,3},{8,12},{12,8},{9,1... | collective-permute-start | bytes 2359304 | tf_op jit(solution)/shard_map/ppermute | solution.py:42
  106.9 13.6 %collective-permute-start.25 = (bf16[2,2,2,48,512]{4,3,2,1,0:T(8,128)(2,1)}, bf16[2,2,2,48,512]{4,3,2,1,0:T(8,128)(2,1)}, u32[]{:S(2)}, u32[]{:S(2)}) collective-permute-start(bf16[2,2,2,48,512]{4,3,2,1,0:T(8,128)(2,1)} %collective-permute-done.22.refs_3_), channel_id=1, source_target_pairs={{0,4},{4,0},{1,5},{5,1},{2,6},{6,2},{3,7},{7,3},{8,12},{12,8},{9,1... | collective-permute-start | bytes 1179656 | tf_op jit(solution)/shard_map/ppermute | solution.py:42
  111.1 17.2 %collective-permute-start.38 = (bf16[2,2,2,48,512]{4,3,2,1,0:T(8,128)(2,1)S(1)}, bf16[2,2,2,48,512]{4,3,2,1,0:T(8,128)(2,1)}, u32[]{:S(2)}, u32[]{:S(2)}) collective-permute-start(bf16[2,2,2,48,512]{4,3,2,1,0:T(8,128)(2,1)S(1)} %collective-permute-done.33.refs_1_), channel_id=1, source_target_pairs={{0,4},{4,0},{1,5},{5,1},{2,6},{6,2},{3,7},{7,3},{8,12},{12,8},{9,1... | collective-permute-start | bytes 1179656 | tf_op jit(solution)/shard_map/ppermute | solution.py:42
  111.9 17.8 %collective-permute-start.39 = (bf16[2,2,2,48,512]{4,3,2,1,0:T(8,128)(2,1)}, bf16[2,2,2,48,512]{4,3,2,1,0:T(8,128)(2,1)}, u32[]{:S(2)}, u32[]{:S(2)}) collective-permute-start(bf16[2,2,2,48,512]{4,3,2,1,0:T(8,128)(2,1)} %collective-permute-done.36.refs_3_), channel_id=1, source_target_pairs={{0,4},{4,0},{1,5},{5,1},{2,6},{6,2},{3,7},{7,3},{8,12},{12,8},{9,1... | collective-permute-start | bytes 1179656 | tf_op jit(solution)/shard_map/ppermute | solution.py:42
  125.3 11.9 %collective-permute-start.27 = (bf16[128,512]{1,0:T(8,128)(2,1)S(1)}, bf16[128,512]{1,0:T(8,128)(2,1)S(1)}, u32[]{:S(2)}, u32[]{:S(2)}) collective-permute-start(bf16[128,512]{1,0:T(8,128)(2,1)S(1)} %shard_map.98.refs_0_), channel_id=1, source_target_pairs={{0,2},{1,3},{2,0},{3,1},{4,6},{5,7},{6,4},{7,5},{8,10},{9,11},{10,... | collective-permute-start | bytes 393224 | tf_op jit(solution)/shard_map/ppermute | solution.py:46
  126.6 10.7 %collective-permute-start.26 = (bf16[128,512]{1,0:T(8,128)(2,1)S(1)}, bf16[128,512]{1,0:T(8,128)(2,1)S(1)}, u32[]{:S(2)}, u32[]{:S(2)}) collective-permute-start(bf16[128,512]{1,0:T(8,128)(2,1)S(1)} %shard_map.98.refs_0_), channel_id=1, source_target_pairs={{0,1},{1,0},{2,3},{3,2},{4,5},{5,4},{6,7},{7,6},{8,9},{9,8},{10,11... | collective-permute-start | bytes 393224 | tf_op jit(solution)/shard_map/ppermute | solution.py:46
  128.3 9.9 %collective-permute-start.40 = (bf16[128,512]{1,0:T(8,128)(2,1)S(1)}, bf16[128,512]{1,0:T(8,128)(2,1)S(1)}, u32[]{:S(2)}, u32[]{:S(2)}) collective-permute-start(bf16[128,512]{1,0:T(8,128)(2,1)S(1)} %shard_map.98.refs_0_), channel_id=1, source_target_pairs={{0,3},{1,2},{2,1},{3,0},{4,7},{5,6},{6,5},{7,4},{8,11},{9,10},{10,... | collective-permute-start | bytes 393224 | tf_op jit(solution)/shard_map/ppermute | solution.py:46
  140.7 12.8 %collective-permute-start.42 = (bf16[128,512]{1,0:T(8,128)(2,1)S(1)}, bf16[128,512]{1,0:T(8,128)(2,1)S(1)}, u32[]{:S(2)}, u32[]{:S(2)}) collective-permute-start(bf16[128,512]{1,0:T(8,128)(2,1)S(1)} %get-tuple-element.62), channel_id=1, source_target_pairs={{0,2},{1,3},{2,0},{3,1},{4,6},{5,7},{6,4},{7,5},{8,10},{9,11},{10,... | collective-permute-start | bytes 393224 | tf_op jit(solution)/shard_map/ppermute | solution.py:46
  143.0 10.4 %collective-permute-start.43 = (bf16[128,512]{1,0:T(8,128)(2,1)S(1)}, bf16[128,512]{1,0:T(8,128)(2,1)S(1)}, u32[]{:S(2)}, u32[]{:S(2)}) collective-permute-start(bf16[128,512]{1,0:T(8,128)(2,1)S(1)} %get-tuple-element.63), channel_id=1, source_target_pairs={{0,1},{1,0},{2,3},{3,2},{4,5},{5,4},{6,7},{7,6},{8,9},{9,8},{10,11... | collective-permute-start | bytes 393224 | tf_op jit(solution)/shard_map/ppermute | solution.py:46
  (41 other events, 260.2 us)

commit v4 on v3

--- a/solution.py
+++ b/solution.py
@@ -347,20 +347,28 @@
     total = jnp.stack(totals)
     got = swap(total.astype(BF16), "zh")
     delta = (total + got.astype(F32)[:, ::-1]) / workers
-    new_momentum = outer_beta * momentum + delta[:, 0]
-    new_outer = outer_params - outer_rate * (delta[:, 0] + outer_beta * new_momentum)
+
+    def outer_update(summed):
+        moment_next = outer_beta * momentum + summed
+        return outer_params - outer_rate * (summed + outer_beta * moment_next), moment_next
+
+    here_outer, _ = outer_update(delta[:, 0])
     other_outer = far_state - outer_rate * (1 + outer_beta) * delta[:, 1]
     weights = [
-        jnp.stack([new_outer[m].astype(BF16), other_outer[m].astype(BF16)]) for m in range(matrices)
+        jnp.stack([here_outer[m].astype(BF16), other_outer[m].astype(BF16)]) for m in range(matrices)
     ]
     gathered = []
     for m in range(matrices):
         both = weights[m]
         if m == 1:
             taken = quarters_of(both)
-            taken = [taken[0]] + [mp_swap(taken[k], k) for k in range(1, groups)]
-            both = jnp.stack(taken).reshape(both.shape)
+            got2 = mp_swap(jnp.stack([taken[2], taken[3]]), 2)
+            got1 = mp_swap(jnp.stack([taken[1], got2[1]]), 1)
+            both = jnp.stack([taken[0], got1[0], got2[0], got1[1]]).reshape(both.shape)
         two = jnp.stack([both, plane_swap(both, 1, False)])
+        if m == 0:
+            two, late = lax.optimization_barrier((two, delta[:, 0]))
+            new_outer, new_momentum = outer_update(late)
         rest = plane_swap(two, 3, False)
         fore = jnp.stack([two, plane_swap(two, 3, True)])
         hind = jnp.stack([rest, plane_swap(rest, 1, True)])

time: 166 us -> 167 us (level)
  waiting for transfers between devices: 77.2 us -> 68.3 us
  starting transfers between devices: 55.3 us -> 63.4 us
    ppermute x22, waiting for transfers between devices: 34.4 us -> 26.5 us  [plane_swap(): return lax.ppermute(value, PLANE, pairs)]
    ppermute x22, starting transfers between devices: 29.7 us -> 36.3 us  [plane_swap(): return lax.ppermute(value, PLANE, pairs)]
    ppermute x14 -> x13, starting transfers between devices: 17.8 us -> 18.5 us  [mp_swap(): return lax.ppermute(value, 'mp', [(i, i ^ mask) for i in range(4)])]
    ppermute x14 -> x13, waiting for transfers between devices: 28.2 us -> 28.3 us  [mp_swap(): return lax.ppermute(value, 'mp', [(i, i ^ mask) for i in range(4)])]
    unnamed x38 -> x44, local copies, waits for them, and re-layouts: 9.86 us -> 9.89 us
  transfers between devices with their start and end apart: 46 -> 45, of which waited for: 24 -> 22; matrix products, arithmetic and copies ran while one was open for 2% -> 4% of each run, Pallas kernels for 5% -> 5%
where the time goes in v4:
time: 167 us; the launch traced here: 164 us
  waiting for transfers between devices  68.3 us (41%)
  starting transfers between devices  63.4 us (38%)
  local copies, waits for them, and re-layouts  15 us (9%)
  Pallas kernels  12.6 us (8%)
  other arithmetic  3.94 us (2%)
    ppermute x22, starting transfers between devices, plane_swap(): return lax.ppermute(value, PLANE, pairs)  36.3 us
    ppermute x13, waiting for transfers between devices, mp_swap(): return lax.ppermute(value, 'mp', [(i, i ^ mask) for i in range(4)])  28.3 us
    ppermute x22, waiting for transfers between devices, plane_swap(): return lax.ppermute(value, PLANE, pairs)  26.5 us
    ppermute x13, starting transfers between devices, mp_swap(): return lax.ppermute(value, 'mp', [(i, i ^ mask) for i in range(4)])  18.5 us
    ppermute x10, waiting for transfers between devices, swap(): return lax.ppermute(value, axis, [(0, 1), (1, 0)])  13.5 us
    pallas_call x11, Pallas kernels, local(): pl.pallas_call(body, in_specs=[spec] * len(ins), out_specs=[spec] * len(o...  10.4 us
    unnamed x44, local copies, waits for them, and re-layouts  9.89 us
    ppermute x10, starting transfers between devices, swap(): return lax.ppermute(value, axis, [(0, 1), (1, 0)])  8.58 us
  transfers between devices with their start and end apart: 45, of which 22 were waited for; matrix products, arithmetic and copies ran while one was open for 4% of the time, Pallas kernels for 5%

profile of v4, /device:TPU:2, one launch (start us, length us, event | category | flops | bytes accessed | tf_op | source)
XLA Modules:
  0.0 164.4 jit_solution(14828894262360176308)
XLA Ops:
  6.5 2.3 %collective-permute-start.2 = (bf16[4,2,48,512]{3,2,1,0:T(8,128)(2,1)S(1)}, bf16[4,2,48,512]{3,2,1,0:T(8,128)(2,1)S(1)}, u32[]{:S(2)}, u32[]{:S(2)}) collective-permute-start(bf16[4,2,48,512]{3,2,1,0:T(8,128)(2,1)S(1)} %get-tuple-element.41), channel_id=1, source_target_pairs={{0,8},{4,36},{8,0},{12,44},{16,24},{20,52},{24,16},{28,60},{32,40}... | collective-permute-start | bytes 1179656 | tf_op jit(solution)/shard_map/ppermute | solution.py:38
  12.2 2.4 %collective-permute-done.2 = bf16[4,2,48,512]{3,2,1,0:T(8,128)(2,1)S(1)} collective-permute-done((bf16[4,2,48,512]{3,2,1,0:T(8,128)(2,1)S(1)}, bf16[4,2,48,512]{3,2,1,0:T(8,128)(2,1)S(1)}, u32[]{:S(2)}, u32[]{:S(2)}) %collective-permute-start.2) | collective-permute-done | bytes 393248 | tf_op jit(solution)/shard_map/ppermute | solution.py:38
  17.5 2.8 %collective-permute-start.9 = (bf16[4,2,48,512]{3,2,1,0:T(8,128)(2,1)S(1)}, bf16[4,2,48,512]{3,2,1,0:T(8,128)(2,1)S(1)}, u32[]{:S(2)}, u32[]{:S(2)}) collective-permute-start(bf16[4,2,48,512]{3,2,1,0:T(8,128)(2,1)S(1)} %add_convert_fusion), channel_id=1, source_target_pairs={{0,8},{4,36},{8,0},{12,44},{16,24},{20,52},{24,16},{28,60},{32,40}... | collective-permute-start | bytes 1179656 | tf_op jit(solution)/shard_map/ppermute | solution.py:38
  20.3 2.3 %collective-permute-done.3 = bf16[4,2,48,512]{3,2,1,0:T(8,128)(2,1)S(1)} collective-permute-done((bf16[4,2,48,512]{3,2,1,0:T(8,128)(2,1)S(1)}, bf16[4,2,48,512]{3,2,1,0:T(8,128)(2,1)S(1)}, u32[]{:S(2)}, u32[]{:S(2)}) %collective-permute-start.3) | collective-permute-done | bytes 393248 | tf_op jit(solution)/shard_map/ppermute | solution.py:38
  22.8 2.9 %collective-permute-start.4 = (bf16[2,2,48,512]{3,2,1,0:T(8,128)(2,1)S(1)}, bf16[2,2,48,512]{3,2,1,0:T(8,128)(2,1)S(1)}, u32[]{:S(2)}, u32[]{:S(2)}) collective-permute-start(bf16[2,2,48,512]{3,2,1,0:T(8,128)(2,1)S(1)} %slice.130), channel_id=1, source_target_pairs={{0,96},{4,28},{8,104},{12,20},{16,112},{20,12},{24,120},{28,4},{32... | collective-permute-start | bytes 589832 | tf_op jit(solution)/shard_map/ppermute | solution.py:38
  25.7 3.2 %collective-permute-done.7 = bf16[4,2,48,512]{3,2,1,0:T(8,128)(2,1)S(1)} collective-permute-done((bf16[4,2,48,512]{3,2,1,0:T(8,128)(2,1)S(1)}, bf16[4,2,48,512]{3,2,1,0:T(8,128)(2,1)S(1)}, u32[]{:S(2)}, u32[]{:S(2)}) %collective-permute-start.7) | collective-permute-done | bytes 393248 | tf_op jit(solution)/shard_map/ppermute | solution.py:38
  31.4 3.5 %collective-permute-done.10 = bf16[2,2,48,512]{3,2,1,0:T(8,128)(2,1)S(1)} collective-permute-done((bf16[2,2,48,512]{3,2,1,0:T(8,128)(2,1)S(1)}, bf16[2,2,48,512]{3,2,1,0:T(8,128)(2,1)S(1)}, u32[]{:S(2)}, u32[]{:S(2)}) %collective-permute-start.10) | collective-permute-done | bytes 196640 | tf_op jit(solution)/shard_map/ppermute | solution.py:38
  34.9 2.7 %collective-permute-start.11 = (bf16[2,48,512]{2,1,0:T(8,128)(2,1)S(1)}, bf16[2,48,512]{2,1,0:T(8,128)(2,1)S(1)}, u32[]{:S(2)}, u32[]{:S(2)}) collective-permute-start(bf16[2,48,512]{2,1,0:T(8,128)(2,1)S(1)} %fusion.9), channel_id=1, source_target_pairs={{0,96},{4,28},{8,104},{12,20},{16,112},{20,12},{24,120},{28,4},{32... | collective-permute-start | bytes 294920 | tf_op jit(solution)/shard_map/ppermute | solution.py:38
  37.7 3.1 %collective-permute-done.11 = bf16[2,48,512]{2,1,0:T(8,128)(2,1)S(1)} collective-permute-done((bf16[2,48,512]{2,1,0:T(8,128)(2,1)S(1)}, bf16[2,48,512]{2,1,0:T(8,128)(2,1)S(1)}, u32[]{:S(2)}, u32[]{:S(2)}) %collective-permute-start.11) | collective-permute-done | bytes 98336 | tf_op jit(solution)/shard_map/ppermute | solution.py:38
  40.9 6.9 %collective-permute-start.12 = (bf16[2,2,48,512]{3,2,0,1:T(8,128)(2,1)S(1)}, bf16[2,2,48,512]{3,2,0,1:T(8,128)(2,1)S(1)}, u32[]{:S(2)}, u32[]{:S(2)}) collective-permute-start(bf16[2,2,48,512]{3,2,0,1:T(8,128)(2,1)S(1)} %fusion), channel_id=1, source_target_pairs={{0,128},{128,0},{1,129},{129,1},{2,130},{130,2},{3,131},{131,3},{4... | collective-permute-start | bytes 589832 | tf_op jit(solution)/shard_map/ppermute | solution.py:42
  47.9 7.3 %collective-permute-done.12 = bf16[2,2,48,512]{3,2,0,1:T(8,128)(2,1)S(1)} collective-permute-done((bf16[2,2,48,512]{3,2,0,1:T(8,128)(2,1)S(1)}, bf16[2,2,48,512]{3,2,0,1:T(8,128)(2,1)S(1)}, u32[]{:S(2)}, u32[]{:S(2)}) %collective-permute-start.12) | collective-permute-done | bytes 196640 | tf_op jit(solution)/shard_map/ppermute | solution.py:42
  55.4 4.8 %collective-permute-done.13 = f32[2,48,512]{2,1,0:T(8,128)S(1)} collective-permute-done((f32[2,48,512]{2,1,0:T(8,128)S(1)}, f32[2,48,512]{2,1,0:T(8,128)S(1)}, u32[]{:S(2)}, u32[]{:S(2)}) %collective-permute-start.13) | collective-permute-done | bytes 196640 | tf_op jit(solution)/shard_map/ppermute | solution.py:42
  60.4 2.5 %collective-permute-start.28 = (bf16[2,24,512]{2,1,0:T(8,128)(2,1)S(1)}, bf16[2,24,512]{2,1,0:T(8,128)(2,1)S(1)}, u32[]{:S(2)}, u32[]{:S(2)}) collective-permute-start(bf16[2,24,512]{2,1,0:T(8,128)(2,1)S(1)} %pad_maximum_fusion.12), channel_id=1, source_target_pairs={{0,2},{1,3},{2,0},{3,1},{4,6},{5,7},{6,4},{7,5},{8,10},{9,11},{10,... | collective-permute-start | bytes 147464 | tf_op jit(solution)/shard_map/ppermute | solution.py:46
  72.3 3.3 %collective-permute-start.20 = (bf16[2,2,48,512]{3,2,1,0:T(8,128)(2,1)S(1)}, bf16[2,2,48,512]{3,2,1,0:T(8,128)(2,1)S(1)}, u32[]{:S(2)}, u32[]{:S(2)}) collective-permute-start(bf16[2,2,48,512]{3,2,1,0:T(8,128)(2,1)S(1)} %pad_maximum_fusion.7), channel_id=1, source_target_pairs={{0,96},{4,28},{8,104},{12,20},{16,112},{20,12},{24,120},{28,4},{32... | collective-permute-start | bytes 589832 | tf_op jit(solution)/shard_map/ppermute | solution.py:38
  82.1 2.2 %collective-permute-start.21 = (bf16[2,2,48,512]{3,2,1,0:T(8,128)(2,1)S(1)}, bf16[2,2,48,512]{3,2,1,0:T(8,128)(2,1)S(1)}, u32[]{:S(2)}, u32[]{:S(2)}) collective-permute-start(bf16[2,2,48,512]{3,2,1,0:T(8,128)(2,1)S(1)} %collective-permute-done.20), channel_id=1, source_target_pairs={{0,8},{4,36},{8,0},{12,44},{16,24},{20,52},{24,16},{28,60},{32,40}... | collective-permute-start | bytes 589832 | tf_op jit(solution)/shard_map/ppermute | solution.py:38
  84.4 2.6 %collective-permute-start.19 = (bf16[2,2,2,48,512]{4,3,2,1,0:T(8,128)(2,1)S(1)}, bf16[2,2,2,48,512]{4,3,2,1,0:T(8,128)(2,1)S(1)}, u32[]{:S(2)}, u32[]{:S(2)}) collective-permute-start(bf16[2,2,2,48,512]{4,3,2,1,0:T(8,128)(2,1)S(1)} %get-tuple-element.78.refs_0_), channel_id=1, source_target_pairs={{0,8},{4,36},{8,0},{12,44},{16,24},{20,52},{24,16},{28,60},{32,40}... | collective-permute-start | bytes 1179656 | tf_op jit(solution)/shard_map/ppermute | solution.py:38
  90.1 4.8 %collective-permute-done.34 = bf16[2,2,48,512]{3,2,1,0:T(8,128)(2,1)S(1)} collective-permute-done((bf16[2,2,48,512]{3,2,1,0:T(8,128)(2,1)S(1)}, bf16[2,2,48,512]{3,2,1,0:T(8,128)(2,1)S(1)}, u32[]{:S(2)}, u32[]{:S(2)}) %collective-permute-start.34) | collective-permute-done | bytes 196640 | tf_op jit(solution)/shard_map/ppermute | solution.py:38
  99.3 3.1 %collective-permute-done.17.refs_3_ = bf16[128,768]{1,0:T(8,128)(2,1)S(1)} collective-permute-done((bf16[128,768]{1,0:T(8,128)(2,1)S(1)}, bf16[128,768]{1,0:T(8,128)(2,1)S(1)}, u32[]{:S(2)}, u32[]{:S(2)}) %collective-permute-start.17) | collective-permute-done | bytes 196640 | tf_op jit(solution)/shard_map/ppermute | solution.py:46
  106.3 4.1 %collective-permute-done.35.refs_3_ = bf16[2,2,2,48,512]{4,3,2,1,0:T(8,128)(2,1)} collective-permute-done((bf16[2,2,2,48,512]{4,3,2,1,0:T(8,128)(2,1)S(1)}, bf16[2,2,2,48,512]{4,3,2,1,0:T(8,128)(2,1)}, u32[]{:S(2)}, u32[]{:S(2)}) %collective-permute-start.35) | collective-permute-done | bytes 393248 | tf_op jit(solution)/shard_map/ppermute | solution.py:38
  132.0 7.4 %collective-permute-done.27.refs_2_ = bf16[128,512]{1,0:T(8,128)(2,1)S(1)} collective-permute-done((bf16[128,512]{1,0:T(8,128)(2,1)S(1)}, bf16[128,512]{1,0:T(8,128)(2,1)S(1)}, u32[]{:S(2)}, u32[]{:S(2)}) %collective-permute-start.27) | collective-permute-done | bytes 131104 | tf_op jit(solution)/shard_map/ppermute | solution.py:46
  145.7 3.8 %collective-permute-done.40.refs_1_ = bf16[128,512]{1,0:T(8,128)(2,1)S(1)} collective-permute-done((bf16[128,512]{1,0:T(8,128)(2,1)S(1)}, bf16[128,512]{1,0:T(8,128)(2,1)S(1)}, u32[]{:S(2)}, u32[]{:S(2)}) %collective-permute-start.40) | collective-permute-done | bytes 131104 | tf_op jit(solution)/shard_map/ppermute | solution.py:46
  149.5 3.9 %collective-permute-done.41.refs_2_ = bf16[128,512]{1,0:T(8,128)(2,1)S(1)} collective-permute-done((bf16[128,512]{1,0:T(8,128)(2,1)S(1)}, bf16[128,512]{1,0:T(8,128)(2,1)S(1)}, u32[]{:S(2)}, u32[]{:S(2)}) %collective-permute-start.41) | collective-permute-done | bytes 131104 | tf_op jit(solution)/shard_map/ppermute | solution.py:46
  154.0 4.5 %collective-permute-done.43 = f32[8,128]{1,0:T(8,128)S(1)} collective-permute-done((f32[8,128]{1,0:T(8,128)S(1)}, f32[8,128]{1,0:T(8,128)S(1)}, u32[]{:S(2)}, u32[]{:S(2)}) %collective-permute-start.43) | collective-permute-done | bytes 4128 | tf_op jit(solution)/shard_map/ppermute | solution.py:46
  162.1 2.2 %shard_map.105 = bf16[3072,512]{1,0:T(8,128)(2,1)} custom-call(f32[3072,512]{1,0:T(8,128)S(1)} %shard_map.104.grad_ref, bf16[3072,512]{1,0:T(8,128)(2,1)S(1)} %bitcast.72, f32[8,128]{1,0:T(8,128)S(1)} %add.73.squares_ref), custom_call_target="tpu_custom_call" | custom-call | tf_op jit(solution)/shard_map/pallas_call | solution.py:295
  (162 shorter events, 74.5 us)
Async XLA Ops:
  6.5 8.1 %collective-permute-start.2 = (bf16[4,2,48,512]{3,2,1,0:T(8,128)(2,1)S(1)}, bf16[4,2,48,512]{3,2,1,0:T(8,128)(2,1)S(1)}, u32[]{:S(2)}, u32[]{:S(2)}) collective-permute-start(bf16[4,2,48,512]{3,2,1,0:T(8,128)(2,1)S(1)} %get-tuple-element.41), channel_id=1, source_target_pairs={{0,8},{4,36},{8,0},{12,44},{16,24},{20,52},{24,16},{28,60},{32,40}... | collective-permute-start | bytes 1179656 | tf_op jit(solution)/shard_map/ppermute | solution.py:38
  10.4 9.9 %collective-permute-start.1 = (bf16[4,2,48,512]{3,2,1,0:T(8,128)(2,1)S(1)}, bf16[4,2,48,512]{3,2,1,0:T(8,128)(2,1)S(1)}, u32[]{:S(2)}, u32[]{:S(2)}) collective-permute-start(bf16[4,2,48,512]{3,2,1,0:T(8,128)(2,1)S(1)} %get-tuple-element.39), channel_id=1, source_target_pairs={{0,8},{4,36},{8,0},{12,44},{16,24},{20,52},{24,16},{28,60},{32,40}... | collective-permute-start | bytes 1179656 | tf_op jit(solution)/shard_map/ppermute | solution.py:38
  16.1 12.8 %collective-permute-start.7 = (bf16[4,2,48,512]{3,2,1,0:T(8,128)(2,1)S(1)}, bf16[4,2,48,512]{3,2,1,0:T(8,128)(2,1)S(1)}, u32[]{:S(2)}, u32[]{:S(2)}) collective-permute-start(bf16[4,2,48,512]{3,2,1,0:T(8,128)(2,1)S(1)} %get-tuple-element.48), channel_id=1, source_target_pairs={{0,24},{4,100},{8,16},{12,108},{16,8},{20,116},{24,0},{28,124},{32... | collective-permute-start | bytes 1179656 | tf_op jit(solution)/shard_map/ppermute | solution.py:38
  17.5 11.4 %collective-permute-start.9 = (bf16[4,2,48,512]{3,2,1,0:T(8,128)(2,1)S(1)}, bf16[4,2,48,512]{3,2,1,0:T(8,128)(2,1)S(1)}, u32[]{:S(2)}, u32[]{:S(2)}) collective-permute-start(bf16[4,2,48,512]{3,2,1,0:T(8,128)(2,1)S(1)} %add_convert_fusion), channel_id=1, source_target_pairs={{0,8},{4,36},{8,0},{12,44},{16,24},{20,52},{24,16},{28,60},{32,40}... | collective-permute-start | bytes 1179656 | tf_op jit(solution)/shard_map/ppermute | solution.py:38
  40.9 14.4 %collective-permute-start.12 = (bf16[2,2,48,512]{3,2,0,1:T(8,128)(2,1)S(1)}, bf16[2,2,48,512]{3,2,0,1:T(8,128)(2,1)S(1)}, u32[]{:S(2)}, u32[]{:S(2)}) collective-permute-start(bf16[2,2,48,512]{3,2,0,1:T(8,128)(2,1)S(1)} %fusion), channel_id=1, source_target_pairs={{0,128},{128,0},{1,129},{129,1},{2,130},{130,2},{3,131},{131,3},{4... | collective-permute-start | bytes 589832 | tf_op jit(solution)/shard_map/ppermute | solution.py:42
  47.8 12.4 %collective-permute-start.13 = (f32[2,48,512]{2,1,0:T(8,128)S(1)}, f32[2,48,512]{2,1,0:T(8,128)S(1)}, u32[]{:S(2)}, u32[]{:S(2)}) collective-permute-start(f32[2,48,512]{2,1,0:T(8,128)S(1)} %multiply_subtract_fusion.1), channel_id=1, source_target_pairs={{0,128},{128,0},{1,129},{129,1},{2,130},{130,2},{3,131},{131,3},{4... | collective-permute-start | bytes 589832 | tf_op jit(solution)/shard_map/ppermute | solution.py:42
  72.3 9.0 %collective-permute-start.20 = (bf16[2,2,48,512]{3,2,1,0:T(8,128)(2,1)S(1)}, bf16[2,2,48,512]{3,2,1,0:T(8,128)(2,1)S(1)}, u32[]{:S(2)}, u32[]{:S(2)}) collective-permute-start(bf16[2,2,48,512]{3,2,1,0:T(8,128)(2,1)S(1)} %pad_maximum_fusion.7), channel_id=1, source_target_pairs={{0,96},{4,28},{8,104},{12,20},{16,112},{20,12},{24,120},{28,4},{32... | collective-permute-start | bytes 589832 | tf_op jit(solution)/shard_map/ppermute | solution.py:38
  77.7 9.3 %collective-permute-start.31 = (bf16[2,2,48,512]{3,2,1,0:T(8,128)(2,1)S(1)}, bf16[2,2,48,512]{3,2,1,0:T(8,128)(2,1)S(1)}, u32[]{:S(2)}, u32[]{:S(2)}) collective-permute-start(bf16[2,2,48,512]{3,2,1,0:T(8,128)(2,1)S(1)} %get-tuple-element.84), channel_id=1, source_target_pairs={{0,24},{4,100},{8,16},{12,108},{16,8},{20,116},{24,0},{28,124},{32... | collective-permute-start | bytes 589832 | tf_op jit(solution)/shard_map/ppermute | solution.py:38
  79.3 18.4 %collective-permute-start.15 = (bf16[128,768]{1,0:T(8,128)(2,1)S(1)}, bf16[128,768]{1,0:T(8,128)(2,1)S(1)}, u32[]{:S(2)}, u32[]{:S(2)}) collective-permute-start(bf16[128,768]{1,0:T(8,128)(2,1)S(1)} %copy-done.6), channel_id=1, source_target_pairs={{0,1},{1,0},{2,3},{3,2},{4,5},{5,4},{6,7},{7,6},{8,9},{9,8},{10,11... | collective-permute-start | bytes 589832 | tf_op jit(solution)/shard_map/ppermute | solution.py:46
  81.3 16.5 %collective-permute-start.16 = (bf16[128,768]{1,0:T(8,128)(2,1)S(1)}, bf16[128,768]{1,0:T(8,128)(2,1)S(1)}, u32[]{:S(2)}, u32[]{:S(2)}) collective-permute-start(bf16[128,768]{1,0:T(8,128)(2,1)S(1)} %copy-done.6), channel_id=1, source_target_pairs={{0,2},{1,3},{2,0},{3,1},{4,6},{5,7},{6,4},{7,5},{8,10},{9,11},{10,... | collective-permute-start | bytes 589832 | tf_op jit(solution)/shard_map/ppermute | solution.py:46
  84.4 20.4 %collective-permute-start.19 = (bf16[2,2,2,48,512]{4,3,2,1,0:T(8,128)(2,1)S(1)}, bf16[2,2,2,48,512]{4,3,2,1,0:T(8,128)(2,1)S(1)}, u32[]{:S(2)}, u32[]{:S(2)}) collective-permute-start(bf16[2,2,2,48,512]{4,3,2,1,0:T(8,128)(2,1)S(1)} %get-tuple-element.78.refs_0_), channel_id=1, source_target_pairs={{0,8},{4,36},{8,0},{12,44},{16,24},{20,52},{24,16},{28,60},{32,40}... | collective-permute-start | bytes 1179656 | tf_op jit(solution)/shard_map/ppermute | solution.py:38
  88.0 16.9 %collective-permute-start.32 = (bf16[2,2,2,48,512]{4,3,2,1,0:T(8,128)(2,1)S(1)}, bf16[2,2,2,48,512]{4,3,2,1,0:T(8,128)(2,1)S(1)}, u32[]{:S(2)}, u32[]{:S(2)}) collective-permute-start(bf16[2,2,2,48,512]{4,3,2,1,0:T(8,128)(2,1)S(1)} %get-tuple-element.74.refs_0_), channel_id=1, source_target_pairs={{0,8},{4,36},{8,0},{12,44},{16,24},{20,52},{24,16},{28,60},{32,40}... | collective-permute-start | bytes 1179656 | tf_op jit(solution)/shard_map/ppermute | solution.py:38
  97.7 22.0 %collective-permute-start.23 = (bf16[2,2,2,2,48,512]{5,4,3,2,1,0:T(8,128)(2,1)}, bf16[2,2,2,2,48,512]{5,4,3,2,1,0:T(8,128)(2,1)S(1)}, u32[]{:S(2)}, u32[]{:S(2)}) collective-permute-start(bf16[2,2,2,2,48,512]{5,4,3,2,1,0:T(8,128)(2,1)} %pad_maximum_fusion), channel_id=1, source_target_pairs={{0,4},{4,0},{1,5},{5,1},{2,6},{6,2},{3,7},{7,3},{8,12},{12,8},{9,1... | collective-permute-start | bytes 2359304 | tf_op jit(solution)/shard_map/ppermute | solution.py:42
  97.8 8.3 %collective-permute-start.22 = (bf16[2,2,2,48,512]{4,3,2,1,0:T(8,128)(2,1)S(1)}, bf16[2,2,2,48,512]{4,3,2,1,0:T(8,128)(2,1)}, u32[]{:S(2)}, u32[]{:S(2)}) collective-permute-start(bf16[2,2,2,48,512]{4,3,2,1,0:T(8,128)(2,1)S(1)} %get-tuple-element.80.refs_2_), channel_id=1, source_target_pairs={{0,24},{4,100},{8,16},{12,108},{16,8},{20,116},{24,0},{28,124},{32... | collective-permute-start | bytes 1179656 | tf_op jit(solution)/shard_map/ppermute | solution.py:38
  102.5 7.9 %collective-permute-start.35 = (bf16[2,2,2,48,512]{4,3,2,1,0:T(8,128)(2,1)S(1)}, bf16[2,2,2,48,512]{4,3,2,1,0:T(8,128)(2,1)}, u32[]{:S(2)}, u32[]{:S(2)}) collective-permute-start(bf16[2,2,2,48,512]{4,3,2,1,0:T(8,128)(2,1)S(1)} %get-tuple-element.76.refs_2_), channel_id=1, source_target_pairs={{0,24},{4,100},{8,16},{12,108},{16,8},{20,116},{24,0},{28,124},{32... | collective-permute-start | bytes 1179656 | tf_op jit(solution)/shard_map/ppermute | solution.py:38
  104.8 24.4 %collective-permute-start.36 = (bf16[2,2,2,2,48,512]{5,4,3,2,1,0:T(8,128)(2,1)}, bf16[2,2,2,2,48,512]{5,4,3,2,1,0:T(8,128)(2,1)S(1)}, u32[]{:S(2)}, u32[]{:S(2)}) collective-permute-start(bf16[2,2,2,2,48,512]{5,4,3,2,1,0:T(8,128)(2,1)} %pad_maximum_fusion.1), channel_id=1, source_target_pairs={{0,4},{4,0},{1,5},{5,1},{2,6},{6,2},{3,7},{7,3},{8,12},{12,8},{9,1... | collective-permute-start | bytes 2359304 | tf_op jit(solution)/shard_map/ppermute | solution.py:42
  106.2 13.6 %collective-permute-start.25 = (bf16[2,2,2,48,512]{4,3,2,1,0:T(8,128)(2,1)}, bf16[2,2,2,48,512]{4,3,2,1,0:T(8,128)(2,1)}, u32[]{:S(2)}, u32[]{:S(2)}) collective-permute-start(bf16[2,2,2,48,512]{4,3,2,1,0:T(8,128)(2,1)} %collective-permute-done.22.refs_3_), channel_id=1, source_target_pairs={{0,4},{4,0},{1,5},{5,1},{2,6},{6,2},{3,7},{7,3},{8,12},{12,8},{9,1... | collective-permute-start | bytes 1179656 | tf_op jit(solution)/shard_map/ppermute | solution.py:42
  110.4 16.8 %collective-permute-start.37 = (bf16[2,2,2,48,512]{4,3,2,1,0:T(8,128)(2,1)S(1)}, bf16[2,2,2,48,512]{4,3,2,1,0:T(8,128)(2,1)}, u32[]{:S(2)}, u32[]{:S(2)}) collective-permute-start(bf16[2,2,2,48,512]{4,3,2,1,0:T(8,128)(2,1)S(1)} %collective-permute-done.32.refs_1_), channel_id=1, source_target_pairs={{0,4},{4,0},{1,5},{5,1},{2,6},{6,2},{3,7},{7,3},{8,12},{12,8},{9,1... | collective-permute-start | bytes 1179656 | tf_op jit(solution)/shard_map/ppermute | solution.py:42
  111.2 18.0 %collective-permute-start.38 = (bf16[2,2,2,48,512]{4,3,2,1,0:T(8,128)(2,1)}, bf16[2,2,2,48,512]{4,3,2,1,0:T(8,128)(2,1)}, u32[]{:S(2)}, u32[]{:S(2)}) collective-permute-start(bf16[2,2,2,48,512]{4,3,2,1,0:T(8,128)(2,1)} %collective-permute-done.35.refs_3_), channel_id=1, source_target_pairs={{0,4},{4,0},{1,5},{5,1},{2,6},{6,2},{3,7},{7,3},{8,12},{12,8},{9,1... | collective-permute-start | bytes 1179656 | tf_op jit(solution)/shard_map/ppermute | solution.py:42
  126.4 12.9 %collective-permute-start.27 = (bf16[128,512]{1,0:T(8,128)(2,1)S(1)}, bf16[128,512]{1,0:T(8,128)(2,1)S(1)}, u32[]{:S(2)}, u32[]{:S(2)}) collective-permute-start(bf16[128,512]{1,0:T(8,128)(2,1)S(1)} %shard_map.98.refs_0_), channel_id=1, source_target_pairs={{0,2},{1,3},{2,0},{3,1},{4,6},{5,7},{6,4},{7,5},{8,10},{9,11},{10,... | collective-permute-start | bytes 393224 | tf_op jit(solution)/shard_map/ppermute | solution.py:46
  127.1 13.1 %collective-permute-start.39 = (bf16[128,512]{1,0:T(8,128)(2,1)S(1)}, bf16[128,512]{1,0:T(8,128)(2,1)S(1)}, u32[]{:S(2)}, u32[]{:S(2)}) collective-permute-start(bf16[128,512]{1,0:T(8,128)(2,1)S(1)} %shard_map.98.refs_0_), channel_id=1, source_target_pairs={{0,3},{1,2},{2,1},{3,0},{4,7},{5,6},{6,5},{7,4},{8,11},{9,10},{10,... | collective-permute-start | bytes 393224 | tf_op jit(solution)/shard_map/ppermute | solution.py:46
  141.2 8.3 %collective-permute-start.40 = (bf16[128,512]{1,0:T(8,128)(2,1)S(1)}, bf16[128,512]{1,0:T(8,128)(2,1)S(1)}, u32[]{:S(2)}, u32[]{:S(2)}) collective-permute-start(bf16[128,512]{1,0:T(8,128)(2,1)S(1)} %get-tuple-element.65), channel_id=1, source_target_pairs={{0,3},{1,2},{2,1},{3,0},{4,7},{5,6},{6,5},{7,4},{8,11},{9,10},{10,... | collective-permute-start | bytes 393224 | tf_op jit(solution)/shard_map/ppermute | solution.py:46
  143.2 10.2 %collective-permute-start.41 = (bf16[128,512]{1,0:T(8,128)(2,1)S(1)}, bf16[128,512]{1,0:T(8,128)(2,1)S(1)}, u32[]{:S(2)}, u32[]{:S(2)}) collective-permute-start(bf16[128,512]{1,0:T(8,128)(2,1)S(1)} %get-tuple-element.66), channel_id=1, source_target_pairs={{0,2},{1,3},{2,0},{3,1},{4,6},{5,7},{6,4},{7,5},{8,10},{9,11},{10,... | collective-permute-start | bytes 393224 | tf_op jit(solution)/shard_map/ppermute | solution.py:46
  144.0 9.3 %collective-permute-start.42 = (bf16[128,512]{1,0:T(8,128)(2,1)S(1)}, bf16[128,512]{1,0:T(8,128)(2,1)S(1)}, u32[]{:S(2)}, u32[]{:S(2)}) collective-permute-start(bf16[128,512]{1,0:T(8,128)(2,1)S(1)} %get-tuple-element.67), channel_id=1, source_target_pairs={{0,1},{1,0},{2,3},{3,2},{4,5},{5,4},{6,7},{7,6},{8,9},{9,8},{10,11... | collective-permute-start | bytes 393224 | tf_op jit(solution)/shard_map/ppermute | solution.py:46
  (43 other events, 327.0 us)

commit v5 on v4

--- a/solution.py
+++ b/solution.py
@@ -363,8 +363,9 @@
         if m == 1:
             taken = quarters_of(both)
             got2 = mp_swap(jnp.stack([taken[2], taken[3]]), 2)
-            got1 = mp_swap(jnp.stack([taken[1], got2[1]]), 1)
-            both = jnp.stack([taken[0], got1[0], got2[0], got1[1]]).reshape(both.shape)
+            far_one, far_two = got2[0], got2[1]
+            got1 = mp_swap(jnp.stack([taken[1], far_two]), 1)
+            both = jnp.stack([taken[0], got1[0], far_one, got1[1]]).reshape(both.shape)
         two = jnp.stack([both, plane_swap(both, 1, False)])
         if m == 0:
             two, late = lax.optimization_barrier((two, delta[:, 0]))
@@ -392,8 +393,7 @@
     dctx_parts = [mine] + [mp_swap(sends[k - 1], k) for k in (3, 2, 1)]
     pulled, squares = values_grad(dctx_parts, probs, gram, width)
     grad = weight_grad(turned, pulled)
-    squares = squares + mp_swap(squares, 2)
-    squares = squares + mp_swap(squares, 1)
+    squares = squares + sum(mp_swap(squares, k) for k in (3, 2, 1))
     new_local = inner_update(grad, value_proj, squares, width * cols * groups)
     return (new_outer, new_momentum, new_local[None])
 

time: 167 us -> 166 us (level)
  waiting for transfers between devices: 68.3 us -> 62.5 us
  starting transfers between devices: 63.4 us -> 67.7 us
    ppermute x13 -> x14, waiting for transfers between devices: 28.3 us -> 22.5 us  [mp_swap(): return lax.ppermute(value, 'mp', [(i, i ^ mask) for i in range(4)])]
    ppermute x13 -> x14, starting transfers between devices: 18.5 us -> 22.8 us  [mp_swap(): return lax.ppermute(value, 'mp', [(i, i ^ mask) for i in range(4)])]
  transfers between devices with their start and end apart: 45 -> 46, of which waited for: 22 -> 21; matrix products, arithmetic and copies ran while one was open for 4% -> 4% of each run, Pallas kernels for 5% -> 5%
where the time goes in v5:
time: 166 us; the launch traced here: 163 us
  starting transfers between devices  67.7 us (41%)
  waiting for transfers between devices  62.5 us (38%)
  local copies, waits for them, and re-layouts  15 us (9%)
  Pallas kernels  12.6 us (8%)
  other arithmetic  3.92 us (2%)
    ppermute x22, starting transfers between devices, plane_swap(): return lax.ppermute(value, PLANE, pairs)  36.3 us
    ppermute x22, waiting for transfers between devices, plane_swap(): return lax.ppermute(value, PLANE, pairs)  26.5 us
    ppermute x14, starting transfers between devices, mp_swap(): return lax.ppermute(value, 'mp', [(i, i ^ mask) for i in range(4)])  22.8 us
    ppermute x14, waiting for transfers between devices, mp_swap(): return lax.ppermute(value, 'mp', [(i, i ^ mask) for i in range(4)])  22.5 us
    ppermute x10, waiting for transfers between devices, swap(): return lax.ppermute(value, axis, [(0, 1), (1, 0)])  13.5 us
    pallas_call x11, Pallas kernels, local(): pl.pallas_call(body, in_specs=[spec] * len(ins), out_specs=[spec] * len(o...  10.4 us
    unnamed x44, local copies, waits for them, and re-layouts  9.9 us
    ppermute x10, starting transfers between devices, swap(): return lax.ppermute(value, axis, [(0, 1), (1, 0)])  8.58 us
  transfers between devices with their start and end apart: 46, of which 21 were waited for; matrix products, arithmetic and copies ran while one was open for 4% of the time, Pallas kernels for 5%

profile of v5, /device:TPU:2, one launch (start us, length us, event | category | flops | bytes accessed | tf_op | source)
XLA Modules:
  0.0 163.0 jit_solution(6870208015033255509)
XLA Ops:
  6.5 2.3 %collective-permute-start.2 = (bf16[4,2,48,512]{3,2,1,0:T(8,128)(2,1)S(1)}, bf16[4,2,48,512]{3,2,1,0:T(8,128)(2,1)S(1)}, u32[]{:S(2)}, u32[]{:S(2)}) collective-permute-start(bf16[4,2,48,512]{3,2,1,0:T(8,128)(2,1)S(1)} %get-tuple-element.41), channel_id=1, source_target_pairs={{0,8},{4,36},{8,0},{12,44},{16,24},{20,52},{24,16},{28,60},{32,40}... | collective-permute-start | bytes 1179656 | tf_op jit(solution)/shard_map/ppermute | solution.py:38
  12.2 2.4 %collective-permute-done.2 = bf16[4,2,48,512]{3,2,1,0:T(8,128)(2,1)S(1)} collective-permute-done((bf16[4,2,48,512]{3,2,1,0:T(8,128)(2,1)S(1)}, bf16[4,2,48,512]{3,2,1,0:T(8,128)(2,1)S(1)}, u32[]{:S(2)}, u32[]{:S(2)}) %collective-permute-start.2) | collective-permute-done | bytes 393248 | tf_op jit(solution)/shard_map/ppermute | solution.py:38
  17.5 2.8 %collective-permute-start.9 = (bf16[4,2,48,512]{3,2,1,0:T(8,128)(2,1)S(1)}, bf16[4,2,48,512]{3,2,1,0:T(8,128)(2,1)S(1)}, u32[]{:S(2)}, u32[]{:S(2)}) collective-permute-start(bf16[4,2,48,512]{3,2,1,0:T(8,128)(2,1)S(1)} %add_convert_fusion), channel_id=1, source_target_pairs={{0,8},{4,36},{8,0},{12,44},{16,24},{20,52},{24,16},{28,60},{32,40}... | collective-permute-start | bytes 1179656 | tf_op jit(solution)/shard_map/ppermute | solution.py:38
  20.3 2.3 %collective-permute-done.3 = bf16[4,2,48,512]{3,2,1,0:T(8,128)(2,1)S(1)} collective-permute-done((bf16[4,2,48,512]{3,2,1,0:T(8,128)(2,1)S(1)}, bf16[4,2,48,512]{3,2,1,0:T(8,128)(2,1)S(1)}, u32[]{:S(2)}, u32[]{:S(2)}) %collective-permute-start.3) | collective-permute-done | bytes 393248 | tf_op jit(solution)/shard_map/ppermute | solution.py:38
  22.8 2.9 %collective-permute-start.4 = (bf16[2,2,48,512]{3,2,1,0:T(8,128)(2,1)S(1)}, bf16[2,2,48,512]{3,2,1,0:T(8,128)(2,1)S(1)}, u32[]{:S(2)}, u32[]{:S(2)}) collective-permute-start(bf16[2,2,48,512]{3,2,1,0:T(8,128)(2,1)S(1)} %slice.130), channel_id=1, source_target_pairs={{0,96},{4,28},{8,104},{12,20},{16,112},{20,12},{24,120},{28,4},{32... | collective-permute-start | bytes 589832 | tf_op jit(solution)/shard_map/ppermute | solution.py:38
  25.7 3.2 %collective-permute-done.7 = bf16[4,2,48,512]{3,2,1,0:T(8,128)(2,1)S(1)} collective-permute-done((bf16[4,2,48,512]{3,2,1,0:T(8,128)(2,1)S(1)}, bf16[4,2,48,512]{3,2,1,0:T(8,128)(2,1)S(1)}, u32[]{:S(2)}, u32[]{:S(2)}) %collective-permute-start.7) | collective-permute-done | bytes 393248 | tf_op jit(solution)/shard_map/ppermute | solution.py:38
  31.4 3.5 %collective-permute-done.10 = bf16[2,2,48,512]{3,2,1,0:T(8,128)(2,1)S(1)} collective-permute-done((bf16[2,2,48,512]{3,2,1,0:T(8,128)(2,1)S(1)}, bf16[2,2,48,512]{3,2,1,0:T(8,128)(2,1)S(1)}, u32[]{:S(2)}, u32[]{:S(2)}) %collective-permute-start.10) | collective-permute-done | bytes 196640 | tf_op jit(solution)/shard_map/ppermute | solution.py:38
  34.9 2.7 %collective-permute-start.11 = (bf16[2,48,512]{2,1,0:T(8,128)(2,1)S(1)}, bf16[2,48,512]{2,1,0:T(8,128)(2,1)S(1)}, u32[]{:S(2)}, u32[]{:S(2)}) collective-permute-start(bf16[2,48,512]{2,1,0:T(8,128)(2,1)S(1)} %fusion.9), channel_id=1, source_target_pairs={{0,96},{4,28},{8,104},{12,20},{16,112},{20,12},{24,120},{28,4},{32... | collective-permute-start | bytes 294920 | tf_op jit(solution)/shard_map/ppermute | solution.py:38
  37.7 3.1 %collective-permute-done.11 = bf16[2,48,512]{2,1,0:T(8,128)(2,1)S(1)} collective-permute-done((bf16[2,48,512]{2,1,0:T(8,128)(2,1)S(1)}, bf16[2,48,512]{2,1,0:T(8,128)(2,1)S(1)}, u32[]{:S(2)}, u32[]{:S(2)}) %collective-permute-start.11) | collective-permute-done | bytes 98336 | tf_op jit(solution)/shard_map/ppermute | solution.py:38
  40.9 6.9 %collective-permute-start.12 = (bf16[2,2,48,512]{3,2,0,1:T(8,128)(2,1)S(1)}, bf16[2,2,48,512]{3,2,0,1:T(8,128)(2,1)S(1)}, u32[]{:S(2)}, u32[]{:S(2)}) collective-permute-start(bf16[2,2,48,512]{3,2,0,1:T(8,128)(2,1)S(1)} %fusion), channel_id=1, source_target_pairs={{0,128},{128,0},{1,129},{129,1},{2,130},{130,2},{3,131},{131,3},{4... | collective-permute-start | bytes 589832 | tf_op jit(solution)/shard_map/ppermute | solution.py:42
  47.9 7.3 %collective-permute-done.12 = bf16[2,2,48,512]{3,2,0,1:T(8,128)(2,1)S(1)} collective-permute-done((bf16[2,2,48,512]{3,2,0,1:T(8,128)(2,1)S(1)}, bf16[2,2,48,512]{3,2,0,1:T(8,128)(2,1)S(1)}, u32[]{:S(2)}, u32[]{:S(2)}) %collective-permute-start.12) | collective-permute-done | bytes 196640 | tf_op jit(solution)/shard_map/ppermute | solution.py:42
  55.4 4.8 %collective-permute-done.13 = f32[2,48,512]{2,1,0:T(8,128)S(1)} collective-permute-done((f32[2,48,512]{2,1,0:T(8,128)S(1)}, f32[2,48,512]{2,1,0:T(8,128)S(1)}, u32[]{:S(2)}, u32[]{:S(2)}) %collective-permute-start.13) | collective-permute-done | bytes 196640 | tf_op jit(solution)/shard_map/ppermute | solution.py:42
  60.4 2.5 %collective-permute-start.28 = (bf16[2,24,512]{2,1,0:T(8,128)(2,1)S(1)}, bf16[2,24,512]{2,1,0:T(8,128)(2,1)S(1)}, u32[]{:S(2)}, u32[]{:S(2)}) collective-permute-start(bf16[2,24,512]{2,1,0:T(8,128)(2,1)S(1)} %pad_maximum_fusion.12), channel_id=1, source_target_pairs={{0,2},{1,3},{2,0},{3,1},{4,6},{5,7},{6,4},{7,5},{8,10},{9,11},{10,... | collective-permute-start | bytes 147464 | tf_op jit(solution)/shard_map/ppermute | solution.py:46
  72.3 3.3 %collective-permute-start.20 = (bf16[2,2,48,512]{3,2,1,0:T(8,128)(2,1)S(1)}, bf16[2,2,48,512]{3,2,1,0:T(8,128)(2,1)S(1)}, u32[]{:S(2)}, u32[]{:S(2)}) collective-permute-start(bf16[2,2,48,512]{3,2,1,0:T(8,128)(2,1)S(1)} %pad_maximum_fusion.7), channel_id=1, source_target_pairs={{0,96},{4,28},{8,104},{12,20},{16,112},{20,12},{24,120},{28,4},{32... | collective-permute-start | bytes 589832 | tf_op jit(solution)/shard_map/ppermute | solution.py:38
  82.1 2.2 %collective-permute-start.21 = (bf16[2,2,48,512]{3,2,1,0:T(8,128)(2,1)S(1)}, bf16[2,2,48,512]{3,2,1,0:T(8,128)(2,1)S(1)}, u32[]{:S(2)}, u32[]{:S(2)}) collective-permute-start(bf16[2,2,48,512]{3,2,1,0:T(8,128)(2,1)S(1)} %collective-permute-done.20), channel_id=1, source_target_pairs={{0,8},{4,36},{8,0},{12,44},{16,24},{20,52},{24,16},{28,60},{32,40}... | collective-permute-start | bytes 589832 | tf_op jit(solution)/shard_map/ppermute | solution.py:38
  84.4 2.6 %collective-permute-start.19 = (bf16[2,2,2,48,512]{4,3,2,1,0:T(8,128)(2,1)S(1)}, bf16[2,2,2,48,512]{4,3,2,1,0:T(8,128)(2,1)S(1)}, u32[]{:S(2)}, u32[]{:S(2)}) collective-permute-start(bf16[2,2,2,48,512]{4,3,2,1,0:T(8,128)(2,1)S(1)} %get-tuple-element.78.refs_0_), channel_id=1, source_target_pairs={{0,8},{4,36},{8,0},{12,44},{16,24},{20,52},{24,16},{28,60},{32,40}... | collective-permute-start | bytes 1179656 | tf_op jit(solution)/shard_map/ppermute | solution.py:38
  90.1 4.8 %collective-permute-done.34 = bf16[2,2,48,512]{3,2,1,0:T(8,128)(2,1)S(1)} collective-permute-done((bf16[2,2,48,512]{3,2,1,0:T(8,128)(2,1)S(1)}, bf16[2,2,48,512]{3,2,1,0:T(8,128)(2,1)S(1)}, u32[]{:S(2)}, u32[]{:S(2)}) %collective-permute-start.34) | collective-permute-done | bytes 196640 | tf_op jit(solution)/shard_map/ppermute | solution.py:38
  99.3 3.1 %collective-permute-done.17.refs_3_ = bf16[128,768]{1,0:T(8,128)(2,1)S(1)} collective-permute-done((bf16[128,768]{1,0:T(8,128)(2,1)S(1)}, bf16[128,768]{1,0:T(8,128)(2,1)S(1)}, u32[]{:S(2)}, u32[]{:S(2)}) %collective-permute-start.17) | collective-permute-done | bytes 196640 | tf_op jit(solution)/shard_map/ppermute | solution.py:46
  106.3 4.1 %collective-permute-done.35.refs_3_ = bf16[2,2,2,48,512]{4,3,2,1,0:T(8,128)(2,1)} collective-permute-done((bf16[2,2,2,48,512]{4,3,2,1,0:T(8,128)(2,1)S(1)}, bf16[2,2,2,48,512]{4,3,2,1,0:T(8,128)(2,1)}, u32[]{:S(2)}, u32[]{:S(2)}) %collective-permute-start.35) | collective-permute-done | bytes 393248 | tf_op jit(solution)/shard_map/ppermute | solution.py:38
  132.0 7.3 %collective-permute-done.27.refs_2_ = bf16[128,512]{1,0:T(8,128)(2,1)S(1)} collective-permute-done((bf16[128,512]{1,0:T(8,128)(2,1)S(1)}, bf16[128,512]{1,0:T(8,128)(2,1)S(1)}, u32[]{:S(2)}, u32[]{:S(2)}) %collective-permute-start.27) | collective-permute-done | bytes 131104 | tf_op jit(solution)/shard_map/ppermute | solution.py:46
  145.7 3.8 %collective-permute-done.40.refs_1_ = bf16[128,512]{1,0:T(8,128)(2,1)S(1)} collective-permute-done((bf16[128,512]{1,0:T(8,128)(2,1)S(1)}, bf16[128,512]{1,0:T(8,128)(2,1)S(1)}, u32[]{:S(2)}, u32[]{:S(2)}) %collective-permute-start.40) | collective-permute-done | bytes 131104 | tf_op jit(solution)/shard_map/ppermute | solution.py:46
  149.5 3.9 %collective-permute-done.41.refs_2_ = bf16[128,512]{1,0:T(8,128)(2,1)S(1)} collective-permute-done((bf16[128,512]{1,0:T(8,128)(2,1)S(1)}, bf16[128,512]{1,0:T(8,128)(2,1)S(1)}, u32[]{:S(2)}, u32[]{:S(2)}) %collective-permute-start.41) | collective-permute-done | bytes 131104 | tf_op jit(solution)/shard_map/ppermute | solution.py:46
  153.9 2.2 %collective-permute-start.43 = (f32[8,128]{1,0:T(8,128)S(1)}, f32[8,128]{1,0:T(8,128)S(1)}, u32[]{:S(2)}, u32[]{:S(2)}) collective-permute-start(f32[8,128]{1,0:T(8,128)S(1)} %get-tuple-element.70), channel_id=1, source_target_pairs={{0,3},{1,2},{2,1},{3,0},{4,7},{5,6},{6,5},{7,4},{8,11},{9,10},{10,... | collective-permute-start | bytes 12296 | tf_op jit(solution)/shard_map/ppermute | solution.py:46
  156.1 2.2 %collective-permute-start.45 = (f32[8,128]{1,0:T(8,128)S(1)}, f32[8,128]{1,0:T(8,128)S(1)}, u32[]{:S(2)}, u32[]{:S(2)}) collective-permute-start(f32[8,128]{1,0:T(8,128)S(1)} %get-tuple-element.70), channel_id=1, source_target_pairs={{0,1},{1,0},{2,3},{3,2},{4,5},{5,4},{6,7},{7,6},{8,9},{9,8},{10,11... | collective-permute-start | bytes 12296 | tf_op jit(solution)/shard_map/ppermute | solution.py:46
  (163 shorter events, 75.3 us)
Async XLA Ops:
  6.5 8.1 %collective-permute-start.2 = (bf16[4,2,48,512]{3,2,1,0:T(8,128)(2,1)S(1)}, bf16[4,2,48,512]{3,2,1,0:T(8,128)(2,1)S(1)}, u32[]{:S(2)}, u32[]{:S(2)}) collective-permute-start(bf16[4,2,48,512]{3,2,1,0:T(8,128)(2,1)S(1)} %get-tuple-element.41), channel_id=1, source_target_pairs={{0,8},{4,36},{8,0},{12,44},{16,24},{20,52},{24,16},{28,60},{32,40}... | collective-permute-start | bytes 1179656 | tf_op jit(solution)/shard_map/ppermute | solution.py:38
  10.4 9.9 %collective-permute-start.1 = (bf16[4,2,48,512]{3,2,1,0:T(8,128)(2,1)S(1)}, bf16[4,2,48,512]{3,2,1,0:T(8,128)(2,1)S(1)}, u32[]{:S(2)}, u32[]{:S(2)}) collective-permute-start(bf16[4,2,48,512]{3,2,1,0:T(8,128)(2,1)S(1)} %get-tuple-element.39), channel_id=1, source_target_pairs={{0,8},{4,36},{8,0},{12,44},{16,24},{20,52},{24,16},{28,60},{32,40}... | collective-permute-start | bytes 1179656 | tf_op jit(solution)/shard_map/ppermute | solution.py:38
  16.1 12.8 %collective-permute-start.7 = (bf16[4,2,48,512]{3,2,1,0:T(8,128)(2,1)S(1)}, bf16[4,2,48,512]{3,2,1,0:T(8,128)(2,1)S(1)}, u32[]{:S(2)}, u32[]{:S(2)}) collective-permute-start(bf16[4,2,48,512]{3,2,1,0:T(8,128)(2,1)S(1)} %get-tuple-element.48), channel_id=1, source_target_pairs={{0,24},{4,100},{8,16},{12,108},{16,8},{20,116},{24,0},{28,124},{32... | collective-permute-start | bytes 1179656 | tf_op jit(solution)/shard_map/ppermute | solution.py:38
  17.5 11.4 %collective-permute-start.9 = (bf16[4,2,48,512]{3,2,1,0:T(8,128)(2,1)S(1)}, bf16[4,2,48,512]{3,2,1,0:T(8,128)(2,1)S(1)}, u32[]{:S(2)}, u32[]{:S(2)}) collective-permute-start(bf16[4,2,48,512]{3,2,1,0:T(8,128)(2,1)S(1)} %add_convert_fusion), channel_id=1, source_target_pairs={{0,8},{4,36},{8,0},{12,44},{16,24},{20,52},{24,16},{28,60},{32,40}... | collective-permute-start | bytes 1179656 | tf_op jit(solution)/shard_map/ppermute | solution.py:38
  40.9 14.4 %collective-permute-start.12 = (bf16[2,2,48,512]{3,2,0,1:T(8,128)(2,1)S(1)}, bf16[2,2,48,512]{3,2,0,1:T(8,128)(2,1)S(1)}, u32[]{:S(2)}, u32[]{:S(2)}) collective-permute-start(bf16[2,2,48,512]{3,2,0,1:T(8,128)(2,1)S(1)} %fusion), channel_id=1, source_target_pairs={{0,128},{128,0},{1,129},{129,1},{2,130},{130,2},{3,131},{131,3},{4... | collective-permute-start | bytes 589832 | tf_op jit(solution)/shard_map/ppermute | solution.py:42
  47.8 12.4 %collective-permute-start.13 = (f32[2,48,512]{2,1,0:T(8,128)S(1)}, f32[2,48,512]{2,1,0:T(8,128)S(1)}, u32[]{:S(2)}, u32[]{:S(2)}) collective-permute-start(f32[2,48,512]{2,1,0:T(8,128)S(1)} %multiply_subtract_fusion.1), channel_id=1, source_target_pairs={{0,128},{128,0},{1,129},{129,1},{2,130},{130,2},{3,131},{131,3},{4... | collective-permute-start | bytes 589832 | tf_op jit(solution)/shard_map/ppermute | solution.py:42
  72.3 9.0 %collective-permute-start.20 = (bf16[2,2,48,512]{3,2,1,0:T(8,128)(2,1)S(1)}, bf16[2,2,48,512]{3,2,1,0:T(8,128)(2,1)S(1)}, u32[]{:S(2)}, u32[]{:S(2)}) collective-permute-start(bf16[2,2,48,512]{3,2,1,0:T(8,128)(2,1)S(1)} %pad_maximum_fusion.7), channel_id=1, source_target_pairs={{0,96},{4,28},{8,104},{12,20},{16,112},{20,12},{24,120},{28,4},{32... | collective-permute-start | bytes 589832 | tf_op jit(solution)/shard_map/ppermute | solution.py:38
  77.7 9.3 %collective-permute-start.31 = (bf16[2,2,48,512]{3,2,1,0:T(8,128)(2,1)S(1)}, bf16[2,2,48,512]{3,2,1,0:T(8,128)(2,1)S(1)}, u32[]{:S(2)}, u32[]{:S(2)}) collective-permute-start(bf16[2,2,48,512]{3,2,1,0:T(8,128)(2,1)S(1)} %get-tuple-element.84), channel_id=1, source_target_pairs={{0,24},{4,100},{8,16},{12,108},{16,8},{20,116},{24,0},{28,124},{32... | collective-permute-start | bytes 589832 | tf_op jit(solution)/shard_map/ppermute | solution.py:38
  79.3 18.4 %collective-permute-start.15 = (bf16[128,768]{1,0:T(8,128)(2,1)S(1)}, bf16[128,768]{1,0:T(8,128)(2,1)S(1)}, u32[]{:S(2)}, u32[]{:S(2)}) collective-permute-start(bf16[128,768]{1,0:T(8,128)(2,1)S(1)} %copy-done.6), channel_id=1, source_target_pairs={{0,1},{1,0},{2,3},{3,2},{4,5},{5,4},{6,7},{7,6},{8,9},{9,8},{10,11... | collective-permute-start | bytes 589832 | tf_op jit(solution)/shard_map/ppermute | solution.py:46
  81.3 16.5 %collective-permute-start.16 = (bf16[128,768]{1,0:T(8,128)(2,1)S(1)}, bf16[128,768]{1,0:T(8,128)(2,1)S(1)}, u32[]{:S(2)}, u32[]{:S(2)}) collective-permute-start(bf16[128,768]{1,0:T(8,128)(2,1)S(1)} %copy-done.6), channel_id=1, source_target_pairs={{0,2},{1,3},{2,0},{3,1},{4,6},{5,7},{6,4},{7,5},{8,10},{9,11},{10,... | collective-permute-start | bytes 589832 | tf_op jit(solution)/shard_map/ppermute | solution.py:46
  84.4 20.4 %collective-permute-start.19 = (bf16[2,2,2,48,512]{4,3,2,1,0:T(8,128)(2,1)S(1)}, bf16[2,2,2,48,512]{4,3,2,1,0:T(8,128)(2,1)S(1)}, u32[]{:S(2)}, u32[]{:S(2)}) collective-permute-start(bf16[2,2,2,48,512]{4,3,2,1,0:T(8,128)(2,1)S(1)} %get-tuple-element.78.refs_0_), channel_id=1, source_target_pairs={{0,8},{4,36},{8,0},{12,44},{16,24},{20,52},{24,16},{28,60},{32,40}... | collective-permute-start | bytes 1179656 | tf_op jit(solution)/shard_map/ppermute | solution.py:38
  88.0 16.9 %collective-permute-start.32 = (bf16[2,2,2,48,512]{4,3,2,1,0:T(8,128)(2,1)S(1)}, bf16[2,2,2,48,512]{4,3,2,1,0:T(8,128)(2,1)S(1)}, u32[]{:S(2)}, u32[]{:S(2)}) collective-permute-start(bf16[2,2,2,48,512]{4,3,2,1,0:T(8,128)(2,1)S(1)} %get-tuple-element.74.refs_0_), channel_id=1, source_target_pairs={{0,8},{4,36},{8,0},{12,44},{16,24},{20,52},{24,16},{28,60},{32,40}... | collective-permute-start | bytes 1179656 | tf_op jit(solution)/shard_map/ppermute | solution.py:38
  97.7 22.0 %collective-permute-start.23 = (bf16[2,2,2,2,48,512]{5,4,3,2,1,0:T(8,128)(2,1)}, bf16[2,2,2,2,48,512]{5,4,3,2,1,0:T(8,128)(2,1)S(1)}, u32[]{:S(2)}, u32[]{:S(2)}) collective-permute-start(bf16[2,2,2,2,48,512]{5,4,3,2,1,0:T(8,128)(2,1)} %pad_maximum_fusion), channel_id=1, source_target_pairs={{0,4},{4,0},{1,5},{5,1},{2,6},{6,2},{3,7},{7,3},{8,12},{12,8},{9,1... | collective-permute-start | bytes 2359304 | tf_op jit(solution)/shard_map/ppermute | solution.py:42
  97.8 8.3 %collective-permute-start.22 = (bf16[2,2,2,48,512]{4,3,2,1,0:T(8,128)(2,1)S(1)}, bf16[2,2,2,48,512]{4,3,2,1,0:T(8,128)(2,1)}, u32[]{:S(2)}, u32[]{:S(2)}) collective-permute-start(bf16[2,2,2,48,512]{4,3,2,1,0:T(8,128)(2,1)S(1)} %get-tuple-element.80.refs_2_), channel_id=1, source_target_pairs={{0,24},{4,100},{8,16},{12,108},{16,8},{20,116},{24,0},{28,124},{32... | collective-permute-start | bytes 1179656 | tf_op jit(solution)/shard_map/ppermute | solution.py:38
  102.5 7.9 %collective-permute-start.35 = (bf16[2,2,2,48,512]{4,3,2,1,0:T(8,128)(2,1)S(1)}, bf16[2,2,2,48,512]{4,3,2,1,0:T(8,128)(2,1)}, u32[]{:S(2)}, u32[]{:S(2)}) collective-permute-start(bf16[2,2,2,48,512]{4,3,2,1,0:T(8,128)(2,1)S(1)} %get-tuple-element.76.refs_2_), channel_id=1, source_target_pairs={{0,24},{4,100},{8,16},{12,108},{16,8},{20,116},{24,0},{28,124},{32... | collective-permute-start | bytes 1179656 | tf_op jit(solution)/shard_map/ppermute | solution.py:38
  104.8 24.4 %collective-permute-start.36 = (bf16[2,2,2,2,48,512]{5,4,3,2,1,0:T(8,128)(2,1)}, bf16[2,2,2,2,48,512]{5,4,3,2,1,0:T(8,128)(2,1)S(1)}, u32[]{:S(2)}, u32[]{:S(2)}) collective-permute-start(bf16[2,2,2,2,48,512]{5,4,3,2,1,0:T(8,128)(2,1)} %pad_maximum_fusion.1), channel_id=1, source_target_pairs={{0,4},{4,0},{1,5},{5,1},{2,6},{6,2},{3,7},{7,3},{8,12},{12,8},{9,1... | collective-permute-start | bytes 2359304 | tf_op jit(solution)/shard_map/ppermute | solution.py:42
  106.2 13.6 %collective-permute-start.25 = (bf16[2,2,2,48,512]{4,3,2,1,0:T(8,128)(2,1)}, bf16[2,2,2,48,512]{4,3,2,1,0:T(8,128)(2,1)}, u32[]{:S(2)}, u32[]{:S(2)}) collective-permute-start(bf16[2,2,2,48,512]{4,3,2,1,0:T(8,128)(2,1)} %collective-permute-done.22.refs_3_), channel_id=1, source_target_pairs={{0,4},{4,0},{1,5},{5,1},{2,6},{6,2},{3,7},{7,3},{8,12},{12,8},{9,1... | collective-permute-start | bytes 1179656 | tf_op jit(solution)/shard_map/ppermute | solution.py:42
  110.4 16.8 %collective-permute-start.37 = (bf16[2,2,2,48,512]{4,3,2,1,0:T(8,128)(2,1)S(1)}, bf16[2,2,2,48,512]{4,3,2,1,0:T(8,128)(2,1)}, u32[]{:S(2)}, u32[]{:S(2)}) collective-permute-start(bf16[2,2,2,48,512]{4,3,2,1,0:T(8,128)(2,1)S(1)} %collective-permute-done.32.refs_1_), channel_id=1, source_target_pairs={{0,4},{4,0},{1,5},{5,1},{2,6},{6,2},{3,7},{7,3},{8,12},{12,8},{9,1... | collective-permute-start | bytes 1179656 | tf_op jit(solution)/shard_map/ppermute | solution.py:42
  111.2 18.0 %collective-permute-start.38 = (bf16[2,2,2,48,512]{4,3,2,1,0:T(8,128)(2,1)}, bf16[2,2,2,48,512]{4,3,2,1,0:T(8,128)(2,1)}, u32[]{:S(2)}, u32[]{:S(2)}) collective-permute-start(bf16[2,2,2,48,512]{4,3,2,1,0:T(8,128)(2,1)} %collective-permute-done.35.refs_3_), channel_id=1, source_target_pairs={{0,4},{4,0},{1,5},{5,1},{2,6},{6,2},{3,7},{7,3},{8,12},{12,8},{9,1... | collective-permute-start | bytes 1179656 | tf_op jit(solution)/shard_map/ppermute | solution.py:42
  126.4 12.9 %collective-permute-start.27 = (bf16[128,512]{1,0:T(8,128)(2,1)S(1)}, bf16[128,512]{1,0:T(8,128)(2,1)S(1)}, u32[]{:S(2)}, u32[]{:S(2)}) collective-permute-start(bf16[128,512]{1,0:T(8,128)(2,1)S(1)} %shard_map.98.refs_0_), channel_id=1, source_target_pairs={{0,2},{1,3},{2,0},{3,1},{4,6},{5,7},{6,4},{7,5},{8,10},{9,11},{10,... | collective-permute-start | bytes 393224 | tf_op jit(solution)/shard_map/ppermute | solution.py:46
  127.1 13.1 %collective-permute-start.39 = (bf16[128,512]{1,0:T(8,128)(2,1)S(1)}, bf16[128,512]{1,0:T(8,128)(2,1)S(1)}, u32[]{:S(2)}, u32[]{:S(2)}) collective-permute-start(bf16[128,512]{1,0:T(8,128)(2,1)S(1)} %shard_map.98.refs_0_), channel_id=1, source_target_pairs={{0,3},{1,2},{2,1},{3,0},{4,7},{5,6},{6,5},{7,4},{8,11},{9,10},{10,... | collective-permute-start | bytes 393224 | tf_op jit(solution)/shard_map/ppermute | solution.py:46
  141.2 8.3 %collective-permute-start.40 = (bf16[128,512]{1,0:T(8,128)(2,1)S(1)}, bf16[128,512]{1,0:T(8,128)(2,1)S(1)}, u32[]{:S(2)}, u32[]{:S(2)}) collective-permute-start(bf16[128,512]{1,0:T(8,128)(2,1)S(1)} %get-tuple-element.65), channel_id=1, source_target_pairs={{0,3},{1,2},{2,1},{3,0},{4,7},{5,6},{6,5},{7,4},{8,11},{9,10},{10,... | collective-permute-start | bytes 393224 | tf_op jit(solution)/shard_map/ppermute | solution.py:46
  143.3 10.1 %collective-permute-start.41 = (bf16[128,512]{1,0:T(8,128)(2,1)S(1)}, bf16[128,512]{1,0:T(8,128)(2,1)S(1)}, u32[]{:S(2)}, u32[]{:S(2)}) collective-permute-start(bf16[128,512]{1,0:T(8,128)(2,1)S(1)} %get-tuple-element.66), channel_id=1, source_target_pairs={{0,2},{1,3},{2,0},{3,1},{4,6},{5,7},{6,4},{7,5},{8,10},{9,11},{10,... | collective-permute-start | bytes 393224 | tf_op jit(solution)/shard_map/ppermute | solution.py:46
  144.1 9.4 %collective-permute-start.42 = (bf16[128,512]{1,0:T(8,128)(2,1)S(1)}, bf16[128,512]{1,0:T(8,128)(2,1)S(1)}, u32[]{:S(2)}, u32[]{:S(2)}) collective-permute-start(bf16[128,512]{1,0:T(8,128)(2,1)S(1)} %get-tuple-element.67), channel_id=1, source_target_pairs={{0,1},{1,0},{2,3},{3,2},{4,5},{5,4},{6,7},{7,6},{8,9},{9,8},{10,11... | collective-permute-start | bytes 393224 | tf_op jit(solution)/shard_map/ppermute | solution.py:46
  (44 other events, 333.7 us)
